TPU v7x, 32 devices: a whole 2x2x4 slice. The times are simulated.
32 devices in a mesh: ctx: 16 (over z, x, core), fsdp: 2 (over y).
Axes of the slice: x: 2, y: 2, z: 4, core: 2. Of those that a mesh axis runs over, the one named last changes fastest.
Arguments:
- block_input: bfloat16 [2, 2048, 1536], P('fsdp', 'ctx'), may hold values from -6 to 6
- out_grad: bfloat16 [2, 2048, 1536], P('fsdp', 'ctx'), may hold values from -6 to 6
- block_ids: int32 [32], replicated, may hold values from 0 to 31, as said below
- gain_attn: bfloat16 [1536], P('fsdp'), may hold values from 0.25 to 1.75
- gain_ffn: bfloat16 [1536], P('fsdp'), may hold values from 0.25 to 1.75
- w_query: bfloat16 [1536, 1536], P('fsdp')
- key_weight: bfloat16 [1536, 768], P('fsdp')
- value_weight: bfloat16 [1536, 768], P('fsdp'), may hold values from -0.15625 to 0.15625
- w_out: bfloat16 [1536, 1536], P(None, 'fsdp'), may hold values from -2.5 to 2.5
- w_gate: bfloat16 [1536, 4096], P(None, 'fsdp'), may hold values from -0.15625 to 0.15625
- w_up: bfloat16 [1536, 4096], P(None, 'fsdp'), may hold values from -0.15625 to 0.15625
- w_down: bfloat16 [4096, 1536], P('fsdp'), may hold values from -0.09375 to 0.09375
Outputs:
- block_output: bfloat16 [2, 2048, 1536], P('fsdp', 'ctx')
- input_grad: float32 [2, 2048, 1536], P('fsdp', 'ctx')
- gain_attn_grad: float32 [1536], P(('ctx', 'fsdp'))
- gain_ffn_grad: float32 [1536], P(('ctx', 'fsdp'))
- grad_query: float32 [1536, 1536], P(('ctx', 'fsdp'))
- grad_key: float32 [1536, 768], P(('ctx', 'fsdp'))
- grad_value: float32 [1536, 768], P(('ctx', 'fsdp'))
- grad_out: float32 [1536, 1536], P(None, ('ctx', 'fsdp'))
- grad_gate: float32 [1536, 4096], P('ctx', 'fsdp')
- grad_up: float32 [1536, 4096], P('ctx', 'fsdp')
- grad_down: float32 [4096, 1536], P('fsdp', 'ctx')
Inputs may be any that keep to these rules, and one draw needn't show every extreme that they name: block_ids is a permutation of the 32 blocks; entries 2i and 2i + 1 are a mirrored pair b and 31 - b, in either order.
All inputs are finite; a program needn't handle non-finite values.
Results may differ from a plain program's by a relative error of at most 0.014.
Values may be sent and summed in bfloat16 or wider, within the bound.
A program may use at most 576 MiB of HBM per device.

v0:
```python
import functools
import math

import jax
import jax.numpy as jnp
import numpy as np
from jax import lax
from jax.experimental import pallas as pl
from jax.experimental.pallas import tpu as pltpu
from jax.sharding import PartitionSpec as P


QUERY_HEADS = 16
KEY_HEADS = 8
HEAD_SIZE = 96
GROUP = QUERY_HEADS // KEY_HEADS
LANES = 128
HEADS_STEP = 4
TILE_BLOCKS = 4

EPS = 1e-05
THETA = 100000.0
NEGATIVE_FLOOR = -1e30
LOG2E = math.log2(math.e)
SCALE = HEAD_SIZE ** (-0.5)
VMEM_BYTES = 66_000_000

F32 = jnp.float32
BF16 = jnp.bfloat16


def dot_nn(left, right):
    return lax.dot_general(left, right, (((1,), (0,)), ((), ())), preferred_element_type=F32)


def dot_nt(left, right):
    return lax.dot_general(left, right, (((1,), (1,)), ((), ())), preferred_element_type=F32)


def frequency_row(width):
    lane = np.arange(width)
    half = HEAD_SIZE // 2
    freq = np.exp(-math.log(THETA) * 2.0 * (lane % HEAD_SIZE % half) / HEAD_SIZE)
    return freq.astype(np.float32)


def sign_row(width):
    lane = np.arange(width)
    return np.where(lane % HEAD_SIZE < HEAD_SIZE // 2, -1.0, 1.0).astype(np.float32)


def swap_halves(value):
    width = value.shape[1]
    half = HEAD_SIZE // 2
    lane = lax.broadcasted_iota(jnp.int32, value.shape, 1)
    lower = lax.rem(lane, HEAD_SIZE) < half
    return jnp.where(lower, pltpu.roll(value, width - half, 1), pltpu.roll(value, half, 1))


def rotary_kernel(sign, first, second, cosine, sine, out):
    total = first[...].astype(F32) + second[...].astype(F32)
    out[...] = (total * cosine[...] + sign * swap_halves(total) * sine[...]).astype(BF16)


def rotary_sum(first, second, cosine, sine):
    rows, width = first.shape
    part = cosine.shape[1]
    spec = pl.BlockSpec((rows, part), lambda i: (0, i))
    table = pl.BlockSpec((rows, part), lambda i: (0, 0))
    return pl.pallas_call(
        functools.partial(rotary_kernel, 1.0),
        out_shape=jax.ShapeDtypeStruct((rows, width), BF16),
        grid=(width // part,),
        in_specs=[spec, spec, table, table],
        out_specs=spec,
        name="rotary_sum",
        cost_estimate=pl.CostEstimate(
            flops=6 * rows * width, bytes_accessed=8 * rows * width, transcendentals=0
        ),
    )(first, second, cosine, sine)


def rotary_kv_kernel(k_own, k_got, v_own, v_got, cosine, sine, out):
    width = k_own.shape[1]
    keys = k_own[...] + k_got[...].astype(F32)
    out[:, :width] = (keys * cosine[...] + swap_halves(keys) * sine[...]).astype(BF16)
    out[:, width:] = (v_own[...] + v_got[...].astype(F32)).astype(BF16)


def rotary_kv(k_own, k_got, v_own, v_got, cosine, sine):
    rows, width = k_own.shape
    return pl.pallas_call(
        rotary_kv_kernel,
        out_shape=jax.ShapeDtypeStruct((rows, 2 * width), BF16),
        name="rotary_kv",
        cost_estimate=pl.CostEstimate(
            flops=8 * rows * width, bytes_accessed=20 * rows * width, transcendentals=0
        ),
    )(k_own, k_got, v_own, v_got, cosine, sine)


def rotary_back_kernel(keys, values, cosine, sine, out):
    width = keys.shape[1]
    total = keys[...]
    out[:, :width] = (total * cosine[...] - swap_halves(total) * sine[...]).astype(BF16)
    out[:, width:] = values[...].astype(BF16)


def rotary_back(keys, values, cosine, sine):
    rows, width = keys.shape
    return pl.pallas_call(
        rotary_back_kernel,
        out_shape=jax.ShapeDtypeStruct((rows, 2 * width), BF16),
        name="rotary_back",
        cost_estimate=pl.CostEstimate(
            flops=6 * rows * width, bytes_accessed=20 * rows * width, transcendentals=0
        ),
    )(keys, values, cosine, sine)


def head_slice(rows, head):
    piece = rows[:, head * HEAD_SIZE : (head + 1) * HEAD_SIZE]
    pad = jnp.zeros((rows.shape[0], LANES - HEAD_SIZE), rows.dtype)
    return jnp.concatenate([piece, pad], axis=1)


def group_rows(rows, key_head):
    return jnp.concatenate(
        [head_slice(rows, key_head * GROUP + r) for r in range(GROUP)], axis=0
    )


def tile_rows(ref, slot_of, tile, block):
    pieces = []
    for i in range(TILE_BLOCKS):
        start = pl.multiple_of(slot_of[tile * TILE_BLOCKS + i] * block, block)
        pieces.append(ref[pl.ds(start, block), :])
    return jnp.concatenate(pieces, axis=0)


def allowed(tile, tile_len, query_block, block, rows):
    key_pos = tile * tile_len + lax.broadcasted_iota(jnp.int32, (tile_len, rows), 0)
    row = lax.broadcasted_iota(jnp.int32, (tile_len, rows), 1)
    query_pos = query_block * block + lax.rem(row, block)
    return key_pos <= query_pos


def fold(value, how):
    return how(value.reshape(value.shape[0] // 8, 8, value.shape[1]), axis=0)


def merge_heads(pieces):
    return jnp.concatenate([piece[:, :HEAD_SIZE] for piece in pieces], axis=1)


def forward_kernel(
    batch, block, slot_of, owned, q_ref, k_ref, v_ref, o_ref, lse_ref, kn, vt, scores, acc, top, total
):
    tile_len = TILE_BLOCKS * block
    rows = GROUP * block
    counts = [(owned[m] + TILE_BLOCKS) // TILE_BLOCKS for m in range(2)]
    most = jnp.maximum(counts[0], counts[1])
    merged = [[None] * (HEADS_STEP * GROUP) for _ in range(2)]
    for first in range(0, HEADS_STEP, batch):

        def pack(tile, carry, first=first):
            k_rows = tile_rows(k_ref, slot_of, tile, block)
            v_rows = tile_rows(v_ref, slot_of, tile, block)
            start = pl.multiple_of(tile * tile_len, tile_len)
            for h in range(batch):
                kn[h, pl.ds(start, tile_len), :] = head_slice(k_rows, first + h)
                vt[h, :, pl.ds(start, tile_len)] = head_slice(v_rows, first + h).T
            return carry

        lax.fori_loop(0, most, pack, 0)
        for m in range(2):
            member = slice(m * block, (m + 1) * block)
            q_rows = q_ref[member, :]
            queries = [group_rows(q_rows, first + h) for h in range(batch)]
            for h in range(batch):
                top[h] = jnp.full((8, rows), NEGATIVE_FLOOR, F32)
                total[h] = jnp.zeros((8, rows), F32)
                acc[h] = jnp.zeros((LANES, rows), F32)

            def score_pass(tile, carry, queries=queries, m=m):
                start = pl.multiple_of(tile * tile_len, tile_len)
                mask = allowed(tile, tile_len, owned[m], block, rows)
                for h in range(batch):
                    value = dot_nt(kn[h, pl.ds(start, tile_len), :], queries[h])
                    value = jnp.where(mask, value * (SCALE * LOG2E), NEGATIVE_FLOOR)
                    scores[h, pl.ds(start, tile_len), :] = value
                    top[h] = jnp.maximum(top[h], fold(value, jnp.max))
                return carry

            lax.fori_loop(0, counts[m], score_pass, 0)
            peaks = [jnp.max(top[h], axis=0, keepdims=True) for h in range(batch)]

            def mix_pass(tile, carry, peaks=peaks):
                start = pl.multiple_of(tile * tile_len, tile_len)
                for h in range(batch):
                    weight = jnp.exp2(scores[h, pl.ds(start, tile_len), :] - peaks[h])
                    total[h] += fold(weight, jnp.sum)
                    acc[h] += dot_nn(vt[h, :, pl.ds(start, tile_len)], weight.astype(BF16))
                return carry

            lax.fori_loop(0, counts[m], mix_pass, 0)
            for h in range(batch):
                denom = jnp.sum(total[h], axis=0, keepdims=True)
                mixed = (acc[h] / denom).T.astype(BF16)
                for r in range(GROUP):
                    merged[m][(first + h) * GROUP + r] = mixed[r * block : (r + 1) * block, :]
                lse_ref[first + h, m : m + 1, :] = peaks[h] + jnp.log2(denom)
    for m in range(2):
        o_ref[m * block : (m + 1) * block, :] = merge_heads(merged[m])


def kv_specs(length, heads_width):
    mode = {} if length <= 4096 else {"pipeline_mode": pl.Buffered(1)}
    return [
        pl.BlockSpec((length, heads_width), lambda i, *_, base=base: (0, base + i), **mode)
        for base in (0, KEY_HEADS // HEADS_STEP)
    ]


def attention_forward(query, all_kv, slot_of, owned, block):
    rows = query.shape[0]
    length = all_kv.shape[0]
    batch = HEADS_STEP if length <= 4096 else 1
    steps = KEY_HEADS // HEADS_STEP
    key_width = HEADS_STEP * HEAD_SIZE
    query_width = key_width * GROUP
    pairs = GROUP * block
    query_spec = pl.BlockSpec((rows, query_width), lambda i, *_: (0, i))
    return pl.pallas_call(
        functools.partial(forward_kernel, batch, block),
        out_shape=(
            jax.ShapeDtypeStruct(query.shape, BF16),
            jax.ShapeDtypeStruct((KEY_HEADS, 2, pairs), F32),
        ),
        grid_spec=pltpu.PrefetchScalarGridSpec(
            num_scalar_prefetch=2,
            grid=(steps,),
            in_specs=[query_spec] + kv_specs(length, key_width),
            out_specs=[
                query_spec,
                pl.BlockSpec((HEADS_STEP, 2, pairs), lambda i, *_: (i, 0, 0)),
            ],
            scratch_shapes=[
                pltpu.VMEM((batch, length, LANES), BF16),
                pltpu.VMEM((batch, LANES, length), BF16),
                pltpu.VMEM((batch, length, pairs), F32),
                pltpu.VMEM((batch, LANES, pairs), F32),
                pltpu.VMEM((batch, 8, pairs), F32),
                pltpu.VMEM((batch, 8, pairs), F32),
            ],
        ),
        compiler_params=pltpu.CompilerParams(vmem_limit_bytes=VMEM_BYTES),
        name="attention_forward",
        cost_estimate=pl.CostEstimate(
            flops=4 * rows * length * query.shape[1] // 2,
            bytes_accessed=2 * all_kv.size,
            transcendentals=rows * length * QUERY_HEADS // 2,
        ),
    )(slot_of, owned, query, all_kv, all_kv)


def backward_kernel(
    batch,
    block,
    slot_of,
    owned,
    block_ids,
    q_ref,
    do_ref,
    o_ref,
    lse_ref,
    cos_ref,
    sin_ref,
    k_ref,
    v_ref,
    dq_ref,
    dk_out,
    dv_out,
    kn,
    vn,
    kt,
    dk,
    dv,
    acc,
):
    tile_len = TILE_BLOCKS * block
    rows = GROUP * block
    counts = [(owned[m] + TILE_BLOCKS) // TILE_BLOCKS for m in range(2)]
    most = jnp.maximum(counts[0], counts[1])
    merged = [[None] * (HEADS_STEP * GROUP) for _ in range(2)]
    for first in range(0, HEADS_STEP, batch):

        def pack(tile, carry, first=first):
            k_rows = tile_rows(k_ref, slot_of, tile, block)
            v_rows = tile_rows(v_ref, slot_of, tile, block)
            start = pl.multiple_of(tile * tile_len, tile_len)
            for h in range(batch):
                piece = head_slice(k_rows, first + h)
                kn[h, pl.ds(start, tile_len), :] = piece
                kt[h, :, pl.ds(start, tile_len)] = piece.T
                vn[h, pl.ds(start, tile_len), :] = head_slice(v_rows, first + h)
            return carry

        lax.fori_loop(0, most, pack, 0)
        dk[...] = jnp.zeros_like(dk)
        dv[...] = jnp.zeros_like(dv)
        for m in range(2):
            member = slice(m * block, (m + 1) * block)
            q_rows, g_rows, o_rows = q_ref[member, :], do_ref[member, :], o_ref[member, :]
            queries = [group_rows(q_rows, first + h) for h in range(batch)]
            grads = [group_rows(g_rows, first + h) for h in range(batch)]
            deltas = []
            for h in range(batch):
                product = grads[h].astype(F32) * group_rows(o_rows, first + h).astype(F32)
                deltas.append(jnp.sum(product.T, axis=0, keepdims=True))
                acc[h] = jnp.zeros((LANES, rows), F32)
            lses = [lse_ref[first + h, m : m + 1, :] for h in range(batch)]

            def grad_pass(tile, carry, queries=queries, grads=grads, deltas=deltas, lses=lses, m=m):
                start = pl.multiple_of(tile * tile_len, tile_len)
                mask = allowed(tile, tile_len, owned[m], block, rows)
                for h in range(batch):
                    value = dot_nt(kn[h, pl.ds(start, tile_len), :], queries[h])
                    value = jnp.where(mask, value * (SCALE * LOG2E) - lses[h], NEGATIVE_FLOOR)
                    prob = jnp.exp2(value)
                    weight = prob.astype(BF16)
                    grad_prob = dot_nt(vn[h, pl.ds(start, tile_len), :], grads[h])
                    grad_score = (prob * (grad_prob - deltas[h]) * SCALE).astype(BF16)
                    dk[h, pl.ds(start, tile_len), :] += dot_nn(grad_score, queries[h])
                    dv[h, pl.ds(start, tile_len), :] += dot_nn(weight, grads[h])
                    acc[h] += dot_nn(kt[h, :, pl.ds(start, tile_len)], grad_score)
                return carry

            lax.fori_loop(0, counts[m], grad_pass, 0)
            cosine = jnp.concatenate([cos_ref[member, :]] * GROUP, axis=0)
            sine = jnp.concatenate([sin_ref[member, :]] * GROUP, axis=0)
            for h in range(batch):
                grad = acc[h].T
                grad = (grad * cosine - swap_halves(grad) * sine).astype(BF16)
                for r in range(GROUP):
                    merged[m][(first + h) * GROUP + r] = grad[r * block : (r + 1) * block, :]

        def unpack(chunk, carry, first=first):
            for source, target in ((dk, dk_out), (dv, dv_out)):
                pieces = []
                for h in range(batch):
                    picked = []
                    for i in range(2):
                        start = pl.multiple_of(block_ids[2 * chunk + i] * block, block)
                        picked.append(source[h, pl.ds(start, block), :].astype(BF16))
                    pieces.append(jnp.concatenate(picked, axis=0))
                lanes = slice(first * HEAD_SIZE, (first + batch) * HEAD_SIZE)
                target[chunk, :, lanes] = merge_heads(pieces)
            return carry

        lax.fori_loop(0, dk_out.shape[0], unpack, 0)
    for m in range(2):
        dq_ref[m * block : (m + 1) * block, :] = merge_heads(merged[m])


def attention_backward(
    query, grad, mixed, lse, cosine, sine, all_kv, slot_of, owned, block_ids, block
):
    rows = query.shape[0]
    length = all_kv.shape[0]
    chunks = length // rows
    batch = HEADS_STEP if length <= 4096 else 1
    steps = KEY_HEADS // HEADS_STEP
    key_width = HEADS_STEP * HEAD_SIZE
    query_width = key_width * GROUP
    pairs = GROUP * block
    query_spec = pl.BlockSpec((rows, query_width), lambda i, *_: (0, i))
    mode = {} if length <= 4096 else {"pipeline_mode": pl.Buffered(1)}
    out_spec = pl.BlockSpec((chunks, rows, key_width), lambda i, *_: (0, 0, i), **mode)
    table = pl.BlockSpec((rows, LANES), lambda i, *_: (0, 0))
    grad_shape = jax.ShapeDtypeStruct((chunks, rows, all_kv.shape[1] // 2), BF16)
    return pl.pallas_call(
        functools.partial(backward_kernel, batch, block),
        out_shape=(jax.ShapeDtypeStruct(query.shape, BF16),) + (grad_shape,) * 2,
        grid_spec=pltpu.PrefetchScalarGridSpec(
            num_scalar_prefetch=3,
            grid=(steps,),
            in_specs=[
                query_spec,
                query_spec,
                query_spec,
                pl.BlockSpec((HEADS_STEP, 2, pairs), lambda i, *_: (i, 0, 0)),
                table,
                table,
            ]
            + kv_specs(length, key_width),
            out_specs=[query_spec] + [out_spec] * 2,
            scratch_shapes=[
                pltpu.VMEM((batch, length, LANES), BF16),
                pltpu.VMEM((batch, length, LANES), BF16),
                pltpu.VMEM((batch, LANES, length), BF16),
                pltpu.VMEM((batch, length, LANES), F32),
                pltpu.VMEM((batch, length, LANES), F32),
                pltpu.VMEM((batch, LANES, pairs), F32),
            ],
        ),
        compiler_params=pltpu.CompilerParams(vmem_limit_bytes=VMEM_BYTES),
        name="attention_backward",
        cost_estimate=pl.CostEstimate(
            flops=10 * rows * length * query.shape[1] // 2,
            bytes_accessed=4 * all_kv.size,
            transcendentals=rows * length * QUERY_HEADS // 2,
        ),
    )(slot_of, owned, block_ids, query, grad, mixed, lse, cosine, sine, all_kv, all_kv)


def place():
    me = lax.axis_index("ctx")
    return me // 4, me // 2 % 2, me % 2


def device_at(line, mid, core):
    return {"ctx": (line * 2 + mid) * 2 + core}


def greet(line, mid, core, count):
    barrier = pltpu.get_barrier_semaphore()

    def call(*where):
        pl.semaphore_signal(
            barrier, inc=1, device_id=device_at(*where), device_id_type=pl.DeviceIdType.MESH
        )

    call(line, 1 - mid, core)
    call(line, mid, 1 - core)

    @pl.when(line > 0)
    def _():
        call(line - 1, mid, core)

    @pl.when(line + 1 < count)
    def _():
        call(line + 1, mid, core)

    ends = jnp.where(line > 0, 1, 0) + jnp.where(line + 1 < count, 1, 0)
    pl.semaphore_wait(barrier, 2 + ends)


def remote(source, target, send, recv, where):
    return pltpu.make_async_remote_copy(
        src_ref=source,
        dst_ref=target,
        send_sem=send,
        recv_sem=recv,
        device_id=device_at(*where),
        device_id_type=pl.DeviceIdType.MESH,
    )


def gather_kernel(
    count, own, out, here, right_send, left_send, mid_send, core_send, line_recv, mid_recv, core_recv
):
    line, mid, core = place()
    rows = own.shape[0]
    greet(line, mid, core, count)

    def slot(j, m, k):
        start = pl.multiple_of(((j * 2 + m) * 2 + k) * rows, rows)
        return out.at[pl.ds(start, rows)]

    def to_right(j, source):
        return remote(source, slot(j, mid, core), right_send.at[j], line_recv.at[j], (line + 1, mid, core))

    def to_left(j, source):
        return remote(source, slot(j, mid, core), left_send.at[j], line_recv.at[j], (line - 1, mid, core))

    def to_mid(j, source):
        return remote(source, slot(j, mid, core), mid_send.at[j], mid_recv.at[j], (line, 1 - mid, core))

    def to_core(j, m, source):
        return remote(
            source, slot(j, m, core), core_send.at[2 * j + m], core_recv.at[2 * j + m], (line, mid, 1 - core)
        )

    keep = pltpu.make_async_copy(own, slot(line, mid, core), here)
    keep.start()
    to_mid(line, own).start()

    @pl.when(line + 1 < count)
    def _():
        to_right(line, own).start()

    @pl.when(line > 0)
    def _():
        to_left(line, own).start()

    to_core(line, mid, own).start()


    def arrived_line(j, step_right):
        block = slot(j, mid, core)
        to_right(j, block).wait_recv()
        if step_right:

            @pl.when(line + 1 < count)
            def _():
                to_right(j, block).start()

        else:

            @pl.when(line > 0)
            def _():
                to_left(j, block).start()

        to_mid(j, block).start()
        to_core(j, mid, block).start()

    def arrived_mid(j):
        block = slot(j, 1 - mid, core)
        remote(block, block, mid_send.at[j], mid_recv.at[j], (line, 1 - mid, core)).wait_recv()
        to_core(j, 1 - mid, block).start()

    for step in range(1, count + 1):
        if step < count:

            @pl.when(line - step >= 0)
            def _(step=step):
                arrived_line(line - step, True)

            @pl.when(line + step < count)
            def _(step=step):
                arrived_line(line + step, False)

        if step == 1:
            arrived_mid(line)
        else:

            @pl.when(line - (step - 1) >= 0)
            def _(step=step):
                arrived_mid(line - (step - 1))

            @pl.when(line + (step - 1) < count)
            def _(step=step):
                arrived_mid(line + (step - 1))

    for j in range(count):
        for m in range(2):
            block = slot(j, m, 1 - core)
            remote(
                block, block, core_send.at[2 * j + m], core_recv.at[2 * j + m], (line, mid, 1 - core)
            ).wait_recv()
    keep.wait()
    for j in range(count):
        block = slot(j, mid, core)
        to_mid(j, block).wait_send()
        for m in range(2):
            to_core(j, m, slot(j, m, core)).wait_send()

        @pl.when(jnp.logical_and(j <= line, line + 1 < count))
        def _(j=j, block=block):
            to_right(j, block).wait_send()

        @pl.when(jnp.logical_and(j >= line, line > 0))
        def _(j=j, block=block):
            to_left(j, block).wait_send()


def gather_ctx(own, collective_id):
    size = lax.axis_size("ctx")
    rows, width = own.shape
    count = size // 4
    dma = pltpu.SemaphoreType.DMA
    return pl.pallas_call(
        functools.partial(gather_kernel, count),
        out_shape=jax.ShapeDtypeStruct((size * rows, width), own.dtype),
        in_specs=[pl.BlockSpec(memory_space=pltpu.VMEM)],
        out_specs=pl.BlockSpec(memory_space=pl.ANY),
        scratch_shapes=[dma(())] + [dma((count,))] * 3 + [dma((2 * count,))] + [dma((count,))] * 2 + [dma((2 * count,))],
        compiler_params=pltpu.CompilerParams(collective_id=collective_id, has_side_effects=True),
        cost_estimate=pl.CostEstimate(
            flops=0, bytes_accessed=100 * size * rows * width, transcendentals=0
        ),
    )(own)


def reduce_kernel(count, parts, *refs):
    sources, outs = refs[:parts], refs[parts : 2 * parts]
    scratch = refs[2 * parts :]
    work, from_core, from_mid, from_right, from_left = (scratch[i * parts : (i + 1) * parts] for i in range(5))
    (load, core_send, core_recv, mid_send, mid_recv, left_send, right_send, right_recv, left_recv) = scratch[5 * parts :]
    line, mid, core = place()
    greet(line, mid, core, count)

    def nearest_last(visit):
        for step in range(count - 1, 0, -1):
            for j in (line - step, line + step):

                @pl.when(jnp.logical_and(j >= 0, j < count))
                def _(j=j):
                    visit(j)

        visit(line)

    def core_copy(s, j, m):
        index = 2 * j + m
        return remote(
            sources[s].at[2 * index + (1 - core)],
            from_core[s].at[index],
            core_send.at[s, index],
            core_recv.at[s, index],
            (line, mid, 1 - core),
        )

    def load_copy(s, j, m):
        index = 2 * j + m
        return pltpu.make_async_copy(sources[s].at[2 * index + core], work[s].at[index], load.at[s, index])

    def mid_copy(s, j):
        return remote(
            work[s].at[2 * j + (1 - mid)],
            from_mid[s].at[j],
            mid_send.at[s, j],
            mid_recv.at[s, j],
            (line, 1 - mid, core),
        )

    def left_copy(s, j):
        return remote(
            work[s].at[2 * j + mid],
            from_right[s].at[j],
            left_send.at[s, j],
            right_recv.at[s, j],
            (line - 1, mid, core),
        )

    def right_copy(s, j):
        return remote(
            work[s].at[2 * j + mid],
            from_left[s].at[j],
            right_send.at[s, j],
            left_recv.at[s, j],
            (line + 1, mid, core),
        )

    def add(s, index, other):
        work[s][index] = (work[s][index].astype(F32) + other.astype(F32)).astype(work[s].dtype)

    for m in (1 - mid, mid):

        def begin(j, m=m):
            for s in range(parts):
                core_copy(s, j, m).start()
                load_copy(s, j, m).start()

        nearest_last(begin)

    def core_sum(s, j, m):
        core_copy(s, j, m).wait_recv()
        load_copy(s, j, m).wait()
        add(s, 2 * j + m, from_core[s][2 * j + m])

    def to_mid(j):
        for s in range(parts):
            core_sum(s, j, 1 - mid)
            mid_copy(s, j).start()

    nearest_last(to_mid)

    def keep_mine(j):
        for s in range(parts):
            core_sum(s, j, mid)

    nearest_last(keep_mine)

    def along(j):
        for s in range(parts):
            mid_copy(s, j).wait_recv()
            add(s, 2 * j + mid, from_mid[s][j])

            @pl.when(j < line)
            def _(s=s):
                @pl.when(line + 1 < count)
                def _():
                    left_copy(s, j).wait_recv()
                    add(s, 2 * j + mid, from_right[s][j])

                left_copy(s, j).start()

            @pl.when(j > line)
            def _(s=s):
                @pl.when(line > 0)
                def _():
                    right_copy(s, j).wait_recv()
                    add(s, 2 * j + mid, from_left[s][j])

                right_copy(s, j).start()

    nearest_last(along)
    for s in range(parts):
        outs[s][...] = work[s][2 * line + mid].astype(F32)

        @pl.when(line + 1 < count)
        def _(s=s):
            left_copy(s, line).wait_recv()
            outs[s][...] += from_right[s][line].astype(F32)

        @pl.when(line > 0)
        def _(s=s):
            right_copy(s, line).wait_recv()
            outs[s][...] += from_left[s][line].astype(F32)

    for s in range(parts):
        for j in range(count):
            mid_copy(s, j).wait_send()
            for m in range(2):
                core_copy(s, j, m).wait_send()

            @pl.when(j < line)
            def _(s=s, j=j):
                left_copy(s, j).wait_send()

            @pl.when(j > line)
            def _(s=s, j=j):
                right_copy(s, j).wait_send()


def reduce_ctx(sources, collective_id):
    size = lax.axis_size("ctx")
    count = size // 4
    parts = len(sources)
    dma = pltpu.SemaphoreType.DMA

    def room(chunks):
        return [pltpu.VMEM((chunks,) + source.shape[1:], source.dtype) for source in sources]

    return pl.pallas_call(
        functools.partial(reduce_kernel, count, parts),
        out_shape=[jax.ShapeDtypeStruct(source.shape[1:], F32) for source in sources],
        in_specs=[pl.BlockSpec(memory_space=pl.ANY)] * parts,
        out_specs=[pl.BlockSpec(memory_space=pltpu.VMEM)] * parts,
        scratch_shapes=room(2 * count) + room(2 * count) + room(count) * 1 + room(count) + room(count)
        + [dma((parts, 2 * count))] * 3
        + [dma((parts, count))] * 6,
        compiler_params=pltpu.CompilerParams(
            collective_id=collective_id, has_side_effects=True, vmem_limit_bytes=VMEM_BYTES
        ),
        cost_estimate=pl.CostEstimate(
            flops=0, bytes_accessed=100 * sum(source.size for source in sources), transcendentals=0
        ),
    )(*sources)


def swap_fsdp(value):
    size = lax.axis_size("fsdp")
    return lax.ppermute(value, "fsdp", [(i, size - 1 - i) for i in range(size)])


def swap_bit(value, bit):
    size = lax.axis_size("ctx")
    return lax.ppermute(value, "ctx", [(i, i ^ (1 << bit)) for i in range(size)])


def bit_order(size, swapped=False):
    bits = list(range(size.bit_length() - 1))
    if swapped and len(bits) > 2:
        bits[1], bits[2] = bits[2], bits[1]
    return bits


def my_bit(bit):
    return lax.axis_index("ctx") >> bit & 1


def pick(value, axis, index):
    return lax.dynamic_index_in_dim(value, index, axis, keepdims=False)


def halve(keep, send, bits):
    left = sorted(bits[1:], reverse=True)
    for stage, bit in enumerate(bits):
        got = swap_bit(send, bit)
        total = keep.astype(F32) + got.astype(F32)
        if not left:
            return total
        axis = left.index(bits[stage + 1])
        mine = my_bit(bits[stage + 1])
        send = (
            pick(keep, axis, 1 - mine).astype(F32) + pick(got, axis, 1 - mine).astype(F32)
        ).astype(BF16)
        keep = (pick(keep, axis, mine).astype(F32) + pick(got, axis, mine).astype(F32)).astype(BF16)
        left = left[:axis] + left[axis + 1 :]


def weight_grad(left, right, bits):
    size = lax.axis_size("ctx")
    width, tokens = left.shape
    rows = width // size
    chunks = left.reshape(size // 2, 2, rows, tokens)

    def piece(core):
        flat = pick(chunks, 1, core).reshape(width // 2, tokens)
        product = dot_nn(flat, right).astype(BF16)
        return product.reshape((2,) * (len(bits) - 1) + (rows, right.shape[1]))

    core = my_bit(0)
    send = piece(1 - core)
    keep = piece(core)
    return halve(keep, send, bits)


def side_parts(left, right):
    size = lax.axis_size("ctx")
    width, tokens = left.shape
    rows = width // (2 * size)
    flat = pick(left.reshape(size, 2, rows, tokens), 1, lax.axis_index("fsdp"))
    product = dot_nn(flat.reshape(size * rows, tokens), right).astype(BF16)
    return product.reshape(size, rows, right.shape[1])


def after(value, anchor):
    return lax.optimization_barrier((value, anchor))[0]


def norm_stats(value):
    inverse = lax.rsqrt(jnp.mean(value * value, axis=-1, keepdims=True) + EPS)
    return (value * inverse, inverse)


def norm_back(grad, normed, inverse, gain):
    scaled = grad * gain
    return inverse * (scaled - normed * jnp.mean(scaled * normed, axis=-1, keepdims=True))


def local(
    block_input,
    out_grad,
    block_ids,
    gain_attn,
    gain_ffn,
    w_query,
    key_weight,
    value_weight,
    w_out,
    w_gate,
    w_up,
    w_down,
):
    ctx_size = lax.axis_size("ctx")
    side = lax.axis_index("fsdp")
    me = lax.axis_index("ctx")
    rows, width = block_input.shape[1:]
    half_width = width // 2
    block = rows // 2
    block_count = 2 * ctx_size

    def by_side(own, other, axis):
        return jnp.where(
            side == 0,
            jnp.concatenate([own, other], axis=axis),
            jnp.concatenate([other, own], axis=axis),
        )

    x_own = block_input[0]
    g_own = out_grad[0]
    x_other = swap_fsdp(x_own)

    block_range = jnp.arange(block_count, dtype=jnp.int32)
    slot_of = jnp.sum(
        jnp.where(block_ids[None, :] == block_range[:, None], block_range[None, :], 0), axis=1
    ).astype(jnp.int32)
    owned = lax.dynamic_slice(block_ids, (2 * me,), (2,))
    positions = (
        owned[:, None] * block + jnp.arange(block, dtype=jnp.int32)[None, :]
    ).reshape(rows)
    part = KEY_HEADS * HEAD_SIZE
    angles = positions.astype(F32)[:, None] * jnp.asarray(frequency_row(part))[None, :]
    cosine = jnp.cos(angles)
    sine = jnp.sin(angles) * jnp.asarray(sign_row(part))[None, :]
    bits, bits_z = bit_order(ctx_size), bit_order(ctx_size, True)

    x_f = x_own.astype(F32)
    normed_one, inverse_one = norm_stats(x_f)
    normed_both = jnp.concatenate([normed_one, norm_stats(x_other.astype(F32))[0]], axis=0)
    own_columns = lax.dynamic_slice_in_dim(normed_both, side * half_width, half_width, axis=1)
    left = (own_columns * gain_attn.astype(F32)).astype(BF16)

    def partial_product(weight):
        product = dot_nn(left, weight)
        return product[:rows], swap_fsdp(product[rows:].astype(BF16))

    k_own, k_got = partial_product(key_weight)
    v_own, v_got = partial_product(value_weight)
    q_own, q_got = partial_product(w_query)
    own_kv = rotary_kv(k_own, k_got, v_own, v_got, cosine, sine)
    all_kv = gather_ctx(own_kv, 1)
    query = rotary_sum(q_own, q_got, cosine, sine)

    g_other = swap_fsdp(after(g_own, v_own))
    gains = jnp.stack([gain_attn, gain_ffn])
    gains = by_side(gains, swap_fsdp(gains), 1).astype(F32)
    gain_one, gain_two = gains[0], gains[1]
    core = me % 2
    out_half = w_out.shape[0] // 2
    mine = lax.dynamic_slice_in_dim(w_out, core * out_half, out_half, axis=0)
    mine = swap_fsdp(after(mine, v_own))
    theirs = swap_bit(mine, 0)
    out_other = jnp.where(
        core == 0,
        jnp.concatenate([mine, theirs], axis=0),
        jnp.concatenate([theirs, mine], axis=0),
    )
    full_out = by_side(w_out, out_other, 1)
    n1_turned = (normed_both * gain_one).astype(BF16).T
    g_both = jnp.concatenate([g_own, g_other], axis=0)

    wide_rows = width // ctx_size
    wide_start = me % (ctx_size // 2) * wide_rows
    w_rows = [
        lax.dynamic_slice_in_dim(w, wide_start, wide_rows, axis=0).reshape(2, -1, w.shape[1])
        for w in (w_query, key_weight, value_weight)
    ]
    w_rows = jnp.concatenate(w_rows, axis=2)
    w_got = swap_fsdp(after(pick(w_rows, 0, 1 - side), v_own))
    w_rows = jnp.where(side == me // (ctx_size // 2), pick(w_rows, 0, side), w_got)

    mixed, lse = attention_forward(query, all_kv, slot_of, owned, block)
    mixed_other = swap_fsdp(mixed)
    resid_mid = x_f + dot_nn(mixed, full_out)
    normed_two, inverse_two = norm_stats(resid_mid)
    n2 = (normed_two * gain_two).astype(BF16)
    n2_both = jnp.concatenate([n2, swap_fsdp(n2)], axis=0)

    gate = dot_nn(n2_both, w_gate)
    up = dot_nn(n2_both, w_up)
    sig = jax.nn.sigmoid(gate)
    silu = gate * sig
    hidden = (silu * up).astype(BF16)
    hidden_grad = dot_nt(g_both, w_down)
    gate_grad = (hidden_grad * up * sig * (1.0 + gate * (1.0 - sig))).astype(BF16)
    up_grad = (hidden_grad * silu).astype(BF16)
    n2_grad = dot_nt(gate_grad, w_gate) + dot_nt(up_grad, w_up)
    n2_grad = n2_grad[:rows] + swap_fsdp(n2_grad[rows:].astype(BF16)).astype(F32)
    ffn = dot_nn(hidden, w_down)
    ffn = ffn[:rows] + swap_fsdp(ffn[rows:].astype(BF16)).astype(F32)
    block_output = (resid_mid + ffn).astype(BF16)
    n2_turned = n2_both.T
    grad_gate = weight_grad(n2_turned, gate_grad, bits)
    grad_up = weight_grad(n2_turned, up_grad, bits)
    grad_down = weight_grad(g_both.T, hidden, bits_z).T

    mid_grad = g_own.astype(F32) + norm_back(n2_grad, normed_two, inverse_two, gain_two)
    mid_grad_b = mid_grad.astype(BF16)
    mid_both = jnp.concatenate([mid_grad_b, swap_fsdp(mid_grad_b)], axis=0)
    mixed_both = jnp.concatenate([mixed, mixed_other], axis=0)
    mixed_grad = dot_nt(mid_grad_b, full_out).astype(BF16)
    cosine_pad = jnp.where(jnp.arange(LANES) < HEAD_SIZE, cosine[:, :LANES], 0.0)
    sine_pad = jnp.where(jnp.arange(LANES) < HEAD_SIZE, sine[:, :LANES], 0.0)
    dq, dk_parts, dv_parts = attention_backward(
        query,
        mixed_grad,
        mixed,
        lse,
        cosine_pad,
        sine_pad,
        all_kv,
        slot_of,
        owned,
        block_ids,
        block,
    )
    dk_sum, dv_sum = reduce_ctx([dk_parts, dv_parts], 2)
    dkv = rotary_back(dk_sum, dv_sum, cosine, sine)
    dkv_both = jnp.concatenate([dkv, swap_fsdp(dkv)], axis=0)
    dq_both = jnp.concatenate([dq, swap_fsdp(dq)], axis=0)

    n1_grad = (
        dot_nt(dq_both, w_query)
        + dot_nt(dkv_both[:, :part], key_weight)
        + dot_nt(dkv_both[:, part:], value_weight)
    )
    n1_got = swap_fsdp(n1_grad[rows:].astype(BF16)).astype(F32)
    n1_grad = by_side(n1_grad[:rows], n1_got, 1)
    input_grad = mid_grad + norm_back(n1_grad, normed_one, inverse_one, gain_one)

    out_parts = side_parts(mid_both.T, mixed_both)
    query_parts = side_parts(n1_turned, dq_both)
    kv_parts = side_parts(n1_turned, dkv_both)
    grad_out, grad_query, grad_kv = reduce_ctx([out_parts, query_parts, kv_parts], 3)
    grad_out = grad_out.T
    grad_key, grad_value = grad_kv[:, :part], grad_kv[:, part:]

    own_rows = wide_rows // 2
    first_row = (2 * me + side) * own_rows
    own_gains = lax.dynamic_slice_in_dim(gains, first_row, own_rows, axis=1)
    grads_one = jnp.concatenate([grad_query, grad_kv], axis=1)
    gain_one_grad = jnp.sum(w_rows.astype(F32) * grads_one, axis=1) / own_gains[0]
    gate_rows = lax.dynamic_slice_in_dim(w_gate, me * wide_rows, wide_rows, axis=0).astype(F32)
    up_rows = lax.dynamic_slice_in_dim(w_up, me * wide_rows, wide_rows, axis=0).astype(F32)
    sums = jnp.sum(gate_rows * grad_gate + up_rows * grad_up, axis=1).reshape(2, own_rows)
    sums = pick(sums, 0, side) + swap_fsdp(pick(sums, 0, 1 - side))
    gain_two_grad = sums / own_gains[1]

    return (
        block_output[None],
        input_grad[None],
        gain_one_grad,
        gain_two_grad,
        grad_query,
        grad_key,
        grad_value,
        grad_out,
        grad_gate,
        grad_up,
        grad_down,
    )


def solution(mesh):
    return jax.shard_map(
        local,
        mesh=mesh,
        in_specs=(
            P("fsdp", "ctx", None),
            P("fsdp", "ctx", None),
            P(),
            P("fsdp"),
            P("fsdp"),
            P("fsdp", None),
            P("fsdp", None),
            P("fsdp", None),
            P(None, "fsdp"),
            P(None, "fsdp"),
            P(None, "fsdp"),
            P("fsdp", None),
        ),
        out_specs=(
            P("fsdp", "ctx", None),
            P("fsdp", "ctx", None),
            P(("ctx", "fsdp")),
            P(("ctx", "fsdp")),
            P(("ctx", "fsdp"), None),
            P(("ctx", "fsdp"), None),
            P(("ctx", "fsdp"), None),
            P(None, ("ctx", "fsdp")),
            P("ctx", "fsdp"),
            P("ctx", "fsdp"),
            P("fsdp", "ctx"),
        ),
        check_vma=False,
    )
```

profile of v0, /device:TPU:0, one launch (start us, length us, event | category | flops | bytes accessed | tf_op | source)
XLA Modules:
  0.0 529.5 jit_solution(8948791212763290611)
XLA Ops:
  0.7 3.1 collective-permute-start
  10.4 2.4 constant_dynamic-slice_fusion.18
  12.8 2.3 fusion.39
  17.6 2.0 collective-permute-start.4
  22.8 22.6 %collective-permute-done.4 = bf16[768,768]{1,0:T(8,128)(2,1)} collective-permute-done((bf16[768,768]{1,0:T(8,128)(2,1)}, bf16[768,768]{1,0:T(8,128)(2,1)}, u32[]{:S(2)}, u32[]{:S(2)}) %collective-permute-start.4) | collective-permute-done | bytes 1179680 | tf_op jit(solution)/shard_map/ppermute | solution.py:755
  47.1 1.9 fusion.72
  49.0 1.8 collective-permute-start.1
  51.7 1.7 collective-permute-start.3
  55.6 9.7 %collective-permute-done.2.k_got = bf16[128,768]{1,0:T(8,128)(2,1)S(1)} collective-permute-done((bf16[128,768]{1,0:T(8,128)(2,1)S(1)}, bf16[128,768]{1,0:T(8,128)(2,1)S(1)}, u32[]{:S(2)}, u32[]{:S(2)}) %collective-permute-start.2) | collective-permute-done | bytes 196640 | tf_op jit(solution)/shard_map/ppermute | solution.py:755
  65.3 4.2 collective-permute-done.3.v_got
  70.2 2.6 rotary_kv.1.own
  72.8 44.6 %shard_map.221.k_ref.v_ref = bf16[2048,1536]{1,0:T(8,128)(2,1)} custom-call(bf16[128,1536]{1,0:T(8,128)(2,1)} %rotary_kv.1.own), custom_call_target="tpu_custom_call" | custom-call | bytes 314572800 | tf_op jit(solution)/shard_map/pallas_call | solution.py:573
  118.2 2.7 rotary_sum.1.q_ref
  120.9 18.8 %attention_forward.1 = (bf16[128,1536]{1,0:T(8,128)(2,1)}, f32[8,2,128]{2,1,0:T(2,128)}) custom-call(s32[32]{0:T(128)} %select_reduce_fusion.slot_of, s32[2]{0:T(128)} %get-tuple-element.45.owned, bf16[128,1536]{1,0:T(8,128)(2,1)} %rotary_sum.1.q_ref, bf16[2048,1536]{1,0:T(8,128)(2,1)} %shard_map.221.k_ref.v_ref, bf16[2048,1536]{1,0:T(8,128)(2,1)} %shard_map.221.k_ref.v_ref), custom_call_target="tpu_custom_call" | custom-call | flops 805306368 | bytes 6291456 | tf_op jit(solution)/shard_map/attention_forward/pallas_call | solution.py:234
  139.7 2.9 maximum_select_fusion.1
  142.9 3.1 multiply_reduce_fusion.2
  152.5 5.4 %collective-permute-done.7 = bf16[128,1536]{1,0:T(8,128)(2,1)} collective-permute-done((bf16[128,1536]{1,0:T(8,128)(2,1)}, bf16[128,1536]{1,0:T(8,128)(2,1)}, u32[]{:S(2)}, u32[]{:S(2)}) %collective-permute-start.7) | collective-permute-done | bytes 393248 | tf_op jit(solution)/shard_map/ppermute | solution.py:755
  158.0 4.8 fusion.55
  162.8 5.0 fusion.54
  167.8 5.5 %multiply_convert_fusion = (bf16[256,2048]{1,0:T(8,128)(2,1)S(1)}, bf16[256,2048]{1,0:T(8,128)(2,1)S(1)}, bf16[256,2048]{1,0:T(8,128)(2,1)S(1)}) fusion(f32[256,2048]{1,0:T(8,128)S(1)} %fusion.55, f32[256,2048]{1,0:T(8,128)S(1)} %fusion.54, bf16[2048,1536]{1,0:T(8,128)(2,1)} %param.25, bf16[128,1536]{1,0:T(8,128)(2,1)} %collective-permute-done.9, ...), kind=kOutput, calls=%fused_computation.20 | convolution fusion | flops 1620049920 | bytes 14417920 | tf_op jit(solution)/shard_map/dot_general | solution.py:37
  173.4 3.1 fusion.76
  176.4 2.0 fusion.53
  178.5 2.3 copy.61
  187.4 1.8 convolution_add_fusion
  189.3 1.6 collective-permute-start.10
  190.9 1.8 fusion.75
  193.3 1.9 copy.63
  195.3 2.0 collective-permute-start.17
  197.3 1.9 constant_dynamic-slice_fusion.9
  199.2 1.9 constant_dynamic-slice_fusion.5
  201.1 1.9 copy.68
  204.0 2.2 copy.74
  206.2 2.7 convolution_convert_fusion.1
  209.6 2.6 fusion.70
  212.2 2.7 convolution_convert_fusion.9.do_ref
  214.9 35.4 %attention_backward.1 = (bf16[128,1536]{1,0:T(8,128)(2,1)}, bf16[16,128,768]{2,1,0:T(8,128)(2,1)}, bf16[16,128,768]{2,1,0:T(8,128)(2,1)}) custom-call(s32[32]{0:T(128)} %select_reduce_fusion.slot_of, s32[2]{0:T(128)} %get-tuple-element.45.owned, s32[32]{0:T(128)} %block_ids.1, bf16[128,1536]{1,0:T(8,128)(2,1)} %rotary_sum.1.q_ref, ...), custom_call_target="tpu_custom_call" | custom-call | flops 2013265920 | bytes 12582912 | tf_op jit(solution)/shard_map/attention_backward/pallas_call | solution.py:382
  250.3 41.3 %shard_map.222 = (f32[128,768]{1,0:T(8,128)}, f32[128,768]{1,0:T(8,128)}) custom-call(bf16[16,128,768]{2,1,0:T(8,128)(2,1)} %get-tuple-element.29.refs_0_, bf16[16,128,768]{2,1,0:T(8,128)(2,1)} %get-tuple-element.30.refs_1_), custom_call_target="tpu_custom_call" | custom-call | bytes 314572800 | tf_op jit(solution)/shard_map/pallas_call | solution.py:736
  291.6 2.4 rotary_back.1
  295.5 2.2 constant_dynamic-slice_fusion.11
  297.9 6.6 %collective-permute-done.12 = bf16[128,1536]{1,0:T(8,128)(2,1)S(1)} collective-permute-done((bf16[128,1536]{1,0:T(8,128)(2,1)}, bf16[128,1536]{1,0:T(8,128)(2,1)S(1)}, u32[]{:S(2)}, u32[]{:S(2)}) %collective-permute-start.12) | collective-permute-done | bytes 393248 | tf_op jit(solution)/shard_map/ppermute | solution.py:755
  307.0 6.8 %collective-permute-done.11 = bf16[128,1536]{1,0:T(8,128)(2,1)S(1)} collective-permute-done((bf16[128,1536]{1,0:T(8,128)(2,1)S(1)}, bf16[128,1536]{1,0:T(8,128)(2,1)S(1)}, u32[]{:S(2)}, u32[]{:S(2)}) %collective-permute-start.11) | collective-permute-done | bytes 393248 | tf_op jit(solution)/shard_map/ppermute | solution.py:755
  317.7 5.2 collective-permute-done.15
  325.3 2.3 copy.59
  327.6 3.4 convolution_convert_fusion.6
  331.0 2.2 convolution_convert_fusion.7
  333.2 4.3 add_convert_fusion.5
  338.9 2.5 collective-permute-start.18
  341.4 4.4 add_convert_fusion.3
  348.8 4.3 add_convert_fusion.1
  354.5 3.3 convolution_convert_fusion.8
  357.8 89.6 %shard_map.223 = (f32[48,1536]{1,0:T(8,128)}, f32[48,1536]{1,0:T(8,128)}, f32[48,1536]{1,0:T(8,128)}) custom-call(bf16[16,48,1536]{2,1,0:T(8,128)(2,1)} %bitcast.193, bf16[16,48,1536]{2,1,0:T(8,128)(2,1)} %bitcast.192, bf16[16,48,1536]{2,1,0:T(8,128)(2,1)} %bitcast.191), custom_call_target="tpu_custom_call" | custom-call | bytes 353894400 | tf_op jit(solution)/shard_map/pallas_call | solution.py:736
  448.8 1.7 fusion.71
  450.5 2.1 fusion.11
  452.8 2.1 fusion.9
  454.9 2.0 collective-permute-start.23
  457.3 1.9 fusion.7
  459.2 1.8 collective-permute-start.28
  461.0 16.3 %collective-permute-done.19 = bf16[2,96,2048]{2,1,0:T(8,128)(2,1)S(1)} collective-permute-done((bf16[2,96,2048]{2,1,0:T(8,128)(2,1)S(1)}, bf16[2,96,2048]{2,1,0:T(8,128)(2,1)S(1)}, u32[]{:S(2)}, u32[]{:S(2)}) %collective-permute-start.19) | collective-permute-done | bytes 786464 | tf_op jit(solution)/shard_map/ppermute | solution.py:760
  477.5 15.1 %collective-permute-done.23 = bf16[2,96,2048]{2,1,0:T(8,128)(2,1)S(1)} collective-permute-done((bf16[2,96,2048]{2,1,0:T(8,128)(2,1)S(1)}, bf16[2,96,2048]{2,1,0:T(8,128)(2,1)S(1)}, u32[]{:S(2)}, u32[]{:S(2)}) %collective-permute-start.23) | collective-permute-done | bytes 786464 | tf_op jit(solution)/shard_map/ppermute | solution.py:760
  494.2 3.0 collective-permute-start.29
  497.1 13.6 %collective-permute-done.20 = bf16[96,2048]{1,0:T(8,128)(2,1)S(1)} collective-permute-done((bf16[96,2048]{1,0:T(8,128)(2,1)S(1)}, bf16[96,2048]{1,0:T(8,128)(2,1)S(1)}, u32[]{:S(2)}, u32[]{:S(2)}) %collective-permute-start.20) | collective-permute-done | bytes 393248 | tf_op jit(solution)/shard_map/ppermute | solution.py:760
  510.7 8.4 %collective-permute-done.24 = bf16[96,2048]{1,0:T(8,128)(2,1)S(1)} collective-permute-done((bf16[96,2048]{1,0:T(8,128)(2,1)S(1)}, bf16[96,2048]{1,0:T(8,128)(2,1)S(1)}, u32[]{:S(2)}, u32[]{:S(2)}) %collective-permute-start.24) | collective-permute-done | bytes 393248 | tf_op jit(solution)/shard_map/ppermute | solution.py:760
  519.1 2.8 add_reduce_fusion
  522.6 3.7 collective-permute-done.29
  (229 shorter events, 57.5 us)
Async XLA Ops:
  0.6 12.1 %copy-start.46 = (f32[768]{0:T(1024)S(1)}, f32[768]{0:T(1024)}, u32[]{:S(2)}) copy-start(f32[768]{0:T(1024)} %constant.208.clone) | copy-start | bytes 9220
  0.7 12.1 %copy-start.47 = (f32[768]{0:T(1024)S(1)}, f32[768]{0:T(1024)}, u32[]{:S(2)}) copy-start(f32[768]{0:T(1024)} %constant.207.clone) | copy-start | bytes 9220
  0.7 14.5 %collective-permute-start = (bf16[128,1536]{1,0:T(8,128)(2,1)}, bf16[128,1536]{1,0:T(8,128)(2,1)S(1)}, u32[]{:S(2)}, u32[]{:S(2)}) collective-permute-start(bf16[128,1536]{1,0:T(8,128)(2,1)} %bitcast.198), channel_id=1, source_target_pairs={{0,1},{1,0},{2,3},{3,2},{4,5},{5,4},{6,7},{7,6},{8,9},{9,8},{10,11... | collective-permute-start | bytes 1179656 | tf_op jit(solution)/shard_map/ppermute | solution.py:755
  5.1 40.9 %collective-permute-start.6 = (bf16[2,768]{1,0:T(2,128)(2,1)S(1)}, bf16[2,768]{1,0:T(2,128)(2,1)S(1)}, u32[]{:S(2)}, u32[]{:S(2)}) collective-permute-start(bf16[2,768]{1,0:T(2,128)(2,1)S(1)} %pad_maximum_fusion.9), channel_id=1, source_target_pairs={{0,1},{1,0},{2,3},{3,2},{4,5},{5,4},{6,7},{7,6},{8,9},{9,8},{10,11... | collective-permute-start | bytes 9224 | tf_op jit(solution)/shard_map/ppermute | solution.py:755
  5.2 9.9 %copy-start.13 = (bf16[1,128,1536]{2,1,0:T(8,128)(2,1)S(1)}, bf16[1,128,1536]{2,1,0:T(8,128)(2,1)}, u32[]{:S(2)}) copy-start(bf16[1,128,1536]{2,1,0:T(8,128)(2,1)} %param.14) | copy-start | bytes 1179652
  16.3 4.8 copy-start
  16.9 28.5 %copy-start.48 = (s32[32]{0:T(128)S(1)}, s32[32]{0:T(128)}, u32[]{:S(2)}) copy-start(s32[32]{0:T(128)} %block_ids.1) | copy-start | bytes 388
  17.6 27.7 %collective-permute-start.4 = (bf16[768,768]{1,0:T(8,128)(2,1)}, bf16[768,768]{1,0:T(8,128)(2,1)}, u32[]{:S(2)}, u32[]{:S(2)}) collective-permute-start(bf16[768,768]{1,0:T(8,128)(2,1)} %constant_dynamic-slice_fusion.18), channel_id=1, source_target_pairs={{0,1},{1,0},{2,3},{3,2},{4,5},{5,4},{6,7},{7,6},{8,9},{9,8},{10,11... | collective-permute-start | bytes 3538952 | tf_op jit(solution)/shard_map/ppermute | solution.py:755
  45.4 94.3 %collective-permute-start.5 = (bf16[768,768]{1,0:T(8,128)(2,1)}, bf16[768,768]{1,0:T(8,128)(2,1)}, u32[]{:S(2)}, u32[]{:S(2)}) collective-permute-start(bf16[768,768]{1,0:T(8,128)(2,1)} %collective-permute-done.4), channel_id=1, source_target_pairs={{0,2},{2,0},{4,6},{6,4},{8,10},{10,8},{12,14},{14,12},{16,18},{18,... | collective-permute-start | bytes 3538952 | tf_op jit(solution)/shard_map/ppermute | solution.py:760
  47.1 3.8 copy-start.8
  47.1 3.7 copy-start.19
  49.0 68.4 %collective-permute-start.1 = (bf16[128,1536]{1,0:T(8,128)(2,1)S(1)}, bf16[128,1536]{1,0:T(8,128)(2,1)S(1)}, u32[]{:S(2)}, u32[]{:S(2)}) collective-permute-start(bf16[128,1536]{1,0:T(8,128)(2,1)S(1)} %slice.158), channel_id=1, source_target_pairs={{0,1},{1,0},{2,3},{3,2},{4,5},{5,4},{6,7},{7,6},{8,9},{9,8},{10,11... | collective-permute-start | bytes 1179656 | tf_op jit(solution)/shard_map/ppermute | solution.py:755
  51.3 14.0 %collective-permute-start.2 = (bf16[128,768]{1,0:T(8,128)(2,1)S(1)}, bf16[128,768]{1,0:T(8,128)(2,1)S(1)}, u32[]{:S(2)}, u32[]{:S(2)}) collective-permute-start(bf16[128,768]{1,0:T(8,128)(2,1)S(1)} %slice.161), channel_id=1, source_target_pairs={{0,1},{1,0},{2,3},{3,2},{4,5},{5,4},{6,7},{7,6},{8,9},{9,8},{10,11... | collective-permute-start | bytes 589832 | tf_op jit(solution)/shard_map/ppermute | solution.py:755
  51.7 17.8 %collective-permute-start.3 = (bf16[128,768]{1,0:T(8,128)(2,1)S(1)}, bf16[128,768]{1,0:T(8,128)(2,1)S(1)}, u32[]{:S(2)}, u32[]{:S(2)}) collective-permute-start(bf16[128,768]{1,0:T(8,128)(2,1)S(1)} %slice.160), channel_id=1, source_target_pairs={{0,1},{1,0},{2,3},{3,2},{4,5},{5,4},{6,7},{7,6},{8,9},{9,8},{10,11... | collective-permute-start | bytes 589832 | tf_op jit(solution)/shard_map/ppermute | solution.py:755
  55.2 95.0 %collective-permute-start.9 = (bf16[128,1536]{1,0:T(8,128)(2,1)}, bf16[128,1536]{1,0:T(8,128)(2,1)}, u32[]{:S(2)}, u32[]{:S(2)}) collective-permute-start(bf16[128,1536]{1,0:T(8,128)(2,1)} %bitcast.2), channel_id=1, source_target_pairs={{0,1},{1,0},{2,3},{3,2},{4,5},{5,4},{6,7},{7,6},{8,9},{9,8},{10,11... | collective-permute-start | bytes 1179656 | tf_op jit(solution)/shard_map/ppermute | solution.py:755
  65.3 4.2 copy-start.43
  139.7 3.2 copy-start.38
  142.6 3.4 copy-start.30
  142.9 5.5 %copy-start.3 = (f32[128,1536]{1,0:T(8,128)S(1)}, f32[128,1536]{1,0:T(8,128)}, u32[]{:S(2)}) copy-start(f32[128,1536]{1,0:T(8,128)} %copy-done.2) | copy-start | bytes 2359300
  146.9 11.1 %collective-permute-start.7 = (bf16[128,1536]{1,0:T(8,128)(2,1)}, bf16[128,1536]{1,0:T(8,128)(2,1)}, u32[]{:S(2)}, u32[]{:S(2)}) collective-permute-start(bf16[128,1536]{1,0:T(8,128)(2,1)} %multiply_convert_fusion.3), channel_id=1, source_target_pairs={{0,1},{1,0},{2,3},{3,2},{4,5},{5,4},{6,7},{7,6},{8,9},{9,8},{10,11... | collective-permute-start | bytes 1179656 | tf_op jit(solution)/shard_map/ppermute | solution.py:755
  148.8 298.5 %collective-permute-start.14 = (bf16[48,3072]{1,0:T(8,128)(2,1)}, bf16[48,3072]{1,0:T(8,128)(2,1)}, u32[]{:S(2)}, u32[]{:S(2)}) collective-permute-start(bf16[48,3072]{1,0:T(8,128)(2,1)} %dynamic-slice_bitcast_fusion), channel_id=1, source_target_pairs={{0,1},{1,0},{2,3},{3,2},{4,5},{5,4},{6,7},{7,6},{8,9},{9,8},{10,11... | collective-permute-start | bytes 884744 | tf_op jit(solution)/shard_map/ppermute | solution.py:755
  162.8 10.5 %slice-start = ((s8[6291456]{0:T(1024)(128)(4,1)}), s8[4194304]{0:T(1024)(128)(4,1)S(1)}, s32[]{:S(2)}) async-start(s8[6291456]{0:T(1024)(128)(4,1)} %bitcast.212), calls=%async_computation | async-start | bytes 8388608
  167.8 5.6 %slice-start.1 = ((s8[6291456]{0:T(1024)(128)(4,1)}), s8[2097152]{0:T(1024)(128)(4,1)S(1)}, s32[]{:S(2)}) async-start(s8[6291456]{0:T(1024)(128)(4,1)} %bitcast.212), calls=%async_computation.1 | async-start | bytes 4194304
  173.3 3.1 copy-start.23
  183.5 3.4 slice-start.2
  185.9 5.0 slice-start.4
  187.4 3.5 slice-start.5
  189.3 19.5 %collective-permute-start.10 = (bf16[128,1536]{1,0:T(8,128)(2,1)S(1)}, bf16[128,1536]{1,0:T(8,128)(2,1)S(1)}, u32[]{:S(2)}, u32[]{:S(2)}) collective-permute-start(bf16[128,1536]{1,0:T(8,128)(2,1)S(1)} %slice.156), channel_id=1, source_target_pairs={{0,1},{1,0},{2,3},{3,2},{4,5},{5,4},{6,7},{7,6},{8,9},{9,8},{10,11... | collective-permute-start | bytes 1179656 | tf_op jit(solution)/shard_map/ppermute | solution.py:755
  192.7 16.9 %collective-permute-start.8 = (bf16[128,1536]{1,0:T(8,128)(2,1)S(1)}, bf16[128,1536]{1,0:T(8,128)(2,1)S(1)}, u32[]{:S(2)}, u32[]{:S(2)}) collective-permute-start(bf16[128,1536]{1,0:T(8,128)(2,1)S(1)} %slice.157), channel_id=1, source_target_pairs={{0,1},{1,0},{2,3},{3,2},{4,5},{5,4},{6,7},{7,6},{8,9},{9,8},{10,11... | collective-permute-start | bytes 1179656 | tf_op jit(solution)/shard_map/ppermute | solution.py:755
  195.3 138.0 %collective-permute-start.17 = (bf16[2,2,2,96,2048]{4,3,0,2,1:T(8,128)(2,1)}, bf16[2,2,2,96,2048]{4,3,0,2,1:T(8,128)(2,1)}, u32[]{:S(2)}, u32[]{:S(2)}) collective-permute-start(bf16[2,2,2,96,2048]{4,3,0,2,1:T(8,128)(2,1)} %copy.63), channel_id=1, source_target_pairs={{0,2},{2,0},{4,6},{6,4},{8,10},{10,8},{12,14},{14,12},{16,18},{18,... | collective-permute-start | bytes 9437192 | tf_op jit(solution)/shard_map/ppermute | solution.py:760
  203.0 138.4 %collective-permute-start.21 = (bf16[2,2,2,96,2048]{4,3,0,2,1:T(8,128)(2,1)}, bf16[2,2,2,96,2048]{4,3,0,2,1:T(8,128)(2,1)}, u32[]{:S(2)}, u32[]{:S(2)}) collective-permute-start(bf16[2,2,2,96,2048]{4,3,0,2,1:T(8,128)(2,1)} %copy.68), channel_id=1, source_target_pairs={{0,2},{2,0},{4,6},{6,4},{8,10},{10,8},{12,14},{14,12},{16,18},{18,... | collective-permute-start | bytes 9437192 | tf_op jit(solution)/shard_map/ppermute | solution.py:760
  208.8 139.4 %collective-permute-start.26 = (bf16[2,2,2,96,2048]{4,3,0,2,1:T(8,128)(2,1)}, bf16[2,2,2,96,2048]{4,3,0,2,1:T(8,128)(2,1)}, u32[]{:S(2)}, u32[]{:S(2)}) collective-permute-start(bf16[2,2,2,96,2048]{4,3,0,2,1:T(8,128)(2,1)} %copy.74), channel_id=1, source_target_pairs={{0,2},{2,0},{4,6},{6,4},{8,10},{10,8},{12,14},{14,12},{16,18},{18,... | collective-permute-start | bytes 9437192 | tf_op jit(solution)/shard_map/ppermute | solution.py:760
  294.0 10.4 %collective-permute-start.12 = (bf16[128,1536]{1,0:T(8,128)(2,1)}, bf16[128,1536]{1,0:T(8,128)(2,1)S(1)}, u32[]{:S(2)}, u32[]{:S(2)}) collective-permute-start(bf16[128,1536]{1,0:T(8,128)(2,1)} %rotary_back.1), channel_id=1, source_target_pairs={{0,1},{1,0},{2,3},{3,2},{4,5},{5,4},{6,7},{7,6},{8,9},{9,8},{10,11... | collective-permute-start | bytes 1179656 | tf_op jit(solution)/shard_map/ppermute | solution.py:755
  295.5 10.4 %copy-start.16 = (bf16[128,1536]{1,0:T(8,128)(2,1)S(1)}, bf16[128,1536]{1,0:T(8,128)(2,1)}, u32[]{:S(2)}) copy-start(bf16[128,1536]{1,0:T(8,128)(2,1)} %rotary_back.1) | copy-start | bytes 1179652
  295.5 10.4 %copy-start.18 = (bf16[768,768]{1,0:T(8,128)(2,1)S(1)}, bf16[768,768]{1,0:T(8,128)(2,1)}, u32[]{:S(2)}) copy-start(bf16[768,768]{1,0:T(8,128)(2,1)} %param.21) | copy-start | bytes 3538948
  297.8 8.7 %copy-start.20 = (bf16[768,768]{1,0:T(8,128)(2,1)S(1)}, bf16[768,768]{1,0:T(8,128)(2,1)}, u32[]{:S(2)}) copy-start(bf16[768,768]{1,0:T(8,128)(2,1)} %param.20) | copy-start | bytes 3538948
  297.8 16.0 %copy-start.36 = (bf16[128,1536]{1,0:T(8,128)(2,1)S(1)}, bf16[128,1536]{1,0:T(8,128)(2,1)}, u32[]{:S(2)}) copy-start(bf16[128,1536]{1,0:T(8,128)(2,1)} %copy-done.35) | copy-start | bytes 1179652
  304.5 9.4 %collective-permute-start.11 = (bf16[128,1536]{1,0:T(8,128)(2,1)S(1)}, bf16[128,1536]{1,0:T(8,128)(2,1)S(1)}, u32[]{:S(2)}, u32[]{:S(2)}) collective-permute-start(bf16[128,1536]{1,0:T(8,128)(2,1)S(1)} %copy-done.41), channel_id=1, source_target_pairs={{0,1},{1,0},{2,3},{3,2},{4,5},{5,4},{6,7},{7,6},{8,9},{9,8},{10,11... | collective-permute-start | bytes 1179656 | tf_op jit(solution)/shard_map/ppermute | solution.py:755
  306.5 8.9 %copy-start.1 = (bf16[768,1536]{1,0:T(8,128)(2,1)S(1)}, bf16[768,1536]{1,0:T(8,128)(2,1)}, u32[]{:S(2)}) copy-start(bf16[768,1536]{1,0:T(8,128)(2,1)} %param.19) | copy-start | bytes 7077892
  313.8 9.1 %collective-permute-start.15 = (bf16[128,1536]{1,0:T(8,128)(2,1)S(1)}, bf16[128,1536]{1,0:T(8,128)(2,1)S(1)}, u32[]{:S(2)}, u32[]{:S(2)}) collective-permute-start(bf16[128,1536]{1,0:T(8,128)(2,1)S(1)} %copy-done.36), channel_id=1, source_target_pairs={{0,1},{1,0},{2,3},{3,2},{4,5},{5,4},{6,7},{7,6},{8,9},{9,8},{10,11... | collective-permute-start | bytes 1179656 | tf_op jit(solution)/shard_map/ppermute | solution.py:755
  322.9 31.5 %collective-permute-start.16 = (bf16[128,1536]{1,0:T(8,128)(2,1)}, bf16[128,1536]{1,0:T(8,128)(2,1)}, u32[]{:S(2)}, u32[]{:S(2)}) collective-permute-start(bf16[128,1536]{1,0:T(8,128)(2,1)} %get-tuple-element.24.o_ref), channel_id=1, source_target_pairs={{0,1},{1,0},{2,3},{3,2},{4,5},{5,4},{6,7},{7,6},{8,9},{9,8},{10,11... | collective-permute-start | bytes 1179656 | tf_op jit(solution)/shard_map/ppermute | solution.py:755
  327.6 3.4 copy-start.22
  327.6 3.4 copy-start.25
  337.6 3.8 copy-start.9
  337.6 3.8 copy-start.10
  338.9 111.6 %collective-permute-start.18 = (bf16[2,2,96,2048]{3,2,1,0:T(8,128)(2,1)}, bf16[2,2,96,2048]{3,2,1,0:T(8,128)(2,1)}, u32[]{:S(2)}, u32[]{:S(2)}) collective-permute-start(bf16[2,2,96,2048]{3,2,1,0:T(8,128)(2,1)} %copy.65), channel_id=1, source_target_pairs={{0,4},{2,6},{4,0},{6,2},{8,12},{10,14},{12,8},{14,10},{16,20},{18,... | collective-permute-start | bytes 4718600 | tf_op jit(solution)/shard_map/ppermute | solution.py:760
  347.1 105.6 %collective-permute-start.22 = (bf16[2,2,96,2048]{3,2,1,0:T(8,128)(2,1)}, bf16[2,2,96,2048]{3,2,1,0:T(8,128)(2,1)}, u32[]{:S(2)}, u32[]{:S(2)}) collective-permute-start(bf16[2,2,96,2048]{3,2,1,0:T(8,128)(2,1)} %copy.70), channel_id=1, source_target_pairs={{0,4},{2,6},{4,0},{6,2},{8,12},{10,14},{12,8},{14,10},{16,20},{18,... | collective-permute-start | bytes 4718600 | tf_op jit(solution)/shard_map/ppermute | solution.py:760
  348.2 102.2 %collective-permute-start.13 = (bf16[128,768]{1,0:T(8,128)(2,1)S(1)}, bf16[128,768]{1,0:T(8,128)(2,1)S(1)}, u32[]{:S(2)}, u32[]{:S(2)}) collective-permute-start(bf16[128,768]{1,0:T(8,128)(2,1)S(1)} %copy-done.45), channel_id=1, source_target_pairs={{0,1},{1,0},{2,3},{3,2},{4,5},{5,4},{6,7},{7,6},{8,9},{9,8},{10,11... | collective-permute-start | bytes 589832 | tf_op jit(solution)/shard_map/ppermute | solution.py:755
  354.5 102.8 %collective-permute-start.27 = (bf16[2,2,96,2048]{3,2,1,0:T(8,128)(2,1)}, bf16[2,2,96,2048]{3,2,1,0:T(8,128)(2,1)}, u32[]{:S(2)}, u32[]{:S(2)}) collective-permute-start(bf16[2,2,96,2048]{3,2,1,0:T(8,128)(2,1)} %copy.76), channel_id=1, source_target_pairs={{0,8},{2,10},{4,12},{6,14},{8,0},{10,2},{12,4},{14,6},{16,24},{18,... | collective-permute-start | bytes 4718600 | tf_op jit(solution)/shard_map/ppermute | solution.py:760
  357.8 89.6 %copy-start.33 = (bf16[2,48,3072]{2,1,0:T(8,128)(2,1)S(1)}, bf16[2,48,3072]{2,1,0:T(8,128)(2,1)}, u32[]{:S(2)}) copy-start(bf16[2,48,3072]{2,1,0:T(8,128)(2,1)} %copy-done.32) | copy-start | bytes 1769476
  447.3 3.2 copy-start.4
  452.7 24.7 %collective-permute-start.19 = (bf16[2,96,2048]{2,1,0:T(8,128)(2,1)S(1)}, bf16[2,96,2048]{2,1,0:T(8,128)(2,1)S(1)}, u32[]{:S(2)}, u32[]{:S(2)}) collective-permute-start(bf16[2,96,2048]{2,1,0:T(8,128)(2,1)S(1)} %get-tuple-element.62), channel_id=1, source_target_pairs={{0,8},{2,10},{4,12},{6,14},{8,0},{10,2},{12,4},{14,6},{16,24},{18,... | collective-permute-start | bytes 2359304 | tf_op jit(solution)/shard_map/ppermute | solution.py:760
  452.8 4.2 copy-start.15
  452.8 4.2 copy-start.26
  452.8 4.5 copy-start.6
  454.9 37.7 %collective-permute-start.23 = (bf16[2,96,2048]{2,1,0:T(8,128)(2,1)S(1)}, bf16[2,96,2048]{2,1,0:T(8,128)(2,1)S(1)}, u32[]{:S(2)}, u32[]{:S(2)}) collective-permute-start(bf16[2,96,2048]{2,1,0:T(8,128)(2,1)S(1)} %get-tuple-element.56), channel_id=1, source_target_pairs={{0,8},{2,10},{4,12},{6,14},{8,0},{10,2},{12,4},{14,6},{16,24},{18,... | collective-permute-start | bytes 2359304 | tf_op jit(solution)/shard_map/ppermute | solution.py:760
  459.2 33.6 %copy-start.28 = (f32[128,1536]{1,0:T(8,128)S(1)}, f32[128,1536]{1,0:T(8,128)}, u32[]{:S(2)}) copy-start(f32[128,1536]{1,0:T(8,128)} %get-tuple-element.43) | copy-start | bytes 2359300
  459.2 34.8 %collective-permute-start.28 = (bf16[2,96,2048]{2,1,0:T(8,128)(2,1)S(1)}, bf16[2,96,2048]{2,1,0:T(8,128)(2,1)S(1)}, u32[]{:S(2)}, u32[]{:S(2)}) collective-permute-start(bf16[2,96,2048]{2,1,0:T(8,128)(2,1)S(1)} %get-tuple-element.50), channel_id=1, source_target_pairs={{0,4},{2,6},{4,0},{6,2},{8,12},{10,14},{12,8},{14,10},{16,20},{18,... | collective-permute-start | bytes 2359304 | tf_op jit(solution)/shard_map/ppermute | solution.py:760
  477.4 33.2 %collective-permute-start.20 = (bf16[96,2048]{1,0:T(8,128)(2,1)S(1)}, bf16[96,2048]{1,0:T(8,128)(2,1)S(1)}, u32[]{:S(2)}, u32[]{:S(2)}) collective-permute-start(bf16[96,2048]{1,0:T(8,128)(2,1)S(1)} %fusion.41), channel_id=1, source_target_pairs={{0,16},{2,18},{4,20},{6,22},{8,24},{10,26},{12,28},{14,30},{16,0},... | collective-permute-start | bytes 1179656 | tf_op jit(solution)/shard_map/ppermute | solution.py:760
  492.7 26.4 %collective-permute-start.24 = (bf16[96,2048]{1,0:T(8,128)(2,1)S(1)}, bf16[96,2048]{1,0:T(8,128)(2,1)S(1)}, u32[]{:S(2)}, u32[]{:S(2)}) collective-permute-start(bf16[96,2048]{1,0:T(8,128)(2,1)S(1)} %fusion.43), channel_id=1, source_target_pairs={{0,16},{2,18},{4,20},{6,22},{8,24},{10,26},{12,28},{14,30},{16,0},... | collective-permute-start | bytes 1179656 | tf_op jit(solution)/shard_map/ppermute | solution.py:760
  494.2 32.1 %collective-permute-start.29 = (bf16[96,2048]{1,0:T(8,128)(2,1)S(1)}, bf16[96,2048]{1,0:T(8,128)(2,1)S(1)}, u32[]{:S(2)}, u32[]{:S(2)}) collective-permute-start(bf16[96,2048]{1,0:T(8,128)(2,1)S(1)} %fusion.45), channel_id=1, source_target_pairs={{0,16},{2,18},{4,20},{6,22},{8,24},{10,26},{12,28},{14,30},{16,0},... | collective-permute-start | bytes 1179656 | tf_op jit(solution)/shard_map/ppermute | solution.py:760
  521.9 5.9 %copy-start.37 = (f32[48,1536]{1,0:T(8,128)S(1)}, f32[48,1536]{1,0:T(8,128)}, u32[]{:S(2)}) copy-start(f32[48,1536]{1,0:T(8,128)} %get-tuple-element.99) | copy-start | bytes 884740
  521.9 6.6 %copy-start.42 = (f32[48,1536]{1,0:T(8,128)S(1)}, f32[48,1536]{1,0:T(8,128)}, u32[]{:S(2)}) copy-start(f32[48,1536]{1,0:T(8,128)} %get-tuple-element.36) | copy-start | bytes 884740
  522.0 5.3 collective-permute-start.25
  (22 other events, 42.8 us)
where the time goes:
time: 536 us; the launch traced here: 530 us
  Pallas kernels  237 us (44%)
  waiting for transfers between devices  118 us (22%)
  matrix products  49.4 us (9%)
  other arithmetic  45.9 us (9%)
  local copies, waits for them, and re-layouts  43.5 us (8%)
  starting transfers between devices  33.9 us (6%)
    pallas_call x2, Pallas kernels, reduce_ctx(): pl.pallas_call(functools.partial(reduce_kernel, count, parts), out_shape=...  131 us
    ppermute x17, waiting for transfers between devices, swap_fsdp(): return lax.ppermute(value, 'fsdp', [(i, size - 1 - i) for i in range(size)])  60.6 us
    ppermute x13, waiting for transfers between devices, swap_bit(): return lax.ppermute(value, 'ctx', [(i, i ^ 1 << bit) for i in range(size)])  57.1 us
    pallas_call x1, Pallas kernels, gather_ctx(): pl.pallas_call(functools.partial(gather_kernel, count), out_shape=jax.Sha...  44.6 us
    pallas_call x1, Pallas kernels, attention_backward(): pl.pallas_call(functools.partial(backward_kernel, batch, block), out_shap...  35.4 us
    dot_general x16, matrix products, dot_nn(): lax.dot_general(left, right, (((1,), (0,)), ((), ())), preferred_element_...  34.4 us
    ppermute x17, starting transfers between devices, swap_fsdp(): return lax.ppermute(value, 'fsdp', [(i, size - 1 - i) for i in range(size)])  20.8 us
    convert_element_type x6, other arithmetic, halve(): (pick(keep, axis, mine).astype(F32) + pick(got, axis, mine).astype(F32))....  19.2 us
  transfers between devices with their start and end apart: 30, of which 12 were waited for; matrix products, arithmetic and copies ran while one was open for 25% of the time, Pallas kernels for 45%

commit v1 on v0

--- a/solution.py
+++ b/solution.py
@@ -15,6 +15,7 @@
 HEAD_SIZE = 96
 GROUP = QUERY_HEADS // KEY_HEADS
 LANES = 128
+PAIR_LANES = 256
 HEADS_STEP = 4
 TILE_BLOCKS = 4
 
@@ -24,6 +25,7 @@
 LOG2E = math.log2(math.e)
 SCALE = HEAD_SIZE ** (-0.5)
 VMEM_BYTES = 66_000_000
+SMALL_VMEM_BYTES = 24_000_000
 
 F32 = jnp.float32
 BF16 = jnp.bfloat16
@@ -118,16 +120,23 @@
     )(keys, values, cosine, sine)
 
 
-def head_slice(rows, head):
-    piece = rows[:, head * HEAD_SIZE : (head + 1) * HEAD_SIZE]
-    pad = jnp.zeros((rows.shape[0], LANES - HEAD_SIZE), rows.dtype)
-    return jnp.concatenate([piece, pad], axis=1)
-
-
-def group_rows(rows, key_head):
-    return jnp.concatenate(
-        [head_slice(rows, key_head * GROUP + r) for r in range(GROUP)], axis=0
-    )
+def pair_lanes(pair):
+    return slice(pair * LANES, pair * LANES + PAIR_LANES)
+
+
+def pair_rows(rows, pair):
+    blocks = []
+    for i in range(2 * GROUP):
+        head = 2 * GROUP * pair + i
+        offset = (2 * pair + i // GROUP) * HEAD_SIZE - pair * LANES
+        pieces = [rows[:, head * HEAD_SIZE : (head + 1) * HEAD_SIZE]]
+        if offset:
+            pieces.insert(0, jnp.zeros((rows.shape[0], offset), rows.dtype))
+        rest = PAIR_LANES - HEAD_SIZE - offset
+        if rest:
+            pieces.append(jnp.zeros((rows.shape[0], rest), rows.dtype))
+        blocks.append(jnp.concatenate(pieces, axis=1))
+    return jnp.concatenate(blocks, axis=0)
 
 
 def tile_rows(ref, slot_of, tile, block):
@@ -138,80 +147,76 @@
     return jnp.concatenate(pieces, axis=0)
 
 
-def allowed(tile, tile_len, query_block, block, rows):
-    key_pos = tile * tile_len + lax.broadcasted_iota(jnp.int32, (tile_len, rows), 0)
-    row = lax.broadcasted_iota(jnp.int32, (tile_len, rows), 1)
-    query_pos = query_block * block + lax.rem(row, block)
+def allowed(tile, tile_len, query_block, block, columns):
+    key_pos = tile * tile_len + lax.broadcasted_iota(jnp.int32, (tile_len, columns), 0)
+    column = lax.broadcasted_iota(jnp.int32, (tile_len, columns), 1)
+    query_pos = query_block * block + lax.rem(column, block)
     return key_pos <= query_pos
+
+
+def vmem_for(length):
+    return SMALL_VMEM_BYTES if length <= 4096 else VMEM_BYTES
 
 
 def fold(value, how):
     return how(value.reshape(value.shape[0] // 8, 8, value.shape[1]), axis=0)
 
 
-def merge_heads(pieces):
-    return jnp.concatenate([piece[:, :HEAD_SIZE] for piece in pieces], axis=1)
-
-
-def forward_kernel(
-    batch, block, slot_of, owned, q_ref, k_ref, v_ref, o_ref, lse_ref, kn, vt, scores, acc, top, total
-):
+def head_rows(turned, block):
+    upright = turned.T.astype(BF16)
+    return [upright[r * block : (r + 1) * block, :] for r in range(GROUP)]
+
+
+def forward_kernel(block, slot_of, owned, q_ref, k_ref, v_ref, o_ref, lse_ref, scores, acc, top, total):
     tile_len = TILE_BLOCKS * block
-    rows = GROUP * block
-    counts = [(owned[m] + TILE_BLOCKS) // TILE_BLOCKS for m in range(2)]
-    most = jnp.maximum(counts[0], counts[1])
-    merged = [[None] * (HEADS_STEP * GROUP) for _ in range(2)]
-    for first in range(0, HEADS_STEP, batch):
-
-        def pack(tile, carry, first=first):
-            k_rows = tile_rows(k_ref, slot_of, tile, block)
-            v_rows = tile_rows(v_ref, slot_of, tile, block)
+    pairs = HEADS_STEP // 2
+    columns = 2 * GROUP * block
+    per_head = GROUP * block
+    for m in range(2):
+        count = (owned[m] + TILE_BLOCKS) // TILE_BLOCKS
+        q_rows = q_ref[m * block : (m + 1) * block, :]
+        queries = [pair_rows(q_rows, p) for p in range(pairs)]
+        top[...] = jnp.full(top.shape, NEGATIVE_FLOOR, F32)
+        total[...] = jnp.zeros(total.shape, F32)
+        acc[...] = jnp.zeros(acc.shape, F32)
+
+        def score_pass(tile, carry, queries=queries, m=m):
             start = pl.multiple_of(tile * tile_len, tile_len)
-            for h in range(batch):
-                kn[h, pl.ds(start, tile_len), :] = head_slice(k_rows, first + h)
-                vt[h, :, pl.ds(start, tile_len)] = head_slice(v_rows, first + h).T
+            mask = allowed(tile, tile_len, owned[m], block, columns)
+            keys = tile_rows(k_ref, slot_of, tile, block)
+            for p in range(pairs):
+                value = dot_nt(keys[:, pair_lanes(p)], queries[p])
+                value = jnp.where(mask, value * (SCALE * LOG2E), NEGATIVE_FLOOR)
+                scores[p, pl.ds(start, tile_len), :] = value
+                top[p] = jnp.maximum(top[p], fold(value, jnp.max))
             return carry
 
-        lax.fori_loop(0, most, pack, 0)
-        for m in range(2):
-            member = slice(m * block, (m + 1) * block)
-            q_rows = q_ref[member, :]
-            queries = [group_rows(q_rows, first + h) for h in range(batch)]
-            for h in range(batch):
-                top[h] = jnp.full((8, rows), NEGATIVE_FLOOR, F32)
-                total[h] = jnp.zeros((8, rows), F32)
-                acc[h] = jnp.zeros((LANES, rows), F32)
-
-            def score_pass(tile, carry, queries=queries, m=m):
-                start = pl.multiple_of(tile * tile_len, tile_len)
-                mask = allowed(tile, tile_len, owned[m], block, rows)
-                for h in range(batch):
-                    value = dot_nt(kn[h, pl.ds(start, tile_len), :], queries[h])
-                    value = jnp.where(mask, value * (SCALE * LOG2E), NEGATIVE_FLOOR)
-                    scores[h, pl.ds(start, tile_len), :] = value
-                    top[h] = jnp.maximum(top[h], fold(value, jnp.max))
-                return carry
-
-            lax.fori_loop(0, counts[m], score_pass, 0)
-            peaks = [jnp.max(top[h], axis=0, keepdims=True) for h in range(batch)]
-
-            def mix_pass(tile, carry, peaks=peaks):
-                start = pl.multiple_of(tile * tile_len, tile_len)
-                for h in range(batch):
-                    weight = jnp.exp2(scores[h, pl.ds(start, tile_len), :] - peaks[h])
-                    total[h] += fold(weight, jnp.sum)
-                    acc[h] += dot_nn(vt[h, :, pl.ds(start, tile_len)], weight.astype(BF16))
-                return carry
-
-            lax.fori_loop(0, counts[m], mix_pass, 0)
-            for h in range(batch):
-                denom = jnp.sum(total[h], axis=0, keepdims=True)
-                mixed = (acc[h] / denom).T.astype(BF16)
-                for r in range(GROUP):
-                    merged[m][(first + h) * GROUP + r] = mixed[r * block : (r + 1) * block, :]
-                lse_ref[first + h, m : m + 1, :] = peaks[h] + jnp.log2(denom)
-    for m in range(2):
-        o_ref[m * block : (m + 1) * block, :] = merge_heads(merged[m])
+        lax.fori_loop(0, count, score_pass, 0)
+        peaks = [jnp.max(top[p], axis=0, keepdims=True) for p in range(pairs)]
+
+        def mix_pass(tile, carry, peaks=peaks):
+            start = pl.multiple_of(tile * tile_len, tile_len)
+            turned = tile_rows(v_ref, slot_of, tile, block).T
+            for p in range(pairs):
+                weight = jnp.exp2(scores[p, pl.ds(start, tile_len), :] - peaks[p])
+                total[p] += fold(weight, jnp.sum)
+                weight = weight.astype(BF16)
+                for i in range(2):
+                    h = 2 * p + i
+                    acc[h] += dot_nn(
+                        turned[h * HEAD_SIZE : (h + 1) * HEAD_SIZE, :],
+                        weight[:, i * per_head : (i + 1) * per_head],
+                    )
+            return carry
+
+        lax.fori_loop(0, count, mix_pass, 0)
+        merged = []
+        for p in range(pairs):
+            denom = jnp.sum(total[p], axis=0, keepdims=True)
+            lse_ref[p, m : m + 1, :] = peaks[p] + jnp.log2(denom)
+            for i in range(2):
+                merged += head_rows(acc[2 * p + i] / denom[:, i * per_head : (i + 1) * per_head], block)
+        o_ref[m * block : (m + 1) * block, :] = jnp.concatenate(merged, axis=1)
 
 
 def kv_specs(length, heads_width):
@@ -225,33 +230,27 @@
 def attention_forward(query, all_kv, slot_of, owned, block):
     rows = query.shape[0]
     length = all_kv.shape[0]
-    batch = HEADS_STEP if length <= 4096 else 1
     steps = KEY_HEADS // HEADS_STEP
+    pairs = HEADS_STEP // 2
     key_width = HEADS_STEP * HEAD_SIZE
-    query_width = key_width * GROUP
-    pairs = GROUP * block
-    query_spec = pl.BlockSpec((rows, query_width), lambda i, *_: (0, i))
+    columns = 2 * GROUP * block
+    query_spec = pl.BlockSpec((rows, key_width * GROUP), lambda i, *_: (0, i))
     return pl.pallas_call(
-        functools.partial(forward_kernel, batch, block),
+        functools.partial(forward_kernel, block),
         out_shape=(
             jax.ShapeDtypeStruct(query.shape, BF16),
-            jax.ShapeDtypeStruct((KEY_HEADS, 2, pairs), F32),
+            jax.ShapeDtypeStruct((KEY_HEADS // 2, 2, columns), F32),
         ),
         grid_spec=pltpu.PrefetchScalarGridSpec(
             num_scalar_prefetch=2,
             grid=(steps,),
             in_specs=[query_spec] + kv_specs(length, key_width),
-            out_specs=[
-                query_spec,
-                pl.BlockSpec((HEADS_STEP, 2, pairs), lambda i, *_: (i, 0, 0)),
-            ],
+            out_specs=[query_spec, pl.BlockSpec((pairs, 2, columns), lambda i, *_: (i, 0, 0))],
             scratch_shapes=[
-                pltpu.VMEM((batch, length, LANES), BF16),
-                pltpu.VMEM((batch, LANES, length), BF16),
-                pltpu.VMEM((batch, length, pairs), F32),
-                pltpu.VMEM((batch, LANES, pairs), F32),
-                pltpu.VMEM((batch, 8, pairs), F32),
-                pltpu.VMEM((batch, 8, pairs), F32),
+                pltpu.VMEM((pairs, length, columns), F32),
+                pltpu.VMEM((HEADS_STEP, HEAD_SIZE, GROUP * block), F32),
+                pltpu.VMEM((pairs, 8, columns), F32),
+                pltpu.VMEM((pairs, 8, columns), F32),
             ],
         ),
         compiler_params=pltpu.CompilerParams(vmem_limit_bytes=VMEM_BYTES),
@@ -265,7 +264,6 @@
 
 
 def backward_kernel(
-    batch,
     block,
     slot_of,
     owned,
@@ -281,86 +279,69 @@
     dq_ref,
     dk_out,
     dv_out,
-    kn,
-    vn,
-    kt,
     dk,
     dv,
     acc,
 ):
     tile_len = TILE_BLOCKS * block
-    rows = GROUP * block
-    counts = [(owned[m] + TILE_BLOCKS) // TILE_BLOCKS for m in range(2)]
-    most = jnp.maximum(counts[0], counts[1])
-    merged = [[None] * (HEADS_STEP * GROUP) for _ in range(2)]
-    for first in range(0, HEADS_STEP, batch):
-
-        def pack(tile, carry, first=first):
-            k_rows = tile_rows(k_ref, slot_of, tile, block)
-            v_rows = tile_rows(v_ref, slot_of, tile, block)
+    pairs = HEADS_STEP // 2
+    columns = 2 * GROUP * block
+    per_head = GROUP * block
+    dk[...] = jnp.zeros_like(dk)
+    dv[...] = jnp.zeros_like(dv)
+    for m in range(2):
+        count = (owned[m] + TILE_BLOCKS) // TILE_BLOCKS
+        member = slice(m * block, (m + 1) * block)
+        q_rows, g_rows, o_rows = q_ref[member, :], do_ref[member, :], o_ref[member, :]
+        queries = [pair_rows(q_rows, p) for p in range(pairs)]
+        grads = [pair_rows(g_rows, p) for p in range(pairs)]
+        deltas = []
+        for p in range(pairs):
+            product = grads[p].astype(F32) * pair_rows(o_rows, p).astype(F32)
+            deltas.append(jnp.sum(product.T, axis=0, keepdims=True))
+        lses = [lse_ref[p, m : m + 1, :] for p in range(pairs)]
+        acc[...] = jnp.zeros(acc.shape, F32)
+
+        def grad_pass(tile, carry, queries=queries, grads=grads, deltas=deltas, lses=lses, m=m):
             start = pl.multiple_of(tile * tile_len, tile_len)
-            for h in range(batch):
-                piece = head_slice(k_rows, first + h)
-                kn[h, pl.ds(start, tile_len), :] = piece
-                kt[h, :, pl.ds(start, tile_len)] = piece.T
-                vn[h, pl.ds(start, tile_len), :] = head_slice(v_rows, first + h)
+            mask = allowed(tile, tile_len, owned[m], block, columns)
+            keys = tile_rows(k_ref, slot_of, tile, block)
+            values = tile_rows(v_ref, slot_of, tile, block)
+            turned = keys.T
+            for p in range(pairs):
+                lanes = pair_lanes(p)
+                value = dot_nt(keys[:, lanes], queries[p])
+                value = jnp.where(mask, value * (SCALE * LOG2E) - lses[p], NEGATIVE_FLOOR)
+                prob = jnp.exp2(value)
+                grad_prob = dot_nt(values[:, lanes], grads[p])
+                grad_score = (prob * (grad_prob - deltas[p]) * SCALE).astype(BF16)
+                dk[pl.ds(start, tile_len), lanes] += dot_nn(grad_score, queries[p])
+                dv[pl.ds(start, tile_len), lanes] += dot_nn(prob.astype(BF16), grads[p])
+                for i in range(2):
+                    h = 2 * p + i
+                    acc[h] += dot_nn(
+                        turned[h * HEAD_SIZE : (h + 1) * HEAD_SIZE, :],
+                        grad_score[:, i * per_head : (i + 1) * per_head],
+                    )
             return carry
 
-        lax.fori_loop(0, most, pack, 0)
-        dk[...] = jnp.zeros_like(dk)
-        dv[...] = jnp.zeros_like(dv)
-        for m in range(2):
-            member = slice(m * block, (m + 1) * block)
-            q_rows, g_rows, o_rows = q_ref[member, :], do_ref[member, :], o_ref[member, :]
-            queries = [group_rows(q_rows, first + h) for h in range(batch)]
-            grads = [group_rows(g_rows, first + h) for h in range(batch)]
-            deltas = []
-            for h in range(batch):
-                product = grads[h].astype(F32) * group_rows(o_rows, first + h).astype(F32)
-                deltas.append(jnp.sum(product.T, axis=0, keepdims=True))
-                acc[h] = jnp.zeros((LANES, rows), F32)
-            lses = [lse_ref[first + h, m : m + 1, :] for h in range(batch)]
-
-            def grad_pass(tile, carry, queries=queries, grads=grads, deltas=deltas, lses=lses, m=m):
-                start = pl.multiple_of(tile * tile_len, tile_len)
-                mask = allowed(tile, tile_len, owned[m], block, rows)
-                for h in range(batch):
-                    value = dot_nt(kn[h, pl.ds(start, tile_len), :], queries[h])
-                    value = jnp.where(mask, value * (SCALE * LOG2E) - lses[h], NEGATIVE_FLOOR)
-                    prob = jnp.exp2(value)
-                    weight = prob.astype(BF16)
-                    grad_prob = dot_nt(vn[h, pl.ds(start, tile_len), :], grads[h])
-                    grad_score = (prob * (grad_prob - deltas[h]) * SCALE).astype(BF16)
-                    dk[h, pl.ds(start, tile_len), :] += dot_nn(grad_score, queries[h])
-                    dv[h, pl.ds(start, tile_len), :] += dot_nn(weight, grads[h])
-                    acc[h] += dot_nn(kt[h, :, pl.ds(start, tile_len)], grad_score)
-                return carry
-
-            lax.fori_loop(0, counts[m], grad_pass, 0)
-            cosine = jnp.concatenate([cos_ref[member, :]] * GROUP, axis=0)
-            sine = jnp.concatenate([sin_ref[member, :]] * GROUP, axis=0)
-            for h in range(batch):
-                grad = acc[h].T
-                grad = (grad * cosine - swap_halves(grad) * sine).astype(BF16)
-                for r in range(GROUP):
-                    merged[m][(first + h) * GROUP + r] = grad[r * block : (r + 1) * block, :]
-
-        def unpack(chunk, carry, first=first):
-            for source, target in ((dk, dk_out), (dv, dv_out)):
-                pieces = []
-                for h in range(batch):
-                    picked = []
-                    for i in range(2):
-                        start = pl.multiple_of(block_ids[2 * chunk + i] * block, block)
-                        picked.append(source[h, pl.ds(start, block), :].astype(BF16))
-                    pieces.append(jnp.concatenate(picked, axis=0))
-                lanes = slice(first * HEAD_SIZE, (first + batch) * HEAD_SIZE)
-                target[chunk, :, lanes] = merge_heads(pieces)
-            return carry
-
-        lax.fori_loop(0, dk_out.shape[0], unpack, 0)
-    for m in range(2):
-        dq_ref[m * block : (m + 1) * block, :] = merge_heads(merged[m])
+        lax.fori_loop(0, count, grad_pass, 0)
+        merged = []
+        for h in range(HEADS_STEP):
+            grad = acc[h]
+            middle = HEAD_SIZE // 2
+            swapped = jnp.concatenate([grad[middle:], grad[:middle]], axis=0)
+            merged += head_rows(grad * cos_ref[m] - swapped * sin_ref[m], block)
+        dq_ref[member, :] = jnp.concatenate(merged, axis=1)
+
+    def unpack(chunk, carry):
+        for source, target in ((dk, dk_out), (dv, dv_out)):
+            for i in range(2):
+                start = pl.multiple_of(block_ids[2 * chunk + i] * block, block)
+                target[chunk, i * block : (i + 1) * block, :] = source[pl.ds(start, block), :].astype(BF16)
+        return carry
+
+    lax.fori_loop(0, dk_out.shape[0], unpack, 0)
 
 
 def attention_backward(
@@ -369,18 +350,17 @@
     rows = query.shape[0]
     length = all_kv.shape[0]
     chunks = length // rows
-    batch = HEADS_STEP if length <= 4096 else 1
     steps = KEY_HEADS // HEADS_STEP
+    pairs = HEADS_STEP // 2
     key_width = HEADS_STEP * HEAD_SIZE
-    query_width = key_width * GROUP
-    pairs = GROUP * block
-    query_spec = pl.BlockSpec((rows, query_width), lambda i, *_: (0, i))
+    columns = 2 * GROUP * block
+    query_spec = pl.BlockSpec((rows, key_width * GROUP), lambda i, *_: (0, i))
     mode = {} if length <= 4096 else {"pipeline_mode": pl.Buffered(1)}
     out_spec = pl.BlockSpec((chunks, rows, key_width), lambda i, *_: (0, 0, i), **mode)
-    table = pl.BlockSpec((rows, LANES), lambda i, *_: (0, 0))
+    table = pl.BlockSpec(cosine.shape, lambda i, *_: (0, 0, 0))
     grad_shape = jax.ShapeDtypeStruct((chunks, rows, all_kv.shape[1] // 2), BF16)
     return pl.pallas_call(
-        functools.partial(backward_kernel, batch, block),
+        functools.partial(backward_kernel, block),
         out_shape=(jax.ShapeDtypeStruct(query.shape, BF16),) + (grad_shape,) * 2,
         grid_spec=pltpu.PrefetchScalarGridSpec(
             num_scalar_prefetch=3,
@@ -389,19 +369,16 @@
                 query_spec,
                 query_spec,
                 query_spec,
-                pl.BlockSpec((HEADS_STEP, 2, pairs), lambda i, *_: (i, 0, 0)),
+                pl.BlockSpec((pairs, 2, columns), lambda i, *_: (i, 0, 0)),
                 table,
                 table,
             ]
             + kv_specs(length, key_width),
             out_specs=[query_spec] + [out_spec] * 2,
             scratch_shapes=[
-                pltpu.VMEM((batch, length, LANES), BF16),
-                pltpu.VMEM((batch, length, LANES), BF16),
-                pltpu.VMEM((batch, LANES, length), BF16),
-                pltpu.VMEM((batch, length, LANES), F32),
-                pltpu.VMEM((batch, length, LANES), F32),
-                pltpu.VMEM((batch, LANES, pairs), F32),
+                pltpu.VMEM((length, key_width), F32),
+                pltpu.VMEM((length, key_width), F32),
+                pltpu.VMEM((HEADS_STEP, HEAD_SIZE, GROUP * block), F32),
             ],
         ),
         compiler_params=pltpu.CompilerParams(vmem_limit_bytes=VMEM_BYTES),
@@ -576,7 +553,9 @@
         in_specs=[pl.BlockSpec(memory_space=pltpu.VMEM)],
         out_specs=pl.BlockSpec(memory_space=pl.ANY),
         scratch_shapes=[dma(())] + [dma((count,))] * 3 + [dma((2 * count,))] + [dma((count,))] * 2 + [dma((2 * count,))],
-        compiler_params=pltpu.CompilerParams(collective_id=collective_id, has_side_effects=True),
+        compiler_params=pltpu.CompilerParams(
+            collective_id=collective_id, has_side_effects=True, vmem_limit_bytes=SMALL_VMEM_BYTES
+        ),
         cost_estimate=pl.CostEstimate(
             flops=0, bytes_accessed=100 * size * rows * width, transcendentals=0
         ),
@@ -742,7 +721,9 @@
         + [dma((parts, 2 * count))] * 3
         + [dma((parts, count))] * 6,
         compiler_params=pltpu.CompilerParams(
-            collective_id=collective_id, has_side_effects=True, vmem_limit_bytes=VMEM_BYTES
+            collective_id=collective_id,
+            has_side_effects=True,
+            vmem_limit_bytes=vmem_for(size * sources[0].shape[1]),
         ),
         cost_estimate=pl.CostEstimate(
             flops=0, bytes_accessed=100 * sum(source.size for source in sources), transcendentals=0
@@ -767,8 +748,19 @@
     return bits
 
 
-def my_bit(bit):
-    return lax.axis_index("ctx") >> bit & 1
+def relative_order(bits):
+    last = len(bits) - 1
+    return [
+        sum(((p >> (last - i)) & 1) << bit for i, bit in enumerate(bits)) for p in range(2 << last)
+    ]
+
+
+def chunk_places(bits):
+    place_of = np.argsort(np.asarray(relative_order(bits))).astype(np.int32)
+    me = lax.axis_index("ctx")
+    distance = jnp.arange(len(place_of), dtype=jnp.int32) ^ me
+    found = distance[:, None] == jnp.arange(len(place_of), dtype=jnp.int32)[None, :]
+    return jnp.sum(jnp.where(found, jnp.asarray(place_of)[None, :], 0), axis=1)
 
 
 def pick(value, axis, index):
@@ -776,36 +768,103 @@
 
 
 def halve(keep, send, bits):
-    left = sorted(bits[1:], reverse=True)
-    for stage, bit in enumerate(bits):
+    for bit in bits:
         got = swap_bit(send, bit)
-        total = keep.astype(F32) + got.astype(F32)
-        if not left:
-            return total
-        axis = left.index(bits[stage + 1])
-        mine = my_bit(bits[stage + 1])
-        send = (
-            pick(keep, axis, 1 - mine).astype(F32) + pick(got, axis, 1 - mine).astype(F32)
-        ).astype(BF16)
-        keep = (pick(keep, axis, mine).astype(F32) + pick(got, axis, mine).astype(F32)).astype(BF16)
-        left = left[:axis] + left[axis + 1 :]
+        if keep.shape[0] == 1:
+            return keep[0].astype(F32) + got[0].astype(F32)
+        mid = keep.shape[0] // 2
+        send = (keep[mid:].astype(F32) + got[mid:].astype(F32)).astype(BF16)
+        keep = (keep[:mid].astype(F32) + got[:mid].astype(F32)).astype(BF16)
 
 
 def weight_grad(left, right, bits):
-    size = lax.axis_size("ctx")
-    width, tokens = left.shape
-    rows = width // size
-    chunks = left.reshape(size // 2, 2, rows, tokens)
-
-    def piece(core):
-        flat = pick(chunks, 1, core).reshape(width // 2, tokens)
-        product = dot_nn(flat, right).astype(BF16)
-        return product.reshape((2,) * (len(bits) - 1) + (rows, right.shape[1]))
-
-    core = my_bit(0)
-    send = piece(1 - core)
-    keep = piece(core)
+    count, rows, tokens = left.shape
+
+    def piece(part):
+        product = dot_nn(part.reshape(count // 2 * rows, tokens), right)
+        return product.astype(BF16).reshape(count // 2, rows, right.shape[1])
+
+    send = piece(left[count // 2 :])
+    keep = piece(left[: count // 2])
     return halve(keep, send, bits)
+
+
+def ffn_kernel(
+    places, n_own, n_other, g_own, g_other, w_gate, w_up, w_down,
+    gate_out, up_out, hidden_out, n_chunks, g_chunks, ng_own, ng_send, ffn_own, ffn_send,
+    n_both, g_both, n_grad, ffn_sum,
+):
+    step, steps = pl.program_id(0), pl.num_programs(0)
+    rows = n_own.shape[0]
+    count, chunk, _ = n_chunks.shape
+
+    @pl.when(step == 0)
+    def _():
+        n_both[:rows], n_both[rows:] = n_own[...], n_other[...]
+        g_both[:rows], g_both[rows:] = g_own[...], g_other[...]
+        for source, target, base in ((n_both, n_chunks, 0), (g_both, g_chunks, count)):
+            turned = source[...].astype(F32).T
+            for c in range(count):
+                target[places[base + c]] = turned[c * chunk : (c + 1) * chunk, :].astype(BF16)
+        n_grad[...] = jnp.zeros(n_grad.shape, F32)
+        ffn_sum[...] = jnp.zeros(ffn_sum.shape, F32)
+
+    wg, wu, wd = w_gate[...], w_up[...], w_down[...]
+    gate = dot_nn(n_both[...], wg)
+    up = dot_nn(n_both[...], wu)
+    hidden_grad = dot_nt(g_both[...], wd)
+    sig = jax.nn.sigmoid(gate)
+    silu = gate * sig
+    hidden = (silu * up).astype(BF16)
+    gate_grad = (hidden_grad * up * sig * (1.0 + gate * (1.0 - sig))).astype(BF16)
+    up_grad = (hidden_grad * silu).astype(BF16)
+    gate_out[...], up_out[...], hidden_out[...] = gate_grad, up_grad, hidden
+    n_grad[...] += dot_nt(gate_grad, wg) + dot_nt(up_grad, wu)
+    ffn_sum[...] += dot_nn(hidden, wd)
+
+    @pl.when(step == steps - 1)
+    def _():
+        ng_own[...], ng_send[...] = n_grad[:rows], n_grad[rows:].astype(BF16)
+        ffn_own[...], ffn_send[...] = ffn_sum[:rows], ffn_sum[rows:].astype(BF16)
+
+
+def ffn(n_own, n_other, g_own, g_other, w_gate, w_up, w_down, places):
+    rows, width = n_own.shape
+    hidden = w_gate.shape[1]
+    count = places.shape[0] // 2
+    tile = min(256, hidden)
+    whole = pl.BlockSpec((rows, width), lambda i, *_: (0, 0))
+    columns = pl.BlockSpec((width, tile), lambda i, *_: (0, i))
+    acts = pl.BlockSpec((2 * rows, tile), lambda i, *_: (0, i))
+    chunks = pl.BlockSpec((count, width // count, 2 * rows), lambda i, *_: (0, 0, 0))
+    act = jax.ShapeDtypeStruct((2 * rows, hidden), BF16)
+    turned = jax.ShapeDtypeStruct((count, width // count, 2 * rows), BF16)
+    own = jax.ShapeDtypeStruct((rows, width), F32)
+    send = jax.ShapeDtypeStruct((rows, width), BF16)
+    return pl.pallas_call(
+        ffn_kernel,
+        out_shape=(act, act, act, turned, turned, own, send, own, send),
+        grid_spec=pltpu.PrefetchScalarGridSpec(
+            num_scalar_prefetch=1,
+            grid=(hidden // tile,),
+            in_specs=[whole] * 4
+            + [columns, columns, pl.BlockSpec((tile, width), lambda i, *_: (i, 0))],
+            out_specs=[acts] * 3 + [chunks] * 2 + [whole] * 4,
+            scratch_shapes=[
+                pltpu.VMEM((2 * rows, width), BF16),
+                pltpu.VMEM((2 * rows, width), BF16),
+                pltpu.VMEM((2 * rows, width), F32),
+                pltpu.VMEM((2 * rows, width), F32),
+            ],
+        ),
+        compiler_params=pltpu.CompilerParams(vmem_limit_bytes=2 * SMALL_VMEM_BYTES),
+        name="ffn",
+        cost_estimate=pl.CostEstimate(
+            flops=24 * rows * width * hidden,
+            bytes_accessed=6 * width * hidden + 12 * rows * hidden,
+            transcendentals=2 * rows * hidden,
+        ),
+    )(places, n_own, n_other, g_own, g_other, w_gate, w_up, w_down)
 
 
 def side_parts(left, right):
@@ -911,57 +970,39 @@
     )
     full_out = by_side(w_out, out_other, 1)
     n1_turned = (normed_both * gain_one).astype(BF16).T
-    g_both = jnp.concatenate([g_own, g_other], axis=0)
-
-    wide_rows = width // ctx_size
-    wide_start = me % (ctx_size // 2) * wide_rows
-    w_rows = [
-        lax.dynamic_slice_in_dim(w, wide_start, wide_rows, axis=0).reshape(2, -1, w.shape[1])
-        for w in (w_query, key_weight, value_weight)
-    ]
-    w_rows = jnp.concatenate(w_rows, axis=2)
-    w_got = swap_fsdp(after(pick(w_rows, 0, 1 - side), v_own))
-    w_rows = jnp.where(side == me // (ctx_size // 2), pick(w_rows, 0, side), w_got)
 
     mixed, lse = attention_forward(query, all_kv, slot_of, owned, block)
     mixed_other = swap_fsdp(mixed)
     resid_mid = x_f + dot_nn(mixed, full_out)
     normed_two, inverse_two = norm_stats(resid_mid)
     n2 = (normed_two * gain_two).astype(BF16)
-    n2_both = jnp.concatenate([n2, swap_fsdp(n2)], axis=0)
-
-    gate = dot_nn(n2_both, w_gate)
-    up = dot_nn(n2_both, w_up)
-    sig = jax.nn.sigmoid(gate)
-    silu = gate * sig
-    hidden = (silu * up).astype(BF16)
-    hidden_grad = dot_nt(g_both, w_down)
-    gate_grad = (hidden_grad * up * sig * (1.0 + gate * (1.0 - sig))).astype(BF16)
-    up_grad = (hidden_grad * silu).astype(BF16)
-    n2_grad = dot_nt(gate_grad, w_gate) + dot_nt(up_grad, w_up)
-    n2_grad = n2_grad[:rows] + swap_fsdp(n2_grad[rows:].astype(BF16)).astype(F32)
-    ffn = dot_nn(hidden, w_down)
-    ffn = ffn[:rows] + swap_fsdp(ffn[rows:].astype(BF16)).astype(F32)
-    block_output = (resid_mid + ffn).astype(BF16)
-    n2_turned = n2_both.T
-    grad_gate = weight_grad(n2_turned, gate_grad, bits)
-    grad_up = weight_grad(n2_turned, up_grad, bits)
-    grad_down = weight_grad(g_both.T, hidden, bits_z).T
+
+    places = jnp.concatenate([chunk_places(bits), chunk_places(bits_z)])
+    gate_grad, up_grad, hidden, n2_chunks, g_chunks, n2_grad, n2_send, ffn_own, ffn_send = ffn(
+        n2, swap_fsdp(n2), g_own, g_other, w_gate, w_up, w_down, places
+    )
+    n2_grad = n2_grad + swap_fsdp(n2_send).astype(F32)
+    ffn_got = swap_fsdp(ffn_send)
+    grad_gate = weight_grad(n2_chunks, gate_grad, bits)
+    grad_up = weight_grad(n2_chunks, up_grad, bits)
+    grad_down = weight_grad(g_chunks, hidden, bits_z).T
 
     mid_grad = g_own.astype(F32) + norm_back(n2_grad, normed_two, inverse_two, gain_two)
     mid_grad_b = mid_grad.astype(BF16)
     mid_both = jnp.concatenate([mid_grad_b, swap_fsdp(mid_grad_b)], axis=0)
     mixed_both = jnp.concatenate([mixed, mixed_other], axis=0)
     mixed_grad = dot_nt(mid_grad_b, full_out).astype(BF16)
-    cosine_pad = jnp.where(jnp.arange(LANES) < HEAD_SIZE, cosine[:, :LANES], 0.0)
-    sine_pad = jnp.where(jnp.arange(LANES) < HEAD_SIZE, sine[:, :LANES], 0.0)
+    row_pos = jnp.concatenate([positions.reshape(2, block)] * GROUP, axis=1).astype(F32)
+    turned_angles = row_pos[:, None, :] * jnp.asarray(frequency_row(HEAD_SIZE))[None, :, None]
+    turned_cosine = jnp.cos(turned_angles)
+    turned_sine = jnp.sin(turned_angles) * jnp.asarray(sign_row(HEAD_SIZE))[None, :, None]
     dq, dk_parts, dv_parts = attention_backward(
         query,
         mixed_grad,
         mixed,
         lse,
-        cosine_pad,
-        sine_pad,
+        turned_cosine,
+        turned_sine,
         all_kv,
         slot_of,
         owned,
@@ -970,8 +1011,19 @@
     )
     dk_sum, dv_sum = reduce_ctx([dk_parts, dv_parts], 2)
     dkv = rotary_back(dk_sum, dv_sum, cosine, sine)
+    block_output = (resid_mid + (ffn_own + after(ffn_got, dq).astype(F32))).astype(BF16)
     dkv_both = jnp.concatenate([dkv, swap_fsdp(dkv)], axis=0)
     dq_both = jnp.concatenate([dq, swap_fsdp(dq)], axis=0)
+
+    wide_rows = width // ctx_size
+    wide_start = me % (ctx_size // 2) * wide_rows
+    w_rows = [
+        lax.dynamic_slice_in_dim(w, wide_start, wide_rows, axis=0).reshape(2, -1, w.shape[1])
+        for w in after((w_query, key_weight, value_weight), dkv_both)
+    ]
+    w_rows = jnp.concatenate(w_rows, axis=2)
+    w_got = swap_fsdp(pick(w_rows, 0, 1 - side))
+    w_rows = jnp.where(side == me // (ctx_size // 2), pick(w_rows, 0, side), w_got)
 
     n1_grad = (
         dot_nt(dq_both, w_query)

time: 536 us -> 497 us (0.927)
  waiting for transfers between devices: 118 us -> 162 us
  Pallas kernels: 237 us -> 194 us
  matrix products: 49.4 us -> 24.9 us
  other arithmetic: 45.9 us -> 30.2 us
    ppermute x13, waiting for transfers between devices: 57.1 us -> 111 us  [swap_bit(): return lax.ppermute(value, 'ctx', [(i, i ^ 1 << bit) for i in range(size)])]
    pallas_call x2, Pallas kernels: 131 us -> 88.7 us  [reduce_ctx(): pl.pallas_call(functools.partial(reduce_kernel, count, parts), out_shape=...]
    dot_general x16 -> x13, matrix products: 34.4 us -> 19.3 us  [dot_nn(): lax.dot_general(left, right, (((1,), (0,)), ((), ())), preferred_element_...]
    unnamed x115 -> x113, local copies, waits for them, and re-layouts: 5.63 us -> 17.9 us
    convert_element_type x10, other arithmetic: 19.5 us -> 8.83 us  [the longest x6 8.47 us: halve(): keep = (keep[:mid].astype(F32) + got[:mid].astype(F32)).astype(BF16)]
    dot_general x7 -> x4, matrix products: 15 us -> 5.55 us  [dot_nt(): lax.dot_general(left, right, (((1,), (1,)), ((), ())), preferred_element_...]
    ppermute x17, waiting for transfers between devices: 60.6 us -> 51.2 us  [swap_fsdp(): return lax.ppermute(value, 'fsdp', [(i, size - 1 - i) for i in range(size)])]
    dynamic_slice x6 -> x2, local copies, waits for them, and re-layouts: 8.4 us -> 1.8 us  [pick(): return lax.dynamic_index_in_dim(value, index, axis, keepdims=False)]
  transfers between devices with their start and end apart: 30 -> 30, of which waited for: 12 -> 12; matrix products, arithmetic and copies ran while one was open for 25% -> 16% of each run, Pallas kernels for 45% -> 40%
where the time goes in v1:
time: 497 us; the launch traced here: 488 us
  Pallas kernels  194 us (39%)
  waiting for transfers between devices  162 us (33%)
  local copies, waits for them, and re-layouts  41.5 us (8%)
  starting transfers between devices  33 us (7%)
  other arithmetic  30.2 us (6%)
  matrix products  24.9 us (5%)
    ppermute x13, waiting for transfers between devices, swap_bit(): return lax.ppermute(value, 'ctx', [(i, i ^ 1 << bit) for i in range(size)])  111 us
    pallas_call x2, Pallas kernels, reduce_ctx(): pl.pallas_call(functools.partial(reduce_kernel, count, parts), out_shape=...  88.7 us
    ppermute x17, waiting for transfers between devices, swap_fsdp(): return lax.ppermute(value, 'fsdp', [(i, size - 1 - i) for i in range(size)])  51.2 us
    pallas_call x1, Pallas kernels, gather_ctx(): pl.pallas_call(functools.partial(gather_kernel, count), out_shape=jax.Sha...  42.4 us
    ppermute x17, starting transfers between devices, swap_fsdp(): return lax.ppermute(value, 'fsdp', [(i, size - 1 - i) for i in range(size)])  23.2 us
    pallas_call x1, Pallas kernels, attention_backward(): pl.pallas_call(functools.partial(backward_kernel, block), out_shape=(jax....  21.9 us
    pallas_call x1, Pallas kernels, ffn(): pl.pallas_call(ffn_kernel, out_shape=(act, act, act, turned, turned, own,...  19.9 us
    dot_general x13, matrix products, dot_nn(): lax.dot_general(left, right, (((1,), (0,)), ((), ())), preferred_element_...  19.3 us
  transfers between devices with their start and end apart: 30, of which 12 were waited for; matrix products, arithmetic and copies ran while one was open for 16% of the time, Pallas kernels for 40%

profile of v1, /device:TPU:0, one launch (start us, length us, event | category | flops | bytes accessed | tf_op | source)
XLA Modules:
  0.0 488.1 jit_solution(4009420771108155578)
XLA Ops:
  0.7 3.1 collective-permute-start
  9.0 1.9 collective-permute-start.14
  11.0 1.1 constant_dynamic-slice_fusion.8
  12.3 1.6 collective-permute-done
  15.7 2.0 collective-permute-start.4
  19.4 1.1 fusion.28
  20.5 2.3 fusion.20
  22.8 22.0 %collective-permute-done.4 = bf16[768,768]{1,0:T(8,128)(2,1)} collective-permute-done((bf16[768,768]{1,0:T(8,128)(2,1)}, bf16[768,768]{1,0:T(8,128)(2,1)}, u32[]{:S(2)}, u32[]{:S(2)}) %collective-permute-start.4) | collective-permute-done | bytes 1179680 | tf_op jit(solution)/shard_map/ppermute | solution.py:736
  46.8 1.8 collective-permute-start.1
  49.6 1.7 collective-permute-start.3
  53.1 10.0 %collective-permute-done.2.k_got = bf16[128,768]{1,0:T(8,128)(2,1)S(1)} collective-permute-done((bf16[128,768]{1,0:T(8,128)(2,1)S(1)}, bf16[128,768]{1,0:T(8,128)(2,1)S(1)}, u32[]{:S(2)}, u32[]{:S(2)}) %collective-permute-start.2) | collective-permute-done | bytes 196640 | tf_op jit(solution)/shard_map/ppermute | solution.py:736
  63.1 1.7 collective-permute-start.8
  64.8 2.5 collective-permute-done.3.v_got
  68.0 2.7 rotary_kv.1.own
  71.6 42.4 %shard_map.257.k_ref.v_ref = bf16[2048,1536]{1,0:T(8,128)(2,1)S(1)} custom-call(bf16[128,1536]{1,0:T(8,128)(2,1)S(1)} %copy-done.3), custom_call_target="tpu_custom_call" | custom-call | bytes 314572800 | tf_op jit(solution)/shard_map/pallas_call | solution.py:550
  114.1 2.6 copy-done
  117.4 2.7 rotary_sum.1.q_ref
  120.1 13.7 %attention_forward.1 = (bf16[128,1536]{1,0:T(8,128)(2,1)}, f32[4,2,256]{2,1,0:T(2,128)}) custom-call(s32[32]{0:T(128)} %select_reduce_fusion.slot_of, s32[2]{0:T(128)} %get-tuple-element.71.owned, bf16[128,1536]{1,0:T(8,128)(2,1)} %rotary_sum.1.q_ref, bf16[2048,1536]{1,0:T(8,128)(2,1)} %copy-done, bf16[2048,1536]{1,0:T(8,128)(2,1)} %copy-done), custom_call_target="tpu_custom_call" | custom-call | flops 805306368 | bytes 6291456 | tf_op jit(solution)/shard_map/attention_forward/pallas_call | solution.py:238
  133.8 2.8 maximum_select_fusion.1
  137.0 3.2 multiply_reduce_fusion.2
  140.4 1.6 collective-permute-start.7
  143.0 2.3 copy.32
  145.3 1.8 constant_dynamic-slice_fusion.3
  148.3 4.2 collective-permute-done.7.n_other
  153.4 19.9 %ffn.1 = (bf16[256,2048]{1,0:T(8,128)(2,1)S(1)}, bf16[256,2048]{1,0:T(8,128)(2,1)S(1)}, bf16[256,2048]{1,0:T(8,128)(2,1)}, bf16[16,96,256]{2,1,0:T(8,128)(2,1)S(...) custom-call(s32[32]{0:T(128)S(1)} %pad_add_fusion.places, ...), custom_call_target="tpu_custom_call" | custom-call | flops 9663676416 | bytes 22020096 | tf_op jit(solution)/shard_map/ffn/pallas_call | solution.py:844
  174.4 2.8 convolution_convert_fusion.4
  178.2 2.7 convolution_convert_fusion.2
  180.8 1.5 collective-permute-start.9
  182.9 2.1 fusion.43
  184.9 2.1 fusion.42
  188.1 2.1 fusion.41
  190.1 2.6 convolution_convert_fusion
  192.7 6.7 %collective-permute-done.10 = bf16[128,1536]{1,0:T(8,128)(2,1)S(1)} collective-permute-done((bf16[128,1536]{1,0:T(8,128)(2,1)S(1)}, bf16[128,1536]{1,0:T(8,128)(2,1)S(1)}, u32[]{:S(2)}, u32[]{:S(2)}) %collective-permute-start.10) | collective-permute-done | bytes 393248 | tf_op jit(solution)/shard_map/ppermute | solution.py:736
  199.7 1.3 fusion.40
  202.2 3.7 convolution_convert_fusion.9.do_ref
  206.0 1.5 collective-permute-start.15
  207.5 21.9 %attention_backward.1 = (bf16[128,1536]{1,0:T(8,128)(2,1)}, bf16[16,128,768]{2,1,0:T(8,128)(2,1)}, bf16[16,128,768]{2,1,0:T(8,128)(2,1)}) custom-call(s32[32]{0:T(128)} %select_reduce_fusion.slot_of, s32[2]{0:T(128)} %get-tuple-element.71.owned, s32[32]{0:T(128)} %block_ids.1, bf16[128,1536]{1,0:T(8,128)(2,1)} %rotary_sum.1.q_ref, ...), custom_call_target="tpu_custom_call" | custom-call | flops 2013265920 | bytes 12582912 | tf_op jit(solution)/shard_map/attention_backward/pallas_call | solution.py:362
  230.0 2.1 fusion.21
  232.1 1.9 copy-done.1
  234.0 1.9 copy-done.2
  235.9 40.0 %shard_map.258 = (f32[128,768]{1,0:T(8,128)S(1)}, f32[128,768]{1,0:T(8,128)S(1)}) custom-call(bf16[16,128,768]{2,1,0:T(8,128)(2,1)S(1)} %copy-done.1, bf16[16,128,768]{2,1,0:T(8,128)(2,1)S(1)} %copy-done.2), custom_call_target="tpu_custom_call" | custom-call | bytes 314572800 | tf_op jit(solution)/shard_map/pallas_call | solution.py:715
  277.4 2.4 rotary_back.1
  279.9 1.6 collective-permute-start.12
  281.5 2.0 maximum_bitcast_fusion
  283.5 2.3 copy.31
  286.9 4.2 collective-permute-done.12
  295.7 1.6 collective-permute-start.13
  297.3 1.9 convolution_convert_fusion.8
  299.2 48.7 %shard_map.259 = (f32[48,1536]{1,0:T(8,128)S(1)}, f32[48,1536]{1,0:T(8,128)S(1)}, f32[48,1536]{1,0:T(8,128)S(1)}) custom-call(bf16[16,48,1536]{2,1,0:T(8,128)(2,1)S(1)} %bitcast.107, bf16[16,48,1536]{2,1,0:T(8,128)(2,1)S(1)} %bitcast.105, bf16[16,48,1536]{2,1,0:T(8,128)(2,1)S(1)} %bitcast.106), custom_call_target="tpu_custom_call" | custom-call | bytes 353894400 | tf_op jit(solution)/shard_map/pallas_call | solution.py:715
  349.9 3.4 fusion.5
  353.3 1.5 collective-permute-start.18
  354.9 1.6 fusion.3
  357.1 1.6 fusion.1
  358.7 1.5 collective-permute-start.27
  360.2 1.2 add_bitcast_fusion.3
  361.5 29.2 %collective-permute-done.18 = bf16[4,96,2048]{2,1,0:T(8,128)(2,1)S(1)} collective-permute-done((bf16[4,96,2048]{2,1,0:T(8,128)(2,1)S(1)}, bf16[4,96,2048]{2,1,0:T(8,128)(2,1)S(1)}, u32[]{:S(2)}, u32[]{:S(2)}) %collective-permute-start.18) | collective-permute-done | bytes 1572896 | tf_op jit(solution)/shard_map/ppermute | solution.py:741
  391.3 1.5 collective-permute-start.19
  392.8 30.3 %collective-permute-done.22 = bf16[4,96,2048]{2,1,0:T(8,128)(2,1)S(1)} collective-permute-done((bf16[4,96,2048]{2,1,0:T(8,128)(2,1)S(1)}, bf16[4,96,2048]{2,1,0:T(8,128)(2,1)S(1)}, u32[]{:S(2)}, u32[]{:S(2)}) %collective-permute-start.22) | collective-permute-done | bytes 1572896 | tf_op jit(solution)/shard_map/ppermute | solution.py:741
  423.8 1.2 collective-permute-start.23
  426.1 24.5 %collective-permute-done.23 = bf16[2,96,2048]{2,1,0:T(8,128)(2,1)S(1)} collective-permute-done((bf16[2,96,2048]{2,1,0:T(8,128)(2,1)S(1)}, bf16[2,96,2048]{2,1,0:T(8,128)(2,1)S(1)}, u32[]{:S(2)}, u32[]{:S(2)}) %collective-permute-start.23) | collective-permute-done | bytes 786464 | tf_op jit(solution)/shard_map/ppermute | solution.py:741
  450.8 3.0 collective-permute-start.29
  453.8 22.7 %collective-permute-done.24 = bf16[1,96,2048]{2,1,0:T(8,128)(2,1)S(1)} collective-permute-done((bf16[1,96,2048]{2,1,0:T(8,128)(2,1)S(1)}, bf16[1,96,2048]{2,1,0:T(8,128)(2,1)S(1)}, u32[]{:S(2)}, u32[]{:S(2)}) %collective-permute-start.24) | collective-permute-done | bytes 393248 | tf_op jit(solution)/shard_map/ppermute | solution.py:741
  476.6 2.8 add_reduce_fusion
  480.4 4.5 collective-permute-done.29
  (211 shorter events, 41.8 us)
Async XLA Ops:
  0.6 10.2 %copy-start.23 = (bf16[1,128,1536]{2,1,0:T(8,128)(2,1)S(1)}, bf16[1,128,1536]{2,1,0:T(8,128)(2,1)}, u32[]{:S(2)}) copy-start(bf16[1,128,1536]{2,1,0:T(8,128)(2,1)} %param.18) | copy-start | bytes 1179652
  0.7 10.3 %copy-start.47 = (bf16[768]{0:T(1024)(128)(2,1)S(1)}, bf16[768]{0:T(1024)(128)(2,1)}, u32[]{:S(2)}) copy-start(bf16[768]{0:T(1024)(128)(2,1)} %param.21) | copy-start | bytes 4612
  0.7 10.4 %copy-start.40 = (bf16[1536,768]{1,0:T(8,128)(2,1)S(1)}, bf16[1536,768]{1,0:T(8,128)(2,1)}, u32[]{:S(2)}) copy-start(bf16[1536,768]{1,0:T(8,128)(2,1)} %param.26) | copy-start | bytes 7077892
  0.7 13.2 %collective-permute-start = (bf16[128,1536]{1,0:T(8,128)(2,1)}, bf16[128,1536]{1,0:T(8,128)(2,1)S(1)}, u32[]{:S(2)}, u32[]{:S(2)}) collective-permute-start(bf16[128,1536]{1,0:T(8,128)(2,1)} %bitcast.121), channel_id=1, source_target_pairs={{0,1},{1,0},{2,3},{3,2},{4,5},{5,4},{6,7},{7,6},{8,9},{9,8},{10,11... | collective-permute-start | bytes 1179656 | tf_op jit(solution)/shard_map/ppermute | solution.py:736
  5.1 39.8 %collective-permute-start.6 = (bf16[2,768]{1,0:T(2,128)(2,1)S(1)}, bf16[2,768]{1,0:T(2,128)(2,1)S(1)}, u32[]{:S(2)}, u32[]{:S(2)}) collective-permute-start(bf16[2,768]{1,0:T(2,128)(2,1)S(1)} %pad_maximum_fusion.3), channel_id=1, source_target_pairs={{0,1},{1,0},{2,3},{3,2},{4,5},{5,4},{6,7},{7,6},{8,9},{9,8},{10,11... | collective-permute-start | bytes 9224 | tf_op jit(solution)/shard_map/ppermute | solution.py:736
  9.0 339.0 %collective-permute-start.14 = (bf16[48,3072]{1,0:T(8,128)(2,1)}, bf16[48,3072]{1,0:T(8,128)(2,1)}, u32[]{:S(2)}, u32[]{:S(2)}) collective-permute-start(bf16[48,3072]{1,0:T(8,128)(2,1)} %dynamic-slice_bitcast_fusion), channel_id=1, source_target_pairs={{0,1},{1,0},{2,3},{3,2},{4,5},{5,4},{6,7},{7,6},{8,9},{9,8},{10,11... | collective-permute-start | bytes 884744 | tf_op jit(solution)/shard_map/ppermute | solution.py:736
  12.3 2.6 copy-start.13
  14.2 3.5 copy-start.50
  14.2 4.9 %copy-start.53 = (s32[16]{0:T(128)S(1)}, s32[16]{0:T(128)}, u32[]{:S(2)}) copy-start(s32[16]{0:T(128)} %constant.103.clone) | copy-start | bytes 196
  14.3 4.9 %copy-start.54 = (s32[16]{0:T(128)S(1)}, s32[16]{0:T(128)}, u32[]{:S(2)}) copy-start(s32[16]{0:T(128)} %constant.104.clone) | copy-start | bytes 196
  14.3 5.1 %copy-start.51 = (f32[96]{0:T(128)S(1)}, f32[96]{0:T(128)}, u32[]{:S(2)}) copy-start(f32[96]{0:T(128)} %constant.106.clone) | copy-start | bytes 1156
  14.3 5.1 %copy-start.52 = (f32[96]{0:T(128)S(1)}, f32[96]{0:T(128)}, u32[]{:S(2)}) copy-start(f32[96]{0:T(128)} %constant.105.clone) | copy-start | bytes 1156
  14.3 6.2 %copy-start.48 = (f32[768]{0:T(1024)S(1)}, f32[768]{0:T(1024)}, u32[]{:S(2)}) copy-start(f32[768]{0:T(1024)} %constant.102.clone) | copy-start | bytes 9220
  14.3 6.2 %copy-start.49 = (f32[768]{0:T(1024)S(1)}, f32[768]{0:T(1024)}, u32[]{:S(2)}) copy-start(f32[768]{0:T(1024)} %constant.101.clone) | copy-start | bytes 9220
  14.4 31.6 %copy-start.11 = (bf16[768,1536]{1,0:T(8,128)(2,1)S(1)}, bf16[768,1536]{1,0:T(8,128)(2,1)}, u32[]{:S(2)}) copy-start(bf16[768,1536]{1,0:T(8,128)(2,1)} %param.23) | copy-start | bytes 7077892
  14.9 2.8 copy-start.34
  15.7 29.1 %collective-permute-start.4 = (bf16[768,768]{1,0:T(8,128)(2,1)}, bf16[768,768]{1,0:T(8,128)(2,1)}, u32[]{:S(2)}, u32[]{:S(2)}) collective-permute-start(bf16[768,768]{1,0:T(8,128)(2,1)} %constant_dynamic-slice_fusion.8), channel_id=1, source_target_pairs={{0,1},{1,0},{2,3},{3,2},{4,5},{5,4},{6,7},{7,6},{8,9},{9,8},{10,11... | collective-permute-start | bytes 3538952 | tf_op jit(solution)/shard_map/ppermute | solution.py:736
  44.8 89.0 %collective-permute-start.5 = (bf16[768,768]{1,0:T(8,128)(2,1)}, bf16[768,768]{1,0:T(8,128)(2,1)}, u32[]{:S(2)}, u32[]{:S(2)}) collective-permute-start(bf16[768,768]{1,0:T(8,128)(2,1)} %collective-permute-done.4), channel_id=1, source_target_pairs={{0,2},{2,0},{4,6},{6,4},{8,10},{10,8},{12,14},{14,12},{16,18},{18,... | collective-permute-start | bytes 3538952 | tf_op jit(solution)/shard_map/ppermute | solution.py:741
  46.0 2.7 copy-start.29
  46.8 16.3 %copy-start.4 = (bf16[1,128,1536]{2,1,0:T(8,128)(2,1)S(1)}, bf16[1,128,1536]{2,1,0:T(8,128)(2,1)}, u32[]{:S(2)}) copy-start(bf16[1,128,1536]{2,1,0:T(8,128)(2,1)} %param.19) | copy-start | bytes 1179652
  46.8 69.8 %collective-permute-start.1 = (bf16[128,1536]{1,0:T(8,128)(2,1)S(1)}, bf16[128,1536]{1,0:T(8,128)(2,1)S(1)}, u32[]{:S(2)}, u32[]{:S(2)}) collective-permute-start(bf16[128,1536]{1,0:T(8,128)(2,1)S(1)} %slice.340), channel_id=1, source_target_pairs={{0,1},{1,0},{2,3},{3,2},{4,5},{5,4},{6,7},{7,6},{8,9},{9,8},{10,11... | collective-permute-start | bytes 1179656 | tf_op jit(solution)/shard_map/ppermute | solution.py:736
  49.2 13.9 %collective-permute-start.2 = (bf16[128,768]{1,0:T(8,128)(2,1)S(1)}, bf16[128,768]{1,0:T(8,128)(2,1)S(1)}, u32[]{:S(2)}, u32[]{:S(2)}) collective-permute-start(bf16[128,768]{1,0:T(8,128)(2,1)S(1)} %slice.343), channel_id=1, source_target_pairs={{0,1},{1,0},{2,3},{3,2},{4,5},{5,4},{6,7},{7,6},{8,9},{9,8},{10,11... | collective-permute-start | bytes 589832 | tf_op jit(solution)/shard_map/ppermute | solution.py:736
  49.6 17.7 %collective-permute-start.3 = (bf16[128,768]{1,0:T(8,128)(2,1)S(1)}, bf16[128,768]{1,0:T(8,128)(2,1)S(1)}, u32[]{:S(2)}, u32[]{:S(2)}) collective-permute-start(bf16[128,768]{1,0:T(8,128)(2,1)S(1)} %slice.342), channel_id=1, source_target_pairs={{0,1},{1,0},{2,3},{3,2},{4,5},{5,4},{6,7},{7,6},{8,9},{9,8},{10,11... | collective-permute-start | bytes 589832 | tf_op jit(solution)/shard_map/ppermute | solution.py:736
  63.1 4.2 copy-start.45
  63.1 84.4 %collective-permute-start.8 = (bf16[128,1536]{1,0:T(8,128)(2,1)S(1)}, bf16[128,1536]{1,0:T(8,128)(2,1)S(1)}, u32[]{:S(2)}, u32[]{:S(2)}) collective-permute-start(bf16[128,1536]{1,0:T(8,128)(2,1)S(1)} %bitcast.108), channel_id=1, source_target_pairs={{0,1},{1,0},{2,3},{3,2},{4,5},{5,4},{6,7},{7,6},{8,9},{9,8},{10,11... | collective-permute-start | bytes 1179656 | tf_op jit(solution)/shard_map/ppermute | solution.py:736
  114.0 2.6 copy-start
  133.8 2.8 copy-start.24
  133.8 3.2 copy-start.41
  136.6 3.6 copy-start.35
  137.0 4.9 %copy-start.14 = (f32[128,1536]{1,0:T(8,128)S(1)}, f32[128,1536]{1,0:T(8,128)}, u32[]{:S(2)}) copy-start(f32[128,1536]{1,0:T(8,128)} %copy-done.13) | copy-start | bytes 2359300
  137.0 4.9 %copy-start.16 = (f32[128,1536]{1,0:T(8,128)S(1)}, f32[128,1536]{1,0:T(8,128)}, u32[]{:S(2)}) copy-start(f32[128,1536]{1,0:T(8,128)} %copy-done.15) | copy-start | bytes 2359300
  140.2 59.5 %copy-start.10 = (f32[128,1536]{1,0:T(8,128)}, f32[128,1536]{1,0:T(8,128)S(1)}, u32[]{:S(2)}) copy-start(f32[128,1536]{1,0:T(8,128)S(1)} %get-tuple-element.105) | copy-start | bytes 2359300
  140.4 12.1 %collective-permute-start.7 = (bf16[128,1536]{1,0:T(8,128)(2,1)S(1)}, bf16[128,1536]{1,0:T(8,128)(2,1)S(1)}, u32[]{:S(2)}, u32[]{:S(2)}) collective-permute-start(bf16[128,1536]{1,0:T(8,128)(2,1)S(1)} %multiply_convert_fusion.n_own), channel_id=1, source_target_pairs={{0,1},{1,0},{2,3},{3,2},{4,5},{5,4},{6,7},{7,6},{8,9},{9,8},{10,11... | collective-permute-start | bytes 1179656 | tf_op jit(solution)/shard_map/ppermute | solution.py:736
  142.0 10.5 %copy-start.5 = (bf16[1,128,1536]{2,1,0:T(8,128)(2,1)S(1)}, bf16[1,128,1536]{2,1,0:T(8,128)(2,1)}, u32[]{:S(2)}) copy-start(bf16[1,128,1536]{2,1,0:T(8,128)(2,1)} %param.19) | copy-start | bytes 1179652
  147.0 148.7 %collective-permute-start.16 = (bf16[128,1536]{1,0:T(8,128)(2,1)}, bf16[128,1536]{1,0:T(8,128)(2,1)}, u32[]{:S(2)}, u32[]{:S(2)}) collective-permute-start(bf16[128,1536]{1,0:T(8,128)(2,1)} %get-tuple-element.36.o_ref), channel_id=1, source_target_pairs={{0,1},{1,0},{2,3},{3,2},{4,5},{5,4},{6,7},{7,6},{8,9},{9,8},{10,11... | collective-permute-start | bytes 1179656 | tf_op jit(solution)/shard_map/ppermute | solution.py:736
  180.8 48.6 %collective-permute-start.9 = (bf16[128,1536]{1,0:T(8,128)(2,1)}, bf16[128,1536]{1,0:T(8,128)(2,1)}, u32[]{:S(2)}, u32[]{:S(2)}) collective-permute-start(bf16[128,1536]{1,0:T(8,128)(2,1)} %get-tuple-element.40), channel_id=1, source_target_pairs={{0,1},{1,0},{2,3},{3,2},{4,5},{5,4},{6,7},{7,6},{8,9},{9,8},{10,11... | collective-permute-start | bytes 1179656 | tf_op jit(solution)/shard_map/ppermute | solution.py:736
  182.4 17.1 %collective-permute-start.10 = (bf16[128,1536]{1,0:T(8,128)(2,1)S(1)}, bf16[128,1536]{1,0:T(8,128)(2,1)S(1)}, u32[]{:S(2)}, u32[]{:S(2)}) collective-permute-start(bf16[128,1536]{1,0:T(8,128)(2,1)S(1)} %get-tuple-element.42), channel_id=1, source_target_pairs={{0,1},{1,0},{2,3},{3,2},{4,5},{5,4},{6,7},{7,6},{8,9},{9,8},{10,11... | collective-permute-start | bytes 1179656 | tf_op jit(solution)/shard_map/ppermute | solution.py:736
  184.9 164.3 %collective-permute-start.17 = (bf16[8,96,2048]{2,1,0:T(8,128)(2,1)}, bf16[8,96,2048]{2,1,0:T(8,128)(2,1)}, u32[]{:S(2)}, u32[]{:S(2)}) collective-permute-start(bf16[8,96,2048]{2,1,0:T(8,128)(2,1)} %bitcast.22), channel_id=1, source_target_pairs={{0,2},{2,0},{4,6},{6,4},{8,10},{10,8},{12,14},{14,12},{16,18},{18,... | collective-permute-start | bytes 9437192 | tf_op jit(solution)/shard_map/ppermute | solution.py:741
  199.4 2.8 copy-start.42
  206.0 73.9 %collective-permute-start.15 = (bf16[128,1536]{1,0:T(8,128)(2,1)}, bf16[128,1536]{1,0:T(8,128)(2,1)}, u32[]{:S(2)}, u32[]{:S(2)}) collective-permute-start(bf16[128,1536]{1,0:T(8,128)(2,1)} %get-tuple-element.68), channel_id=1, source_target_pairs={{0,1},{1,0},{2,3},{3,2},{4,5},{5,4},{6,7},{7,6},{8,9},{9,8},{10,11... | collective-permute-start | bytes 1179656 | tf_op jit(solution)/shard_map/ppermute | solution.py:736
  229.4 56.4 %collective-permute-start.11 = (bf16[128,1536]{1,0:T(8,128)(2,1)}, bf16[128,1536]{1,0:T(8,128)(2,1)}, u32[]{:S(2)}, u32[]{:S(2)}) collective-permute-start(bf16[128,1536]{1,0:T(8,128)(2,1)} %get-tuple-element.44), channel_id=1, source_target_pairs={{0,1},{1,0},{2,3},{3,2},{4,5},{5,4},{6,7},{7,6},{8,9},{9,8},{10,11... | collective-permute-start | bytes 1179656 | tf_op jit(solution)/shard_map/ppermute | solution.py:736
  235.9 43.9 %copy-start.44 = (bf16[128,1536]{1,0:T(8,128)(2,1)S(1)}, bf16[128,1536]{1,0:T(8,128)(2,1)}, u32[]{:S(2)}) copy-start(bf16[128,1536]{1,0:T(8,128)(2,1)} %get-tuple-element.44) | copy-start | bytes 1179652
  279.8 11.2 %copy-start.26 = (bf16[128,1536]{1,0:T(8,128)(2,1)S(1)}, bf16[128,1536]{1,0:T(8,128)(2,1)}, u32[]{:S(2)}) copy-start(bf16[128,1536]{1,0:T(8,128)(2,1)} %rotary_back.1) | copy-start | bytes 1179652
  279.9 11.2 %copy-start.28 = (bf16[768,768]{1,0:T(8,128)(2,1)S(1)}, bf16[768,768]{1,0:T(8,128)(2,1)}, u32[]{:S(2)}) copy-start(bf16[768,768]{1,0:T(8,128)(2,1)} %param.25) | copy-start | bytes 3538948
  279.9 11.2 %collective-permute-start.12 = (bf16[128,1536]{1,0:T(8,128)(2,1)}, bf16[128,1536]{1,0:T(8,128)(2,1)S(1)}, u32[]{:S(2)}, u32[]{:S(2)}) collective-permute-start(bf16[128,1536]{1,0:T(8,128)(2,1)} %rotary_back.1), channel_id=1, source_target_pairs={{0,1},{1,0},{2,3},{3,2},{4,5},{5,4},{6,7},{7,6},{8,9},{9,8},{10,11... | collective-permute-start | bytes 1179656 | tf_op jit(solution)/shard_map/ppermute | solution.py:736
  283.5 8.1 %copy-start.32 = (bf16[16,1,48,256]{3,2,1,0:T(8,128)(2,1)S(1)}, bf16[16,1,48,256]{3,2,1,0:T(8,128)(2,1)}, u32[]{:S(2)}) copy-start(bf16[16,1,48,256]{3,2,1,0:T(8,128)(2,1)} %constant_dynamic-slice_fusion.3) | copy-start | bytes 1179652
  285.9 68.9 %collective-permute-start.21 = (bf16[8,96,2048]{2,1,0:T(8,128)(2,1)}, bf16[8,96,2048]{2,1,0:T(8,128)(2,1)S(1)}, u32[]{:S(2)}, u32[]{:S(2)}) collective-permute-start(bf16[8,96,2048]{2,1,0:T(8,128)(2,1)} %bitcast.26), channel_id=1, source_target_pairs={{0,2},{2,0},{4,6},{6,4},{8,10},{10,8},{12,14},{14,12},{16,18},{18,... | collective-permute-start | bytes 9437192 | tf_op jit(solution)/shard_map/ppermute | solution.py:741
  291.1 66.0 %collective-permute-start.26 = (bf16[8,96,2048]{2,1,0:T(8,128)(2,1)}, bf16[8,96,2048]{2,1,0:T(8,128)(2,1)S(1)}, u32[]{:S(2)}, u32[]{:S(2)}) collective-permute-start(bf16[8,96,2048]{2,1,0:T(8,128)(2,1)} %bitcast.36), channel_id=1, source_target_pairs={{0,2},{2,0},{4,6},{6,4},{8,10},{10,8},{12,14},{14,12},{16,18},{18,... | collective-permute-start | bytes 9437192 | tf_op jit(solution)/shard_map/ppermute | solution.py:741
  295.7 53.2 %collective-permute-start.13 = (bf16[128,768]{1,0:T(8,128)(2,1)S(1)}, bf16[128,768]{1,0:T(8,128)(2,1)S(1)}, u32[]{:S(2)}, u32[]{:S(2)}) collective-permute-start(bf16[128,768]{1,0:T(8,128)(2,1)S(1)} %slice.341), channel_id=1, source_target_pairs={{0,1},{1,0},{2,3},{3,2},{4,5},{5,4},{6,7},{7,6},{8,9},{9,8},{10,11... | collective-permute-start | bytes 589832 | tf_op jit(solution)/shard_map/ppermute | solution.py:736
  299.2 48.7 %copy-start.38 = (bf16[2,48,3072]{2,1,0:T(8,128)(2,1)S(1)}, bf16[2,48,3072]{2,1,0:T(8,128)(2,1)}, u32[]{:S(2)}) copy-start(bf16[2,48,3072]{2,1,0:T(8,128)(2,1)} %copy-done.37) | copy-start | bytes 1769476
  299.2 49.7 %copy-start.25 = (bf16[1,128,1536]{2,1,0:T(8,128)(2,1)S(1)}, bf16[1,128,1536]{2,1,0:T(8,128)(2,1)}, u32[]{:S(2)}) copy-start(bf16[1,128,1536]{2,1,0:T(8,128)(2,1)} %param.18) | copy-start | bytes 1179652
  349.9 4.9 %copy-start.19 = (bf16[384,2048]{1,0:T(8,128)(2,1)S(1)}, bf16[384,2048]{1,0:T(8,128)(2,1)}, u32[]{:S(2)}) copy-start(bf16[384,2048]{1,0:T(8,128)(2,1)} %get-tuple-element.82) | copy-start | bytes 4718596
  349.9 4.9 %copy-start.20 = (bf16[384,2048]{1,0:T(8,128)(2,1)S(1)}, bf16[384,2048]{1,0:T(8,128)(2,1)}, u32[]{:S(2)}) copy-start(bf16[384,2048]{1,0:T(8,128)(2,1)} %get-tuple-element.83) | copy-start | bytes 4718596
  353.3 37.3 %collective-permute-start.18 = (bf16[4,96,2048]{2,1,0:T(8,128)(2,1)S(1)}, bf16[4,96,2048]{2,1,0:T(8,128)(2,1)S(1)}, u32[]{:S(2)}, u32[]{:S(2)}) collective-permute-start(bf16[4,96,2048]{2,1,0:T(8,128)(2,1)S(1)} %get-tuple-element.87), channel_id=1, source_target_pairs={{0,4},{2,6},{4,0},{6,2},{8,12},{10,14},{12,8},{14,10},{16,20},{18,... | collective-permute-start | bytes 4718600 | tf_op jit(solution)/shard_map/ppermute | solution.py:741
  356.5 66.6 %collective-permute-start.22 = (bf16[4,96,2048]{2,1,0:T(8,128)(2,1)S(1)}, bf16[4,96,2048]{2,1,0:T(8,128)(2,1)S(1)}, u32[]{:S(2)}, u32[]{:S(2)}) collective-permute-start(bf16[4,96,2048]{2,1,0:T(8,128)(2,1)S(1)} %get-tuple-element.81), channel_id=1, source_target_pairs={{0,4},{2,6},{4,0},{6,2},{8,12},{10,14},{12,8},{14,10},{16,20},{18,... | collective-permute-start | bytes 4718600 | tf_op jit(solution)/shard_map/ppermute | solution.py:741
  357.1 3.1 copy-start.33
  358.7 66.2 %collective-permute-start.27 = (bf16[4,96,2048]{2,1,0:T(8,128)(2,1)S(1)}, bf16[4,96,2048]{2,1,0:T(8,128)(2,1)S(1)}, u32[]{:S(2)}, u32[]{:S(2)}) collective-permute-start(bf16[4,96,2048]{2,1,0:T(8,128)(2,1)S(1)} %get-tuple-element.75), channel_id=1, source_target_pairs={{0,8},{2,10},{4,12},{6,14},{8,0},{10,2},{12,4},{14,6},{16,24},{18,... | collective-permute-start | bytes 4718600 | tf_op jit(solution)/shard_map/ppermute | solution.py:741
  391.3 34.6 %collective-permute-start.19 = (bf16[2,96,2048]{2,1,0:T(8,128)(2,1)S(1)}, bf16[2,96,2048]{2,1,0:T(8,128)(2,1)S(1)}, u32[]{:S(2)}, u32[]{:S(2)}) collective-permute-start(bf16[2,96,2048]{2,1,0:T(8,128)(2,1)S(1)} %get-tuple-element.85), channel_id=1, source_target_pairs={{0,8},{2,10},{4,12},{6,14},{8,0},{10,2},{12,4},{14,6},{16,24},{18,... | collective-permute-start | bytes 2359304 | tf_op jit(solution)/shard_map/ppermute | solution.py:741
  423.8 26.8 %collective-permute-start.23 = (bf16[2,96,2048]{2,1,0:T(8,128)(2,1)S(1)}, bf16[2,96,2048]{2,1,0:T(8,128)(2,1)S(1)}, u32[]{:S(2)}, u32[]{:S(2)}) collective-permute-start(bf16[2,96,2048]{2,1,0:T(8,128)(2,1)S(1)} %get-tuple-element.79), channel_id=1, source_target_pairs={{0,8},{2,10},{4,12},{6,14},{8,0},{10,2},{12,4},{14,6},{16,24},{18,... | collective-permute-start | bytes 2359304 | tf_op jit(solution)/shard_map/ppermute | solution.py:741
  425.5 25.2 %collective-permute-start.28 = (bf16[2,96,2048]{2,1,0:T(8,128)(2,1)S(1)}, bf16[2,96,2048]{2,1,0:T(8,128)(2,1)S(1)}, u32[]{:S(2)}, u32[]{:S(2)}) collective-permute-start(bf16[2,96,2048]{2,1,0:T(8,128)(2,1)S(1)} %get-tuple-element.73), channel_id=1, source_target_pairs={{0,4},{2,6},{4,0},{6,2},{8,12},{10,14},{12,8},{14,10},{16,20},{18,... | collective-permute-start | bytes 2359304 | tf_op jit(solution)/shard_map/ppermute | solution.py:741
  426.0 27.8 %collective-permute-start.20 = (bf16[1,96,2048]{2,1,0:T(8,128)(2,1)S(1)}, bf16[1,96,2048]{2,1,0:T(8,128)(2,1)S(1)}, u32[]{:S(2)}, u32[]{:S(2)}) collective-permute-start(bf16[1,96,2048]{2,1,0:T(8,128)(2,1)S(1)} %add_convert_fusion.10), channel_id=1, source_target_pairs={{0,16},{2,18},{4,20},{6,22},{8,24},{10,26},{12,28},{14,30},{16,0},... | collective-permute-start | bytes 1179656 | tf_op jit(solution)/shard_map/ppermute | solution.py:741
  450.7 25.9 %collective-permute-start.24 = (bf16[1,96,2048]{2,1,0:T(8,128)(2,1)S(1)}, bf16[1,96,2048]{2,1,0:T(8,128)(2,1)S(1)}, u32[]{:S(2)}, u32[]{:S(2)}) collective-permute-start(bf16[1,96,2048]{2,1,0:T(8,128)(2,1)S(1)} %add_convert_fusion.8), channel_id=1, source_target_pairs={{0,16},{2,18},{4,20},{6,22},{8,24},{10,26},{12,28},{14,30},{16,0},... | collective-permute-start | bytes 1179656 | tf_op jit(solution)/shard_map/ppermute | solution.py:741
  450.8 34.0 %collective-permute-start.29 = (bf16[1,96,2048]{2,1,0:T(8,128)(2,1)S(1)}, bf16[1,96,2048]{2,1,0:T(8,128)(2,1)S(1)}, u32[]{:S(2)}, u32[]{:S(2)}) collective-permute-start(bf16[1,96,2048]{2,1,0:T(8,128)(2,1)S(1)} %add_convert_fusion.6), channel_id=1, source_target_pairs={{0,16},{2,18},{4,20},{6,22},{8,24},{10,26},{12,28},{14,30},{16,0},... | collective-permute-start | bytes 1179656 | tf_op jit(solution)/shard_map/ppermute | solution.py:741
  479.5 6.5 %collective-permute-start.25 = (f32[48]{0:T(128)S(1)}, f32[48]{0:T(128)S(1)}, u32[]{:S(2)}, u32[]{:S(2)}) collective-permute-start(f32[48]{0:T(128)S(1)} %fusion.33), channel_id=1, source_target_pairs={{0,1},{1,0},{2,3},{3,2},{4,5},{5,4},{6,7},{7,6},{8,9},{9,8},{10,11... | collective-permute-start | bytes 584 | tf_op jit(solution)/shard_map/ppermute | solution.py:736
  (21 other events, 30.6 us)

commit v2 on v1

--- a/solution.py
+++ b/solution.py
@@ -17,6 +17,7 @@
 LANES = 128
 PAIR_LANES = 256
 HEADS_STEP = 4
+CTX, FSDP = "ctx", "fsdp"
 TILE_BLOCKS = 4
 
 EPS = 1e-05
@@ -59,29 +60,6 @@
     return jnp.where(lower, pltpu.roll(value, width - half, 1), pltpu.roll(value, half, 1))
 
 
-def rotary_kernel(sign, first, second, cosine, sine, out):
-    total = first[...].astype(F32) + second[...].astype(F32)
-    out[...] = (total * cosine[...] + sign * swap_halves(total) * sine[...]).astype(BF16)
-
-
-def rotary_sum(first, second, cosine, sine):
-    rows, width = first.shape
-    part = cosine.shape[1]
-    spec = pl.BlockSpec((rows, part), lambda i: (0, i))
-    table = pl.BlockSpec((rows, part), lambda i: (0, 0))
-    return pl.pallas_call(
-        functools.partial(rotary_kernel, 1.0),
-        out_shape=jax.ShapeDtypeStruct((rows, width), BF16),
-        grid=(width // part,),
-        in_specs=[spec, spec, table, table],
-        out_specs=spec,
-        name="rotary_sum",
-        cost_estimate=pl.CostEstimate(
-            flops=6 * rows * width, bytes_accessed=8 * rows * width, transcendentals=0
-        ),
-    )(first, second, cosine, sine)
-
-
 def rotary_kv_kernel(k_own, k_got, v_own, v_got, cosine, sine, out):
     width = k_own.shape[1]
     keys = k_own[...] + k_got[...].astype(F32)
@@ -94,7 +72,6 @@
     return pl.pallas_call(
         rotary_kv_kernel,
         out_shape=jax.ShapeDtypeStruct((rows, 2 * width), BF16),
-        name="rotary_kv",
         cost_estimate=pl.CostEstimate(
             flops=8 * rows * width, bytes_accessed=20 * rows * width, transcendentals=0
         ),
@@ -113,7 +90,6 @@
     return pl.pallas_call(
         rotary_back_kernel,
         out_shape=jax.ShapeDtypeStruct((rows, 2 * width), BF16),
-        name="rotary_back",
         cost_estimate=pl.CostEstimate(
             flops=6 * rows * width, bytes_accessed=20 * rows * width, transcendentals=0
         ),
@@ -167,7 +143,11 @@
     return [upright[r * block : (r + 1) * block, :] for r in range(GROUP)]
 
 
-def forward_kernel(block, slot_of, owned, q_ref, k_ref, v_ref, o_ref, lse_ref, scores, acc, top, total):
+def forward_kernel(
+    block, slot_of, owned, q_own, q_got, cosine, sine, k_ref, v_ref, o_ref, lse_ref, q_ref, scores, acc, top, total
+):
+    query = q_own[...] + q_got[...].astype(F32)
+    q_ref[...] = (query * cosine[...] + swap_halves(query) * sine[...]).astype(BF16)
     tile_len = TILE_BLOCKS * block
     pairs = HEADS_STEP // 2
     columns = 2 * GROUP * block
@@ -227,25 +207,31 @@
     ]
 
 
-def attention_forward(query, all_kv, slot_of, owned, block):
-    rows = query.shape[0]
+def attention_forward(q_own, q_got, cosine, sine, all_kv, slot_of, owned, block):
+    rows = q_own.shape[0]
     length = all_kv.shape[0]
     steps = KEY_HEADS // HEADS_STEP
     pairs = HEADS_STEP // 2
     key_width = HEADS_STEP * HEAD_SIZE
     columns = 2 * GROUP * block
     query_spec = pl.BlockSpec((rows, key_width * GROUP), lambda i, *_: (0, i))
+    table = pl.BlockSpec(cosine.shape, lambda i, *_: (0, 0))
     return pl.pallas_call(
         functools.partial(forward_kernel, block),
         out_shape=(
-            jax.ShapeDtypeStruct(query.shape, BF16),
+            jax.ShapeDtypeStruct(q_own.shape, BF16),
             jax.ShapeDtypeStruct((KEY_HEADS // 2, 2, columns), F32),
+            jax.ShapeDtypeStruct(q_own.shape, BF16),
         ),
         grid_spec=pltpu.PrefetchScalarGridSpec(
             num_scalar_prefetch=2,
             grid=(steps,),
-            in_specs=[query_spec] + kv_specs(length, key_width),
-            out_specs=[query_spec, pl.BlockSpec((pairs, 2, columns), lambda i, *_: (i, 0, 0))],
+            in_specs=[query_spec, query_spec, table, table] + kv_specs(length, key_width),
+            out_specs=[
+                query_spec,
+                pl.BlockSpec((pairs, 2, columns), lambda i, *_: (i, 0, 0)),
+                query_spec,
+            ],
             scratch_shapes=[
                 pltpu.VMEM((pairs, length, columns), F32),
                 pltpu.VMEM((HEADS_STEP, HEAD_SIZE, GROUP * block), F32),
@@ -254,13 +240,12 @@
             ],
         ),
         compiler_params=pltpu.CompilerParams(vmem_limit_bytes=VMEM_BYTES),
-        name="attention_forward",
         cost_estimate=pl.CostEstimate(
-            flops=4 * rows * length * query.shape[1] // 2,
+            flops=4 * rows * length * q_own.shape[1] // 2,
             bytes_accessed=2 * all_kv.size,
             transcendentals=rows * length * QUERY_HEADS // 2,
         ),
-    )(slot_of, owned, query, all_kv, all_kv)
+    )(slot_of, owned, q_own, q_got, cosine, sine, all_kv, all_kv)
 
 
 def backward_kernel(
@@ -382,7 +367,6 @@
             ],
         ),
         compiler_params=pltpu.CompilerParams(vmem_limit_bytes=VMEM_BYTES),
-        name="attention_backward",
         cost_estimate=pl.CostEstimate(
             flops=10 * rows * length * query.shape[1] // 2,
             bytes_accessed=4 * all_kv.size,
@@ -392,12 +376,12 @@
 
 
 def place():
-    me = lax.axis_index("ctx")
+    me = lax.axis_index(CTX)
     return me // 4, me // 2 % 2, me % 2
 
 
 def device_at(line, mid, core):
-    return {"ctx": (line * 2 + mid) * 2 + core}
+    return {CTX: (line * 2 + mid) * 2 + core}
 
 
 def greet(line, mid, core, count):
@@ -543,7 +527,7 @@
 
 
 def gather_ctx(own, collective_id):
-    size = lax.axis_size("ctx")
+    size = lax.axis_size(CTX)
     rows, width = own.shape
     count = size // 4
     dma = pltpu.SemaphoreType.DMA
@@ -704,7 +688,7 @@
 
 
 def reduce_ctx(sources, collective_id):
-    size = lax.axis_size("ctx")
+    size = lax.axis_size(CTX)
     count = size // 4
     parts = len(sources)
     dma = pltpu.SemaphoreType.DMA
@@ -732,13 +716,13 @@
 
 
 def swap_fsdp(value):
-    size = lax.axis_size("fsdp")
-    return lax.ppermute(value, "fsdp", [(i, size - 1 - i) for i in range(size)])
+    size = lax.axis_size(FSDP)
+    return lax.ppermute(value, FSDP, [(i, size - 1 - i) for i in range(size)])
 
 
 def swap_bit(value, bit):
-    size = lax.axis_size("ctx")
-    return lax.ppermute(value, "ctx", [(i, i ^ (1 << bit)) for i in range(size)])
+    size = lax.axis_size(CTX)
+    return lax.ppermute(value, CTX, [(i, i ^ (1 << bit)) for i in range(size)])
 
 
 def bit_order(size, swapped=False):
@@ -757,7 +741,7 @@
 
 def chunk_places(bits):
     place_of = np.argsort(np.asarray(relative_order(bits))).astype(np.int32)
-    me = lax.axis_index("ctx")
+    me = lax.axis_index(CTX)
     distance = jnp.arange(len(place_of), dtype=jnp.int32) ^ me
     found = distance[:, None] == jnp.arange(len(place_of), dtype=jnp.int32)[None, :]
     return jnp.sum(jnp.where(found, jnp.asarray(place_of)[None, :], 0), axis=1)
@@ -858,7 +842,6 @@
             ],
         ),
         compiler_params=pltpu.CompilerParams(vmem_limit_bytes=2 * SMALL_VMEM_BYTES),
-        name="ffn",
         cost_estimate=pl.CostEstimate(
             flops=24 * rows * width * hidden,
             bytes_accessed=6 * width * hidden + 12 * rows * hidden,
@@ -868,10 +851,10 @@
 
 
 def side_parts(left, right):
-    size = lax.axis_size("ctx")
+    size = lax.axis_size(CTX)
     width, tokens = left.shape
     rows = width // (2 * size)
-    flat = pick(left.reshape(size, 2, rows, tokens), 1, lax.axis_index("fsdp"))
+    flat = pick(left.reshape(size, 2, rows, tokens), 1, lax.axis_index(FSDP))
     product = dot_nn(flat.reshape(size * rows, tokens), right).astype(BF16)
     return product.reshape(size, rows, right.shape[1])
 
@@ -904,11 +887,10 @@
     w_up,
     w_down,
 ):
-    ctx_size = lax.axis_size("ctx")
-    side = lax.axis_index("fsdp")
-    me = lax.axis_index("ctx")
+    ctx_size = lax.axis_size(CTX)
+    side = lax.axis_index(FSDP)
+    me = lax.axis_index(CTX)
     rows, width = block_input.shape[1:]
-    half_width = width // 2
     block = rows // 2
     block_count = 2 * ctx_size
 
@@ -940,6 +922,7 @@
     x_f = x_own.astype(F32)
     normed_one, inverse_one = norm_stats(x_f)
     normed_both = jnp.concatenate([normed_one, norm_stats(x_other.astype(F32))[0]], axis=0)
+    half_width = width // 2
     own_columns = lax.dynamic_slice_in_dim(normed_both, side * half_width, half_width, axis=1)
     left = (own_columns * gain_attn.astype(F32)).astype(BF16)
 
@@ -952,7 +935,6 @@
     q_own, q_got = partial_product(w_query)
     own_kv = rotary_kv(k_own, k_got, v_own, v_got, cosine, sine)
     all_kv = gather_ctx(own_kv, 1)
-    query = rotary_sum(q_own, q_got, cosine, sine)
 
     g_other = swap_fsdp(after(g_own, v_own))
     gains = jnp.stack([gain_attn, gain_ffn])
@@ -971,7 +953,7 @@
     full_out = by_side(w_out, out_other, 1)
     n1_turned = (normed_both * gain_one).astype(BF16).T
 
-    mixed, lse = attention_forward(query, all_kv, slot_of, owned, block)
+    mixed, lse, query = attention_forward(q_own, q_got, cosine, sine, all_kv, slot_of, owned, block)
     mixed_other = swap_fsdp(mixed)
     resid_mid = x_f + dot_nn(mixed, full_out)
     normed_two, inverse_two = norm_stats(resid_mid)
@@ -989,8 +971,7 @@
 
     mid_grad = g_own.astype(F32) + norm_back(n2_grad, normed_two, inverse_two, gain_two)
     mid_grad_b = mid_grad.astype(BF16)
-    mid_both = jnp.concatenate([mid_grad_b, swap_fsdp(mid_grad_b)], axis=0)
-    mixed_both = jnp.concatenate([mixed, mixed_other], axis=0)
+    mid_other = swap_fsdp(mid_grad_b)
     mixed_grad = dot_nt(mid_grad_b, full_out).astype(BF16)
     row_pos = jnp.concatenate([positions.reshape(2, block)] * GROUP, axis=1).astype(F32)
     turned_angles = row_pos[:, None, :] * jnp.asarray(frequency_row(HEAD_SIZE))[None, :, None]
@@ -1011,7 +992,10 @@
     )
     dk_sum, dv_sum = reduce_ctx([dk_parts, dv_parts], 2)
     dkv = rotary_back(dk_sum, dv_sum, cosine, sine)
-    block_output = (resid_mid + (ffn_own + after(ffn_got, dq).astype(F32))).astype(BF16)
+    ffn_got = after(ffn_got, dq)
+    mid_both = jnp.concatenate([mid_grad_b, mid_other], axis=0)
+    mixed_both = jnp.concatenate([mixed, mixed_other], axis=0)
+    block_output = (resid_mid + (ffn_own + ffn_got.astype(F32))).astype(BF16)
     dkv_both = jnp.concatenate([dkv, swap_fsdp(dkv)], axis=0)
     dq_both = jnp.concatenate([dq, swap_fsdp(dq)], axis=0)
 
@@ -1037,7 +1021,9 @@
     out_parts = side_parts(mid_both.T, mixed_both)
     query_parts = side_parts(n1_turned, dq_both)
     kv_parts = side_parts(n1_turned, dkv_both)
-    grad_out, grad_query, grad_kv = reduce_ctx([out_parts, query_parts, kv_parts], 3)
+    grad_out, grad_query, grad_kv = reduce_ctx(
+        [out_parts, query_parts, kv_parts], 3
+    )
     grad_out = grad_out.T
     grad_key, grad_value = grad_kv[:, :part], grad_kv[:, part:]
 
@@ -1068,35 +1054,13 @@
 
 
 def solution(mesh):
+    tokens, rows, columns, both = P(FSDP, CTX), P(FSDP), P(None, FSDP), P((CTX, FSDP))
     return jax.shard_map(
         local,
         mesh=mesh,
-        in_specs=(
-            P("fsdp", "ctx", None),
-            P("fsdp", "ctx", None),
-            P(),
-            P("fsdp"),
-            P("fsdp"),
-            P("fsdp", None),
-            P("fsdp", None),
-            P("fsdp", None),
-            P(None, "fsdp"),
-            P(None, "fsdp"),
-            P(None, "fsdp"),
-            P("fsdp", None),
-        ),
-        out_specs=(
-            P("fsdp", "ctx", None),
-            P("fsdp", "ctx", None),
-            P(("ctx", "fsdp")),
-            P(("ctx", "fsdp")),
-            P(("ctx", "fsdp"), None),
-            P(("ctx", "fsdp"), None),
-            P(("ctx", "fsdp"), None),
-            P(None, ("ctx", "fsdp")),
-            P("ctx", "fsdp"),
-            P("ctx", "fsdp"),
-            P("fsdp", "ctx"),
-        ),
+        in_specs=(tokens, tokens, P()) + (rows,) * 5 + (columns,) * 3 + (rows,),
+        out_specs=(tokens, tokens) + (both,) * 5 + (P(None, (CTX, FSDP)),)
+        + (P(CTX, FSDP),) * 2
+        + (P(FSDP, CTX),),
         check_vma=False,
     )

time: 497 us -> 495 us (level)
  no operation moved by 1% of the time
where the time goes in v2:
time: 495 us; the launch traced here: 486 us
  Pallas kernels  193 us (39%)
  waiting for transfers between devices  162 us (33%)
  local copies, waits for them, and re-layouts  41.5 us (8%)
  starting transfers between devices  33.1 us (7%)
  other arithmetic  30.2 us (6%)
  matrix products  24.9 us (5%)
    ppermute x13, waiting for transfers between devices, swap_bit(): return lax.ppermute(value, CTX, [(i, i ^ 1 << bit) for i in range(size)])  111 us
    pallas_call x2, Pallas kernels, reduce_ctx(): pl.pallas_call(functools.partial(reduce_kernel, count, parts), out_shape=...  88.7 us
    ppermute x17, waiting for transfers between devices, swap_fsdp(): return lax.ppermute(value, FSDP, [(i, size - 1 - i) for i in range(size)])  51.1 us
    pallas_call x1, Pallas kernels, gather_ctx(): pl.pallas_call(functools.partial(gather_kernel, count), out_shape=jax.Sha...  42.4 us
    ppermute x17, starting transfers between devices, swap_fsdp(): return lax.ppermute(value, FSDP, [(i, size - 1 - i) for i in range(size)])  23.2 us
    pallas_call x1, Pallas kernels, attention_backward(): pl.pallas_call(functools.partial(backward_kernel, block), out_shape=(jax....  21.9 us
    pallas_call x1, Pallas kernels, ffn(): pl.pallas_call(ffn_kernel, out_shape=(act, act, act, turned, turned, own,...  19.9 us
    dot_general x13, matrix products, dot_nn(): lax.dot_general(left, right, (((1,), (0,)), ((), ())), preferred_element_...  19.3 us
  transfers between devices with their start and end apart: 30, of which 12 were waited for; matrix products, arithmetic and copies ran while one was open for 16% of the time, Pallas kernels for 40%

profile of v2, /device:TPU:0, one launch (start us, length us, event | category | flops | bytes accessed | tf_op | source)
XLA Modules:
  0.0 486.4 jit_solution(1034075302818786793)
XLA Ops:
  0.7 3.1 collective-permute-start
  9.0 1.9 collective-permute-start.14
  11.0 1.1 constant_dynamic-slice_fusion.8
  12.3 1.6 collective-permute-done
  15.7 2.0 collective-permute-start.4
  19.4 1.1 fusion.28
  20.5 2.3 fusion.20
  22.8 22.0 %collective-permute-done.4 = bf16[768,768]{1,0:T(8,128)(2,1)} collective-permute-done((bf16[768,768]{1,0:T(8,128)(2,1)}, bf16[768,768]{1,0:T(8,128)(2,1)}, u32[]{:S(2)}, u32[]{:S(2)}) %collective-permute-start.4) | collective-permute-done | bytes 1179680 | tf_op jit(solution)/shard_map/ppermute | solution.py:720
  46.8 1.8 collective-permute-start.1
  49.6 1.7 collective-permute-start.3
  53.1 10.0 %collective-permute-done.2.k_got = bf16[128,768]{1,0:T(8,128)(2,1)S(1)} collective-permute-done((bf16[128,768]{1,0:T(8,128)(2,1)S(1)}, bf16[128,768]{1,0:T(8,128)(2,1)S(1)}, u32[]{:S(2)}, u32[]{:S(2)}) %collective-permute-start.2) | collective-permute-done | bytes 196640 | tf_op jit(solution)/shard_map/ppermute | solution.py:720
  63.1 1.7 collective-permute-start.8
  64.8 2.5 collective-permute-done.3.v_got
  68.0 2.7 shard_map.257.own
  71.6 42.4 %shard_map.258.k_ref.v_ref = bf16[2048,1536]{1,0:T(8,128)(2,1)S(1)} custom-call(bf16[128,1536]{1,0:T(8,128)(2,1)S(1)} %copy-done.3), custom_call_target="tpu_custom_call" | custom-call | bytes 314572800 | tf_op jit(solution)/shard_map/pallas_call | solution.py:534
  114.1 2.6 copy-done
  117.4 14.7 %shard_map.259 = (bf16[128,1536]{1,0:T(8,128)(2,1)}, f32[4,2,256]{2,1,0:T(2,128)}, bf16[128,1536]{1,0:T(8,128)(2,1)}) custom-call(s32[32]{0:T(128)} %select_reduce_fusion.slot_of, s32[2]{0:T(128)} %get-tuple-element.73.owned, f32[128,1536]{1,0:T(8,128)} %slice.236.q_own, bf16[128,1536]{1,0:T(8,128)(2,1)} %copy-done.44, f32[128,768]{1,0:T(8,128)} %get-tuple-element.99.cosine, ...), custom_call_target="tpu_custom_call" | custom-call | flops 805306368 | bytes 6291456 | tf_op jit(solution)/shard_map/pallas_call | solution.py:219
  132.2 2.8 maximum_select_fusion.1
  135.4 3.2 multiply_reduce_fusion.2
  138.7 1.6 collective-permute-start.7
  141.3 2.3 copy.32
  143.6 1.8 constant_dynamic-slice_fusion.3
  146.6 4.2 collective-permute-done.7.n_other
  151.8 19.9 %shard_map.260 = (bf16[256,2048]{1,0:T(8,128)(2,1)S(1)}, bf16[256,2048]{1,0:T(8,128)(2,1)S(1)}, bf16[256,2048]{1,0:T(8,128)(2,1)}, bf16[16,96,256]{2,1,0:T(8,128...) custom-call(s32[32]{0:T(128)S(1)} %pad_add_fusion.places, ...), custom_call_target="tpu_custom_call" | custom-call | flops 9663676416 | bytes 22020096 | tf_op jit(solution)/shard_map/pallas_call | solution.py:828
  172.7 2.8 convolution_convert_fusion.4
  176.5 2.7 convolution_convert_fusion.2
  179.2 1.5 collective-permute-start.9
  181.2 2.1 fusion.43
  183.3 2.1 fusion.42
  186.4 2.1 fusion.41
  188.4 2.6 convolution_convert_fusion
  191.1 6.7 %collective-permute-done.10 = bf16[128,1536]{1,0:T(8,128)(2,1)S(1)} collective-permute-done((bf16[128,1536]{1,0:T(8,128)(2,1)S(1)}, bf16[128,1536]{1,0:T(8,128)(2,1)S(1)}, u32[]{:S(2)}, u32[]{:S(2)}) %collective-permute-start.10) | collective-permute-done | bytes 393248 | tf_op jit(solution)/shard_map/ppermute | solution.py:720
  198.0 1.3 fusion.40
  200.5 3.7 convolution_convert_fusion.9.do_ref
  204.3 1.6 collective-permute-start.15
  205.8 21.9 %shard_map.261 = (bf16[128,1536]{1,0:T(8,128)(2,1)}, bf16[16,128,768]{2,1,0:T(8,128)(2,1)}, bf16[16,128,768]{2,1,0:T(8,128)(2,1)}) custom-call(s32[32]{0:T(128)} %select_reduce_fusion.slot_of, s32[2]{0:T(128)} %get-tuple-element.73.owned, s32[32]{0:T(128)} %block_ids.1, bf16[128,1536]{1,0:T(8,128)(2,1)} %get-tuple-element.42.q_ref, ...), custom_call_target="tpu_custom_call" | custom-call | flops 2013265920 | bytes 12582912 | tf_op jit(solution)/shard_map/pallas_call | solution.py:347
  228.3 2.1 fusion.21
  230.4 1.9 copy-done.1
  232.3 1.9 copy-done.2
  234.2 40.0 %shard_map.262 = (f32[128,768]{1,0:T(8,128)S(1)}, f32[128,768]{1,0:T(8,128)S(1)}) custom-call(bf16[16,128,768]{2,1,0:T(8,128)(2,1)S(1)} %copy-done.1, bf16[16,128,768]{2,1,0:T(8,128)(2,1)S(1)} %copy-done.2), custom_call_target="tpu_custom_call" | custom-call | bytes 314572800 | tf_op jit(solution)/shard_map/pallas_call | solution.py:699
  275.7 2.4 shard_map.263
  278.2 1.6 collective-permute-start.12
  279.8 2.0 maximum_bitcast_fusion
  281.9 2.3 copy.31
  284.2 1.0 constant_dynamic-update-slice_fusion
  285.2 4.1 collective-permute-done.12
  294.0 1.6 collective-permute-start.13
  295.7 1.9 convolution_convert_fusion.8
  297.6 48.7 %shard_map.264 = (f32[48,1536]{1,0:T(8,128)S(1)}, f32[48,1536]{1,0:T(8,128)S(1)}, f32[48,1536]{1,0:T(8,128)S(1)}) custom-call(bf16[16,48,1536]{2,1,0:T(8,128)(2,1)S(1)} %bitcast.107, bf16[16,48,1536]{2,1,0:T(8,128)(2,1)S(1)} %bitcast.105, bf16[16,48,1536]{2,1,0:T(8,128)(2,1)S(1)} %bitcast.106), custom_call_target="tpu_custom_call" | custom-call | bytes 353894400 | tf_op jit(solution)/shard_map/pallas_call | solution.py:699
  348.3 3.4 fusion.5
  351.6 1.5 collective-permute-start.18
  353.2 1.6 fusion.3
  355.5 1.6 fusion.1
  357.1 1.5 collective-permute-start.27
  358.6 1.2 add_bitcast_fusion.3
  359.8 29.2 %collective-permute-done.18 = bf16[4,96,2048]{2,1,0:T(8,128)(2,1)S(1)} collective-permute-done((bf16[4,96,2048]{2,1,0:T(8,128)(2,1)S(1)}, bf16[4,96,2048]{2,1,0:T(8,128)(2,1)S(1)}, u32[]{:S(2)}, u32[]{:S(2)}) %collective-permute-start.18) | collective-permute-done | bytes 1572896 | tf_op jit(solution)/shard_map/ppermute | solution.py:725
  389.6 1.5 collective-permute-start.19
  391.2 30.3 %collective-permute-done.22 = bf16[4,96,2048]{2,1,0:T(8,128)(2,1)S(1)} collective-permute-done((bf16[4,96,2048]{2,1,0:T(8,128)(2,1)S(1)}, bf16[4,96,2048]{2,1,0:T(8,128)(2,1)S(1)}, u32[]{:S(2)}, u32[]{:S(2)}) %collective-permute-start.22) | collective-permute-done | bytes 1572896 | tf_op jit(solution)/shard_map/ppermute | solution.py:725
  422.1 1.2 collective-permute-start.23
  424.4 24.5 %collective-permute-done.23 = bf16[2,96,2048]{2,1,0:T(8,128)(2,1)S(1)} collective-permute-done((bf16[2,96,2048]{2,1,0:T(8,128)(2,1)S(1)}, bf16[2,96,2048]{2,1,0:T(8,128)(2,1)S(1)}, u32[]{:S(2)}, u32[]{:S(2)}) %collective-permute-start.23) | collective-permute-done | bytes 786464 | tf_op jit(solution)/shard_map/ppermute | solution.py:725
  449.2 3.0 collective-permute-start.29
  452.2 22.7 %collective-permute-done.24 = bf16[1,96,2048]{2,1,0:T(8,128)(2,1)S(1)} collective-permute-done((bf16[1,96,2048]{2,1,0:T(8,128)(2,1)S(1)}, bf16[1,96,2048]{2,1,0:T(8,128)(2,1)S(1)}, u32[]{:S(2)}, u32[]{:S(2)}) %collective-permute-start.24) | collective-permute-done | bytes 393248 | tf_op jit(solution)/shard_map/ppermute | solution.py:725
  474.9 2.8 add_reduce_fusion
  478.7 4.5 collective-permute-done.29
  (210 shorter events, 40.7 us)
Async XLA Ops:
  0.6 10.2 %copy-start.23 = (bf16[1,128,1536]{2,1,0:T(8,128)(2,1)S(1)}, bf16[1,128,1536]{2,1,0:T(8,128)(2,1)}, u32[]{:S(2)}) copy-start(bf16[1,128,1536]{2,1,0:T(8,128)(2,1)} %param.18) | copy-start | bytes 1179652
  0.7 10.3 %copy-start.47 = (bf16[768]{0:T(1024)(128)(2,1)S(1)}, bf16[768]{0:T(1024)(128)(2,1)}, u32[]{:S(2)}) copy-start(bf16[768]{0:T(1024)(128)(2,1)} %param.21) | copy-start | bytes 4612
  0.7 10.4 %copy-start.40 = (bf16[1536,768]{1,0:T(8,128)(2,1)S(1)}, bf16[1536,768]{1,0:T(8,128)(2,1)}, u32[]{:S(2)}) copy-start(bf16[1536,768]{1,0:T(8,128)(2,1)} %param.26) | copy-start | bytes 7077892
  0.7 13.2 %collective-permute-start = (bf16[128,1536]{1,0:T(8,128)(2,1)}, bf16[128,1536]{1,0:T(8,128)(2,1)S(1)}, u32[]{:S(2)}, u32[]{:S(2)}) collective-permute-start(bf16[128,1536]{1,0:T(8,128)(2,1)} %bitcast.121), channel_id=1, source_target_pairs={{0,1},{1,0},{2,3},{3,2},{4,5},{5,4},{6,7},{7,6},{8,9},{9,8},{10,11... | collective-permute-start | bytes 1179656 | tf_op jit(solution)/shard_map/ppermute | solution.py:720
  5.1 39.8 %collective-permute-start.6 = (bf16[2,768]{1,0:T(2,128)(2,1)S(1)}, bf16[2,768]{1,0:T(2,128)(2,1)S(1)}, u32[]{:S(2)}, u32[]{:S(2)}) collective-permute-start(bf16[2,768]{1,0:T(2,128)(2,1)S(1)} %pad_maximum_fusion.3), channel_id=1, source_target_pairs={{0,1},{1,0},{2,3},{3,2},{4,5},{5,4},{6,7},{7,6},{8,9},{9,8},{10,11... | collective-permute-start | bytes 9224 | tf_op jit(solution)/shard_map/ppermute | solution.py:720
  9.0 337.3 %collective-permute-start.14 = (bf16[48,3072]{1,0:T(8,128)(2,1)}, bf16[48,3072]{1,0:T(8,128)(2,1)}, u32[]{:S(2)}, u32[]{:S(2)}) collective-permute-start(bf16[48,3072]{1,0:T(8,128)(2,1)} %dynamic-slice_bitcast_fusion), channel_id=1, source_target_pairs={{0,1},{1,0},{2,3},{3,2},{4,5},{5,4},{6,7},{7,6},{8,9},{9,8},{10,11... | collective-permute-start | bytes 884744 | tf_op jit(solution)/shard_map/ppermute | solution.py:720
  12.3 2.6 copy-start.13
  14.2 3.5 copy-start.50
  14.2 4.9 %copy-start.53 = (s32[16]{0:T(128)S(1)}, s32[16]{0:T(128)}, u32[]{:S(2)}) copy-start(s32[16]{0:T(128)} %constant.103.clone) | copy-start | bytes 196
  14.3 4.9 %copy-start.54 = (s32[16]{0:T(128)S(1)}, s32[16]{0:T(128)}, u32[]{:S(2)}) copy-start(s32[16]{0:T(128)} %constant.104.clone) | copy-start | bytes 196
  14.3 5.1 %copy-start.51 = (f32[96]{0:T(128)S(1)}, f32[96]{0:T(128)}, u32[]{:S(2)}) copy-start(f32[96]{0:T(128)} %constant.106.clone) | copy-start | bytes 1156
  14.3 5.1 %copy-start.52 = (f32[96]{0:T(128)S(1)}, f32[96]{0:T(128)}, u32[]{:S(2)}) copy-start(f32[96]{0:T(128)} %constant.105.clone) | copy-start | bytes 1156
  14.3 6.2 %copy-start.48 = (f32[768]{0:T(1024)S(1)}, f32[768]{0:T(1024)}, u32[]{:S(2)}) copy-start(f32[768]{0:T(1024)} %constant.102.clone) | copy-start | bytes 9220
  14.3 6.2 %copy-start.49 = (f32[768]{0:T(1024)S(1)}, f32[768]{0:T(1024)}, u32[]{:S(2)}) copy-start(f32[768]{0:T(1024)} %constant.101.clone) | copy-start | bytes 9220
  14.4 31.6 %copy-start.11 = (bf16[768,1536]{1,0:T(8,128)(2,1)S(1)}, bf16[768,1536]{1,0:T(8,128)(2,1)}, u32[]{:S(2)}) copy-start(bf16[768,1536]{1,0:T(8,128)(2,1)} %param.23) | copy-start | bytes 7077892
  14.9 2.8 copy-start.34
  15.7 29.1 %collective-permute-start.4 = (bf16[768,768]{1,0:T(8,128)(2,1)}, bf16[768,768]{1,0:T(8,128)(2,1)}, u32[]{:S(2)}, u32[]{:S(2)}) collective-permute-start(bf16[768,768]{1,0:T(8,128)(2,1)} %constant_dynamic-slice_fusion.8), channel_id=1, source_target_pairs={{0,1},{1,0},{2,3},{3,2},{4,5},{5,4},{6,7},{7,6},{8,9},{9,8},{10,11... | collective-permute-start | bytes 3538952 | tf_op jit(solution)/shard_map/ppermute | solution.py:720
  44.8 87.3 %collective-permute-start.5 = (bf16[768,768]{1,0:T(8,128)(2,1)}, bf16[768,768]{1,0:T(8,128)(2,1)}, u32[]{:S(2)}, u32[]{:S(2)}) collective-permute-start(bf16[768,768]{1,0:T(8,128)(2,1)} %collective-permute-done.4), channel_id=1, source_target_pairs={{0,2},{2,0},{4,6},{6,4},{8,10},{10,8},{12,14},{14,12},{16,18},{18,... | collective-permute-start | bytes 3538952 | tf_op jit(solution)/shard_map/ppermute | solution.py:725
  46.0 2.7 copy-start.29
  46.8 16.3 %copy-start.4 = (bf16[1,128,1536]{2,1,0:T(8,128)(2,1)S(1)}, bf16[1,128,1536]{2,1,0:T(8,128)(2,1)}, u32[]{:S(2)}) copy-start(bf16[1,128,1536]{2,1,0:T(8,128)(2,1)} %param.19) | copy-start | bytes 1179652
  46.8 69.8 %collective-permute-start.1 = (bf16[128,1536]{1,0:T(8,128)(2,1)S(1)}, bf16[128,1536]{1,0:T(8,128)(2,1)S(1)}, u32[]{:S(2)}, u32[]{:S(2)}) collective-permute-start(bf16[128,1536]{1,0:T(8,128)(2,1)S(1)} %slice.340), channel_id=1, source_target_pairs={{0,1},{1,0},{2,3},{3,2},{4,5},{5,4},{6,7},{7,6},{8,9},{9,8},{10,11... | collective-permute-start | bytes 1179656 | tf_op jit(solution)/shard_map/ppermute | solution.py:720
  49.2 13.9 %collective-permute-start.2 = (bf16[128,768]{1,0:T(8,128)(2,1)S(1)}, bf16[128,768]{1,0:T(8,128)(2,1)S(1)}, u32[]{:S(2)}, u32[]{:S(2)}) collective-permute-start(bf16[128,768]{1,0:T(8,128)(2,1)S(1)} %slice.343), channel_id=1, source_target_pairs={{0,1},{1,0},{2,3},{3,2},{4,5},{5,4},{6,7},{7,6},{8,9},{9,8},{10,11... | collective-permute-start | bytes 589832 | tf_op jit(solution)/shard_map/ppermute | solution.py:720
  49.6 17.7 %collective-permute-start.3 = (bf16[128,768]{1,0:T(8,128)(2,1)S(1)}, bf16[128,768]{1,0:T(8,128)(2,1)S(1)}, u32[]{:S(2)}, u32[]{:S(2)}) collective-permute-start(bf16[128,768]{1,0:T(8,128)(2,1)S(1)} %slice.342), channel_id=1, source_target_pairs={{0,1},{1,0},{2,3},{3,2},{4,5},{5,4},{6,7},{7,6},{8,9},{9,8},{10,11... | collective-permute-start | bytes 589832 | tf_op jit(solution)/shard_map/ppermute | solution.py:720
  63.1 4.2 copy-start.45
  63.1 82.8 %collective-permute-start.8 = (bf16[128,1536]{1,0:T(8,128)(2,1)S(1)}, bf16[128,1536]{1,0:T(8,128)(2,1)S(1)}, u32[]{:S(2)}, u32[]{:S(2)}) collective-permute-start(bf16[128,1536]{1,0:T(8,128)(2,1)S(1)} %bitcast.108), channel_id=1, source_target_pairs={{0,1},{1,0},{2,3},{3,2},{4,5},{5,4},{6,7},{7,6},{8,9},{9,8},{10,11... | collective-permute-start | bytes 1179656 | tf_op jit(solution)/shard_map/ppermute | solution.py:720
  114.0 2.6 copy-start
  132.1 2.8 copy-start.24
  132.1 3.2 copy-start.41
  134.9 3.6 copy-start.35
  135.4 4.9 %copy-start.14 = (f32[128,1536]{1,0:T(8,128)S(1)}, f32[128,1536]{1,0:T(8,128)}, u32[]{:S(2)}) copy-start(f32[128,1536]{1,0:T(8,128)} %copy-done.13) | copy-start | bytes 2359300
  135.4 4.9 %copy-start.16 = (f32[128,1536]{1,0:T(8,128)S(1)}, f32[128,1536]{1,0:T(8,128)}, u32[]{:S(2)}) copy-start(f32[128,1536]{1,0:T(8,128)} %copy-done.15) | copy-start | bytes 2359300
  138.5 59.5 %copy-start.10 = (f32[128,1536]{1,0:T(8,128)}, f32[128,1536]{1,0:T(8,128)S(1)}, u32[]{:S(2)}) copy-start(f32[128,1536]{1,0:T(8,128)S(1)} %get-tuple-element.107) | copy-start | bytes 2359300
  138.7 12.1 %collective-permute-start.7 = (bf16[128,1536]{1,0:T(8,128)(2,1)S(1)}, bf16[128,1536]{1,0:T(8,128)(2,1)S(1)}, u32[]{:S(2)}, u32[]{:S(2)}) collective-permute-start(bf16[128,1536]{1,0:T(8,128)(2,1)S(1)} %multiply_convert_fusion.n_own), channel_id=1, source_target_pairs={{0,1},{1,0},{2,3},{3,2},{4,5},{5,4},{6,7},{7,6},{8,9},{9,8},{10,11... | collective-permute-start | bytes 1179656 | tf_op jit(solution)/shard_map/ppermute | solution.py:720
  140.3 10.5 %copy-start.5 = (bf16[1,128,1536]{2,1,0:T(8,128)(2,1)S(1)}, bf16[1,128,1536]{2,1,0:T(8,128)(2,1)}, u32[]{:S(2)}) copy-start(bf16[1,128,1536]{2,1,0:T(8,128)(2,1)} %param.19) | copy-start | bytes 1179652
  145.3 148.7 %collective-permute-start.16 = (bf16[128,1536]{1,0:T(8,128)(2,1)}, bf16[128,1536]{1,0:T(8,128)(2,1)}, u32[]{:S(2)}, u32[]{:S(2)}) collective-permute-start(bf16[128,1536]{1,0:T(8,128)(2,1)} %get-tuple-element.37.o_ref), channel_id=1, source_target_pairs={{0,1},{1,0},{2,3},{3,2},{4,5},{5,4},{6,7},{7,6},{8,9},{9,8},{10,11... | collective-permute-start | bytes 1179656 | tf_op jit(solution)/shard_map/ppermute | solution.py:720
  179.2 48.6 %collective-permute-start.9 = (bf16[128,1536]{1,0:T(8,128)(2,1)}, bf16[128,1536]{1,0:T(8,128)(2,1)}, u32[]{:S(2)}, u32[]{:S(2)}) collective-permute-start(bf16[128,1536]{1,0:T(8,128)(2,1)} %get-tuple-element.41), channel_id=1, source_target_pairs={{0,1},{1,0},{2,3},{3,2},{4,5},{5,4},{6,7},{7,6},{8,9},{9,8},{10,11... | collective-permute-start | bytes 1179656 | tf_op jit(solution)/shard_map/ppermute | solution.py:720
  180.7 17.1 %collective-permute-start.10 = (bf16[128,1536]{1,0:T(8,128)(2,1)S(1)}, bf16[128,1536]{1,0:T(8,128)(2,1)S(1)}, u32[]{:S(2)}, u32[]{:S(2)}) collective-permute-start(bf16[128,1536]{1,0:T(8,128)(2,1)S(1)} %get-tuple-element.44), channel_id=1, source_target_pairs={{0,1},{1,0},{2,3},{3,2},{4,5},{5,4},{6,7},{7,6},{8,9},{9,8},{10,11... | collective-permute-start | bytes 1179656 | tf_op jit(solution)/shard_map/ppermute | solution.py:720
  183.3 164.3 %collective-permute-start.17 = (bf16[8,96,2048]{2,1,0:T(8,128)(2,1)}, bf16[8,96,2048]{2,1,0:T(8,128)(2,1)}, u32[]{:S(2)}, u32[]{:S(2)}) collective-permute-start(bf16[8,96,2048]{2,1,0:T(8,128)(2,1)} %bitcast.22), channel_id=1, source_target_pairs={{0,2},{2,0},{4,6},{6,4},{8,10},{10,8},{12,14},{14,12},{16,18},{18,... | collective-permute-start | bytes 9437192 | tf_op jit(solution)/shard_map/ppermute | solution.py:725
  197.7 2.8 copy-start.42
  204.3 73.9 %collective-permute-start.15 = (bf16[128,1536]{1,0:T(8,128)(2,1)}, bf16[128,1536]{1,0:T(8,128)(2,1)}, u32[]{:S(2)}, u32[]{:S(2)}) collective-permute-start(bf16[128,1536]{1,0:T(8,128)(2,1)} %get-tuple-element.70), channel_id=1, source_target_pairs={{0,1},{1,0},{2,3},{3,2},{4,5},{5,4},{6,7},{7,6},{8,9},{9,8},{10,11... | collective-permute-start | bytes 1179656 | tf_op jit(solution)/shard_map/ppermute | solution.py:720
  227.8 56.4 %collective-permute-start.11 = (bf16[128,1536]{1,0:T(8,128)(2,1)}, bf16[128,1536]{1,0:T(8,128)(2,1)}, u32[]{:S(2)}, u32[]{:S(2)}) collective-permute-start(bf16[128,1536]{1,0:T(8,128)(2,1)} %get-tuple-element.46), channel_id=1, source_target_pairs={{0,1},{1,0},{2,3},{3,2},{4,5},{5,4},{6,7},{7,6},{8,9},{9,8},{10,11... | collective-permute-start | bytes 1179656 | tf_op jit(solution)/shard_map/ppermute | solution.py:720
  234.2 43.9 %copy-start.43 = (bf16[128,1536]{1,0:T(8,128)(2,1)S(1)}, bf16[128,1536]{1,0:T(8,128)(2,1)}, u32[]{:S(2)}) copy-start(bf16[128,1536]{1,0:T(8,128)(2,1)} %get-tuple-element.46) | copy-start | bytes 1179652
  278.1 11.2 %copy-start.26 = (bf16[128,1536]{1,0:T(8,128)(2,1)S(1)}, bf16[128,1536]{1,0:T(8,128)(2,1)}, u32[]{:S(2)}) copy-start(bf16[128,1536]{1,0:T(8,128)(2,1)} %shard_map.263) | copy-start | bytes 1179652
  278.1 11.2 %copy-start.28 = (bf16[768,768]{1,0:T(8,128)(2,1)S(1)}, bf16[768,768]{1,0:T(8,128)(2,1)}, u32[]{:S(2)}) copy-start(bf16[768,768]{1,0:T(8,128)(2,1)} %param.25) | copy-start | bytes 3538948
  278.2 11.2 %collective-permute-start.12 = (bf16[128,1536]{1,0:T(8,128)(2,1)}, bf16[128,1536]{1,0:T(8,128)(2,1)S(1)}, u32[]{:S(2)}, u32[]{:S(2)}) collective-permute-start(bf16[128,1536]{1,0:T(8,128)(2,1)} %shard_map.263), channel_id=1, source_target_pairs={{0,1},{1,0},{2,3},{3,2},{4,5},{5,4},{6,7},{7,6},{8,9},{9,8},{10,11... | collective-permute-start | bytes 1179656 | tf_op jit(solution)/shard_map/ppermute | solution.py:720
  281.9 8.0 %copy-start.32 = (bf16[16,1,48,256]{3,2,1,0:T(8,128)(2,1)S(1)}, bf16[16,1,48,256]{3,2,1,0:T(8,128)(2,1)}, u32[]{:S(2)}) copy-start(bf16[16,1,48,256]{3,2,1,0:T(8,128)(2,1)} %constant_dynamic-slice_fusion.3) | copy-start | bytes 1179652
  284.2 68.9 %collective-permute-start.21 = (bf16[8,96,2048]{2,1,0:T(8,128)(2,1)}, bf16[8,96,2048]{2,1,0:T(8,128)(2,1)S(1)}, u32[]{:S(2)}, u32[]{:S(2)}) collective-permute-start(bf16[8,96,2048]{2,1,0:T(8,128)(2,1)} %bitcast.26), channel_id=1, source_target_pairs={{0,2},{2,0},{4,6},{6,4},{8,10},{10,8},{12,14},{14,12},{16,18},{18,... | collective-permute-start | bytes 9437192 | tf_op jit(solution)/shard_map/ppermute | solution.py:725
  289.4 66.1 %collective-permute-start.26 = (bf16[8,96,2048]{2,1,0:T(8,128)(2,1)}, bf16[8,96,2048]{2,1,0:T(8,128)(2,1)S(1)}, u32[]{:S(2)}, u32[]{:S(2)}) collective-permute-start(bf16[8,96,2048]{2,1,0:T(8,128)(2,1)} %bitcast.36), channel_id=1, source_target_pairs={{0,2},{2,0},{4,6},{6,4},{8,10},{10,8},{12,14},{14,12},{16,18},{18,... | collective-permute-start | bytes 9437192 | tf_op jit(solution)/shard_map/ppermute | solution.py:725
  294.0 53.2 %collective-permute-start.13 = (bf16[128,768]{1,0:T(8,128)(2,1)S(1)}, bf16[128,768]{1,0:T(8,128)(2,1)S(1)}, u32[]{:S(2)}, u32[]{:S(2)}) collective-permute-start(bf16[128,768]{1,0:T(8,128)(2,1)S(1)} %slice.341), channel_id=1, source_target_pairs={{0,1},{1,0},{2,3},{3,2},{4,5},{5,4},{6,7},{7,6},{8,9},{9,8},{10,11... | collective-permute-start | bytes 589832 | tf_op jit(solution)/shard_map/ppermute | solution.py:720
  297.6 48.7 %copy-start.38 = (bf16[2,48,3072]{2,1,0:T(8,128)(2,1)S(1)}, bf16[2,48,3072]{2,1,0:T(8,128)(2,1)}, u32[]{:S(2)}) copy-start(bf16[2,48,3072]{2,1,0:T(8,128)(2,1)} %copy-done.37) | copy-start | bytes 1769476
  297.6 49.7 %copy-start.25 = (bf16[1,128,1536]{2,1,0:T(8,128)(2,1)S(1)}, bf16[1,128,1536]{2,1,0:T(8,128)(2,1)}, u32[]{:S(2)}) copy-start(bf16[1,128,1536]{2,1,0:T(8,128)(2,1)} %param.18) | copy-start | bytes 1179652
  348.2 4.9 %copy-start.19 = (bf16[384,2048]{1,0:T(8,128)(2,1)S(1)}, bf16[384,2048]{1,0:T(8,128)(2,1)}, u32[]{:S(2)}) copy-start(bf16[384,2048]{1,0:T(8,128)(2,1)} %get-tuple-element.84) | copy-start | bytes 4718596
  348.2 4.9 %copy-start.20 = (bf16[384,2048]{1,0:T(8,128)(2,1)S(1)}, bf16[384,2048]{1,0:T(8,128)(2,1)}, u32[]{:S(2)}) copy-start(bf16[384,2048]{1,0:T(8,128)(2,1)} %get-tuple-element.85) | copy-start | bytes 4718596
  351.6 37.3 %collective-permute-start.18 = (bf16[4,96,2048]{2,1,0:T(8,128)(2,1)S(1)}, bf16[4,96,2048]{2,1,0:T(8,128)(2,1)S(1)}, u32[]{:S(2)}, u32[]{:S(2)}) collective-permute-start(bf16[4,96,2048]{2,1,0:T(8,128)(2,1)S(1)} %get-tuple-element.89), channel_id=1, source_target_pairs={{0,4},{2,6},{4,0},{6,2},{8,12},{10,14},{12,8},{14,10},{16,20},{18,... | collective-permute-start | bytes 4718600 | tf_op jit(solution)/shard_map/ppermute | solution.py:725
  354.8 66.6 %collective-permute-start.22 = (bf16[4,96,2048]{2,1,0:T(8,128)(2,1)S(1)}, bf16[4,96,2048]{2,1,0:T(8,128)(2,1)S(1)}, u32[]{:S(2)}, u32[]{:S(2)}) collective-permute-start(bf16[4,96,2048]{2,1,0:T(8,128)(2,1)S(1)} %get-tuple-element.83), channel_id=1, source_target_pairs={{0,4},{2,6},{4,0},{6,2},{8,12},{10,14},{12,8},{14,10},{16,20},{18,... | collective-permute-start | bytes 4718600 | tf_op jit(solution)/shard_map/ppermute | solution.py:725
  355.4 3.1 copy-start.33
  357.1 66.2 %collective-permute-start.27 = (bf16[4,96,2048]{2,1,0:T(8,128)(2,1)S(1)}, bf16[4,96,2048]{2,1,0:T(8,128)(2,1)S(1)}, u32[]{:S(2)}, u32[]{:S(2)}) collective-permute-start(bf16[4,96,2048]{2,1,0:T(8,128)(2,1)S(1)} %get-tuple-element.77), channel_id=1, source_target_pairs={{0,8},{2,10},{4,12},{6,14},{8,0},{10,2},{12,4},{14,6},{16,24},{18,... | collective-permute-start | bytes 4718600 | tf_op jit(solution)/shard_map/ppermute | solution.py:725
  389.6 34.6 %collective-permute-start.19 = (bf16[2,96,2048]{2,1,0:T(8,128)(2,1)S(1)}, bf16[2,96,2048]{2,1,0:T(8,128)(2,1)S(1)}, u32[]{:S(2)}, u32[]{:S(2)}) collective-permute-start(bf16[2,96,2048]{2,1,0:T(8,128)(2,1)S(1)} %get-tuple-element.87), channel_id=1, source_target_pairs={{0,8},{2,10},{4,12},{6,14},{8,0},{10,2},{12,4},{14,6},{16,24},{18,... | collective-permute-start | bytes 2359304 | tf_op jit(solution)/shard_map/ppermute | solution.py:725
  422.1 26.8 %collective-permute-start.23 = (bf16[2,96,2048]{2,1,0:T(8,128)(2,1)S(1)}, bf16[2,96,2048]{2,1,0:T(8,128)(2,1)S(1)}, u32[]{:S(2)}, u32[]{:S(2)}) collective-permute-start(bf16[2,96,2048]{2,1,0:T(8,128)(2,1)S(1)} %get-tuple-element.81), channel_id=1, source_target_pairs={{0,8},{2,10},{4,12},{6,14},{8,0},{10,2},{12,4},{14,6},{16,24},{18,... | collective-permute-start | bytes 2359304 | tf_op jit(solution)/shard_map/ppermute | solution.py:725
  423.9 25.2 %collective-permute-start.28 = (bf16[2,96,2048]{2,1,0:T(8,128)(2,1)S(1)}, bf16[2,96,2048]{2,1,0:T(8,128)(2,1)S(1)}, u32[]{:S(2)}, u32[]{:S(2)}) collective-permute-start(bf16[2,96,2048]{2,1,0:T(8,128)(2,1)S(1)} %get-tuple-element.75), channel_id=1, source_target_pairs={{0,4},{2,6},{4,0},{6,2},{8,12},{10,14},{12,8},{14,10},{16,20},{18,... | collective-permute-start | bytes 2359304 | tf_op jit(solution)/shard_map/ppermute | solution.py:725
  424.3 27.8 %collective-permute-start.20 = (bf16[1,96,2048]{2,1,0:T(8,128)(2,1)S(1)}, bf16[1,96,2048]{2,1,0:T(8,128)(2,1)S(1)}, u32[]{:S(2)}, u32[]{:S(2)}) collective-permute-start(bf16[1,96,2048]{2,1,0:T(8,128)(2,1)S(1)} %add_convert_fusion.10), channel_id=1, source_target_pairs={{0,16},{2,18},{4,20},{6,22},{8,24},{10,26},{12,28},{14,30},{16,0},... | collective-permute-start | bytes 1179656 | tf_op jit(solution)/shard_map/ppermute | solution.py:725
  449.0 25.9 %collective-permute-start.24 = (bf16[1,96,2048]{2,1,0:T(8,128)(2,1)S(1)}, bf16[1,96,2048]{2,1,0:T(8,128)(2,1)S(1)}, u32[]{:S(2)}, u32[]{:S(2)}) collective-permute-start(bf16[1,96,2048]{2,1,0:T(8,128)(2,1)S(1)} %add_convert_fusion.8), channel_id=1, source_target_pairs={{0,16},{2,18},{4,20},{6,22},{8,24},{10,26},{12,28},{14,30},{16,0},... | collective-permute-start | bytes 1179656 | tf_op jit(solution)/shard_map/ppermute | solution.py:725
  449.2 34.0 %collective-permute-start.29 = (bf16[1,96,2048]{2,1,0:T(8,128)(2,1)S(1)}, bf16[1,96,2048]{2,1,0:T(8,128)(2,1)S(1)}, u32[]{:S(2)}, u32[]{:S(2)}) collective-permute-start(bf16[1,96,2048]{2,1,0:T(8,128)(2,1)S(1)} %add_convert_fusion.6), channel_id=1, source_target_pairs={{0,16},{2,18},{4,20},{6,22},{8,24},{10,26},{12,28},{14,30},{16,0},... | collective-permute-start | bytes 1179656 | tf_op jit(solution)/shard_map/ppermute | solution.py:725
  477.8 6.5 %collective-permute-start.25 = (f32[48]{0:T(128)S(1)}, f32[48]{0:T(128)S(1)}, u32[]{:S(2)}, u32[]{:S(2)}) collective-permute-start(f32[48]{0:T(128)S(1)} %fusion.33), channel_id=1, source_target_pairs={{0,1},{1,0},{2,3},{3,2},{4,5},{5,4},{6,7},{7,6},{8,9},{9,8},{10,11... | collective-permute-start | bytes 584 | tf_op jit(solution)/shard_map/ppermute | solution.py:720
  (21 other events, 30.6 us)

commit v3 on v2

--- a/solution.py
+++ b/solution.py
@@ -152,9 +152,11 @@
     pairs = HEADS_STEP // 2
     columns = 2 * GROUP * block
     per_head = GROUP * block
-    for m in range(2):
+
+    def member(m, carry_all):
+        first = pl.multiple_of(m * block, block)
         count = (owned[m] + TILE_BLOCKS) // TILE_BLOCKS
-        q_rows = q_ref[m * block : (m + 1) * block, :]
+        q_rows = q_ref[pl.ds(first, block), :]
         queries = [pair_rows(q_rows, p) for p in range(pairs)]
         top[...] = jnp.full(top.shape, NEGATIVE_FLOOR, F32)
         total[...] = jnp.zeros(total.shape, F32)
@@ -193,10 +195,13 @@
         merged = []
         for p in range(pairs):
             denom = jnp.sum(total[p], axis=0, keepdims=True)
-            lse_ref[p, m : m + 1, :] = peaks[p] + jnp.log2(denom)
+            lse_ref[p, pl.ds(m, 1), :] = peaks[p] + jnp.log2(denom)
             for i in range(2):
                 merged += head_rows(acc[2 * p + i] / denom[:, i * per_head : (i + 1) * per_head], block)
-        o_ref[m * block : (m + 1) * block, :] = jnp.concatenate(merged, axis=1)
+        o_ref[pl.ds(first, block), :] = jnp.concatenate(merged, axis=1)
+        return carry_all
+
+    lax.fori_loop(0, 2, member, 0)
 
 
 def kv_specs(length, heads_width):
@@ -274,9 +279,10 @@
     per_head = GROUP * block
     dk[...] = jnp.zeros_like(dk)
     dv[...] = jnp.zeros_like(dv)
-    for m in range(2):
+
+    def one_member(m, carry_all):
         count = (owned[m] + TILE_BLOCKS) // TILE_BLOCKS
-        member = slice(m * block, (m + 1) * block)
+        member = pl.ds(pl.multiple_of(m * block, block), block)
         q_rows, g_rows, o_rows = q_ref[member, :], do_ref[member, :], o_ref[member, :]
         queries = [pair_rows(q_rows, p) for p in range(pairs)]
         grads = [pair_rows(g_rows, p) for p in range(pairs)]
@@ -284,7 +290,7 @@
         for p in range(pairs):
             product = grads[p].astype(F32) * pair_rows(o_rows, p).astype(F32)
             deltas.append(jnp.sum(product.T, axis=0, keepdims=True))
-        lses = [lse_ref[p, m : m + 1, :] for p in range(pairs)]
+        lses = [lse_ref[p, pl.ds(m, 1), :] for p in range(pairs)]
         acc[...] = jnp.zeros(acc.shape, F32)
 
         def grad_pass(tile, carry, queries=queries, grads=grads, deltas=deltas, lses=lses, m=m):
@@ -318,6 +324,9 @@
             swapped = jnp.concatenate([grad[middle:], grad[:middle]], axis=0)
             merged += head_rows(grad * cos_ref[m] - swapped * sin_ref[m], block)
         dq_ref[member, :] = jnp.concatenate(merged, axis=1)
+        return carry_all
+
+    lax.fori_loop(0, 2, one_member, 0)
 
     def unpack(chunk, carry):
         for source, target in ((dk, dk_out), (dv, dv_out)):
@@ -555,14 +564,17 @@
     greet(line, mid, core, count)
 
     def nearest_last(visit):
-        for step in range(count - 1, 0, -1):
-            for j in (line - step, line + step):
-
-                @pl.when(jnp.logical_and(j >= 0, j < count))
-                def _(j=j):
-                    visit(j)
-
-        visit(line)
+        def body(i, carry):
+            step = count - 1 - i // 2
+            j = line + step * (2 * (i % 2) - 1)
+
+            @pl.when(jnp.logical_and(j >= 0, j < count))
+            def _():
+                visit(j)
+
+            return carry
+
+        lax.fori_loop(0, 2 * count - 1, body, 0)
 
     def core_copy(s, j, m):
         index = 2 * j + m

time: 495 us -> 496 us (level)
  no operation moved by 1% of the time
where the time goes in v3:
time: 496 us; the launch traced here: 487 us
  Pallas kernels  193 us (39%)
  waiting for transfers between devices  162 us (33%)
  local copies, waits for them, and re-layouts  41.5 us (8%)
  starting transfers between devices  33.3 us (7%)
  other arithmetic  30.2 us (6%)
  matrix products  24.9 us (5%)
    ppermute x13, waiting for transfers between devices, swap_bit(): return lax.ppermute(value, CTX, [(i, i ^ 1 << bit) for i in range(size)])  111 us
    pallas_call x2, Pallas kernels, reduce_ctx(): pl.pallas_call(functools.partial(reduce_kernel, count, parts), out_shape=...  88.8 us
    ppermute x17, waiting for transfers between devices, swap_fsdp(): return lax.ppermute(value, FSDP, [(i, size - 1 - i) for i in range(size)])  51.4 us
    pallas_call x1, Pallas kernels, gather_ctx(): pl.pallas_call(functools.partial(gather_kernel, count), out_shape=jax.Sha...  42.4 us
    ppermute x17, starting transfers between devices, swap_fsdp(): return lax.ppermute(value, FSDP, [(i, size - 1 - i) for i in range(size)])  23.1 us
    pallas_call x1, Pallas kernels, attention_backward(): pl.pallas_call(functools.partial(backward_kernel, block), out_shape=(jax....  22.3 us
    pallas_call x1, Pallas kernels, ffn(): pl.pallas_call(ffn_kernel, out_shape=(act, act, act, turned, turned, own,...  19.6 us
    dot_general x13, matrix products, dot_nn(): lax.dot_general(left, right, (((1,), (0,)), ((), ())), preferred_element_...  19.4 us
  transfers between devices with their start and end apart: 30, of which 12 were waited for; matrix products, arithmetic and copies ran while one was open for 16% of the time, Pallas kernels for 40%

profile of v3, /device:TPU:0, one launch (start us, length us, event | category | flops | bytes accessed | tf_op | source)
XLA Modules:
  0.0 487.1 jit_solution(8995468615916614706)
XLA Ops:
  0.7 3.1 collective-permute-start
  9.0 1.9 collective-permute-start.14
  11.0 1.1 constant_dynamic-slice_fusion.8
  12.3 1.6 collective-permute-done
  15.7 2.0 collective-permute-start.4
  19.4 1.1 fusion.28
  20.5 2.3 fusion.20
  22.8 22.0 %collective-permute-done.4 = bf16[768,768]{1,0:T(8,128)(2,1)} collective-permute-done((bf16[768,768]{1,0:T(8,128)(2,1)}, bf16[768,768]{1,0:T(8,128)(2,1)}, u32[]{:S(2)}, u32[]{:S(2)}) %collective-permute-start.4) | collective-permute-done | bytes 1179680 | tf_op jit(solution)/shard_map/ppermute | solution.py:732
  46.8 1.8 collective-permute-start.1
  49.6 1.7 collective-permute-start.3
  53.1 10.0 %collective-permute-done.2.k_got = bf16[128,768]{1,0:T(8,128)(2,1)S(1)} collective-permute-done((bf16[128,768]{1,0:T(8,128)(2,1)S(1)}, bf16[128,768]{1,0:T(8,128)(2,1)S(1)}, u32[]{:S(2)}, u32[]{:S(2)}) %collective-permute-start.2) | collective-permute-done | bytes 196640 | tf_op jit(solution)/shard_map/ppermute | solution.py:732
  63.1 1.7 collective-permute-start.8
  64.8 2.5 collective-permute-done.3.v_got
  68.0 2.7 shard_map.257.own
  71.6 42.4 %shard_map.258.k_ref.v_ref = bf16[2048,1536]{1,0:T(8,128)(2,1)S(1)} custom-call(bf16[128,1536]{1,0:T(8,128)(2,1)S(1)} %copy-done.3), custom_call_target="tpu_custom_call" | custom-call | bytes 314572800 | tf_op jit(solution)/shard_map/pallas_call | solution.py:543
  114.1 2.6 copy-done
  117.4 15.0 %shard_map.259 = (bf16[128,1536]{1,0:T(8,128)(2,1)}, f32[4,2,256]{2,1,0:T(2,128)}, bf16[128,1536]{1,0:T(8,128)(2,1)}) custom-call(s32[32]{0:T(128)} %select_reduce_fusion.slot_of, s32[2]{0:T(128)} %get-tuple-element.73.owned, f32[128,1536]{1,0:T(8,128)} %slice.236.q_own, bf16[128,1536]{1,0:T(8,128)(2,1)} %copy-done.44, f32[128,768]{1,0:T(8,128)} %get-tuple-element.99.cosine, ...), custom_call_target="tpu_custom_call" | custom-call | flops 805306368 | bytes 6291456 | tf_op jit(solution)/shard_map/pallas_call | solution.py:224
  132.5 2.8 maximum_select_fusion.1
  135.7 3.2 multiply_reduce_fusion.2
  139.0 1.6 collective-permute-start.7
  141.6 2.3 copy.32
  143.9 1.8 constant_dynamic-slice_fusion.3
  146.9 4.2 collective-permute-done.7.n_other
  152.1 19.6 %shard_map.260 = (bf16[256,2048]{1,0:T(8,128)(2,1)S(1)}, bf16[256,2048]{1,0:T(8,128)(2,1)S(1)}, bf16[256,2048]{1,0:T(8,128)(2,1)}, bf16[16,96,256]{2,1,0:T(8,128...) custom-call(s32[32]{0:T(128)S(1)} %pad_add_fusion.places, ...), custom_call_target="tpu_custom_call" | custom-call | flops 9663676416 | bytes 22020096 | tf_op jit(solution)/shard_map/pallas_call | solution.py:840
  172.8 2.8 convolution_convert_fusion.4
  176.5 2.7 convolution_convert_fusion.2
  179.2 1.6 collective-permute-start.9
  181.2 2.1 fusion.43
  183.3 2.1 fusion.42
  186.4 2.1 fusion.41
  188.5 2.6 convolution_convert_fusion
  191.1 6.8 %collective-permute-done.10 = bf16[128,1536]{1,0:T(8,128)(2,1)S(1)} collective-permute-done((bf16[128,1536]{1,0:T(8,128)(2,1)S(1)}, bf16[128,1536]{1,0:T(8,128)(2,1)S(1)}, u32[]{:S(2)}, u32[]{:S(2)}) %collective-permute-start.10) | collective-permute-done | bytes 393248 | tf_op jit(solution)/shard_map/ppermute | solution.py:732
  198.1 1.3 fusion.40
  200.7 3.7 convolution_convert_fusion.9.do_ref
  204.4 1.5 collective-permute-start.15
  205.9 22.3 %shard_map.261 = (bf16[128,1536]{1,0:T(8,128)(2,1)}, bf16[16,128,768]{2,1,0:T(8,128)(2,1)}, bf16[16,128,768]{2,1,0:T(8,128)(2,1)}) custom-call(s32[32]{0:T(128)} %select_reduce_fusion.slot_of, s32[2]{0:T(128)} %get-tuple-element.73.owned, s32[32]{0:T(128)} %block_ids.1, bf16[128,1536]{1,0:T(8,128)(2,1)} %get-tuple-element.42.q_ref, ...), custom_call_target="tpu_custom_call" | custom-call | flops 2013265920 | bytes 12582912 | tf_op jit(solution)/shard_map/pallas_call | solution.py:356
  228.8 2.1 fusion.21
  230.9 1.9 copy-done.1
  232.8 1.9 copy-done.2
  234.7 39.9 %shard_map.262 = (f32[128,768]{1,0:T(8,128)S(1)}, f32[128,768]{1,0:T(8,128)S(1)}) custom-call(bf16[16,128,768]{2,1,0:T(8,128)(2,1)S(1)} %copy-done.1, bf16[16,128,768]{2,1,0:T(8,128)(2,1)S(1)} %copy-done.2), custom_call_target="tpu_custom_call" | custom-call | bytes 314572800 | tf_op jit(solution)/shard_map/pallas_call | solution.py:711
  276.1 2.4 shard_map.263
  278.6 1.5 collective-permute-start.12
  280.1 2.0 maximum_bitcast_fusion
  282.1 2.3 copy.31
  285.5 4.3 collective-permute-done.12
  294.4 1.5 collective-permute-start.13
  295.9 1.9 convolution_convert_fusion.8
  297.8 48.9 %shard_map.264 = (f32[48,1536]{1,0:T(8,128)S(1)}, f32[48,1536]{1,0:T(8,128)S(1)}, f32[48,1536]{1,0:T(8,128)S(1)}) custom-call(bf16[16,48,1536]{2,1,0:T(8,128)(2,1)S(1)} %bitcast.107, bf16[16,48,1536]{2,1,0:T(8,128)(2,1)S(1)} %bitcast.105, bf16[16,48,1536]{2,1,0:T(8,128)(2,1)S(1)} %bitcast.106), custom_call_target="tpu_custom_call" | custom-call | bytes 353894400 | tf_op jit(solution)/shard_map/pallas_call | solution.py:711
  348.8 3.4 fusion.5
  352.1 1.5 collective-permute-start.18
  353.7 1.6 fusion.3
  356.0 1.6 fusion.1
  357.6 1.6 collective-permute-start.27
  359.2 1.2 add_bitcast_fusion.3
  360.4 29.1 %collective-permute-done.18 = bf16[4,96,2048]{2,1,0:T(8,128)(2,1)S(1)} collective-permute-done((bf16[4,96,2048]{2,1,0:T(8,128)(2,1)S(1)}, bf16[4,96,2048]{2,1,0:T(8,128)(2,1)S(1)}, u32[]{:S(2)}, u32[]{:S(2)}) %collective-permute-start.18) | collective-permute-done | bytes 1572896 | tf_op jit(solution)/shard_map/ppermute | solution.py:737
  390.1 1.6 collective-permute-start.19
  391.8 30.2 %collective-permute-done.22 = bf16[4,96,2048]{2,1,0:T(8,128)(2,1)S(1)} collective-permute-done((bf16[4,96,2048]{2,1,0:T(8,128)(2,1)S(1)}, bf16[4,96,2048]{2,1,0:T(8,128)(2,1)S(1)}, u32[]{:S(2)}, u32[]{:S(2)}) %collective-permute-start.22) | collective-permute-done | bytes 1572896 | tf_op jit(solution)/shard_map/ppermute | solution.py:737
  422.6 1.3 collective-permute-start.23
  425.0 24.4 %collective-permute-done.23 = bf16[2,96,2048]{2,1,0:T(8,128)(2,1)S(1)} collective-permute-done((bf16[2,96,2048]{2,1,0:T(8,128)(2,1)S(1)}, bf16[2,96,2048]{2,1,0:T(8,128)(2,1)S(1)}, u32[]{:S(2)}, u32[]{:S(2)}) %collective-permute-start.23) | collective-permute-done | bytes 786464 | tf_op jit(solution)/shard_map/ppermute | solution.py:737
  449.7 3.0 collective-permute-start.29
  452.7 22.7 %collective-permute-done.24 = bf16[1,96,2048]{2,1,0:T(8,128)(2,1)S(1)} collective-permute-done((bf16[1,96,2048]{2,1,0:T(8,128)(2,1)S(1)}, bf16[1,96,2048]{2,1,0:T(8,128)(2,1)S(1)}, u32[]{:S(2)}, u32[]{:S(2)}) %collective-permute-start.24) | collective-permute-done | bytes 393248 | tf_op jit(solution)/shard_map/ppermute | solution.py:737
  475.4 2.8 add_reduce_fusion
  478.3 1.0 collective-permute-start.25
  479.3 4.4 collective-permute-done.29
  (210 shorter events, 40.9 us)
Async XLA Ops:
  0.6 10.2 %copy-start.23 = (bf16[1,128,1536]{2,1,0:T(8,128)(2,1)S(1)}, bf16[1,128,1536]{2,1,0:T(8,128)(2,1)}, u32[]{:S(2)}) copy-start(bf16[1,128,1536]{2,1,0:T(8,128)(2,1)} %param.18) | copy-start | bytes 1179652
  0.7 10.3 %copy-start.47 = (bf16[768]{0:T(1024)(128)(2,1)S(1)}, bf16[768]{0:T(1024)(128)(2,1)}, u32[]{:S(2)}) copy-start(bf16[768]{0:T(1024)(128)(2,1)} %param.21) | copy-start | bytes 4612
  0.7 10.4 %copy-start.40 = (bf16[1536,768]{1,0:T(8,128)(2,1)S(1)}, bf16[1536,768]{1,0:T(8,128)(2,1)}, u32[]{:S(2)}) copy-start(bf16[1536,768]{1,0:T(8,128)(2,1)} %param.26) | copy-start | bytes 7077892
  0.7 13.2 %collective-permute-start = (bf16[128,1536]{1,0:T(8,128)(2,1)}, bf16[128,1536]{1,0:T(8,128)(2,1)S(1)}, u32[]{:S(2)}, u32[]{:S(2)}) collective-permute-start(bf16[128,1536]{1,0:T(8,128)(2,1)} %bitcast.121), channel_id=1, source_target_pairs={{0,1},{1,0},{2,3},{3,2},{4,5},{5,4},{6,7},{7,6},{8,9},{9,8},{10,11... | collective-permute-start | bytes 1179656 | tf_op jit(solution)/shard_map/ppermute | solution.py:732
  5.1 39.8 %collective-permute-start.6 = (bf16[2,768]{1,0:T(2,128)(2,1)S(1)}, bf16[2,768]{1,0:T(2,128)(2,1)S(1)}, u32[]{:S(2)}, u32[]{:S(2)}) collective-permute-start(bf16[2,768]{1,0:T(2,128)(2,1)S(1)} %pad_maximum_fusion.3), channel_id=1, source_target_pairs={{0,1},{1,0},{2,3},{3,2},{4,5},{5,4},{6,7},{7,6},{8,9},{9,8},{10,11... | collective-permute-start | bytes 9224 | tf_op jit(solution)/shard_map/ppermute | solution.py:732
  9.0 337.8 %collective-permute-start.14 = (bf16[48,3072]{1,0:T(8,128)(2,1)}, bf16[48,3072]{1,0:T(8,128)(2,1)}, u32[]{:S(2)}, u32[]{:S(2)}) collective-permute-start(bf16[48,3072]{1,0:T(8,128)(2,1)} %dynamic-slice_bitcast_fusion), channel_id=1, source_target_pairs={{0,1},{1,0},{2,3},{3,2},{4,5},{5,4},{6,7},{7,6},{8,9},{9,8},{10,11... | collective-permute-start | bytes 884744 | tf_op jit(solution)/shard_map/ppermute | solution.py:732
  12.3 2.6 copy-start.13
  14.2 3.5 copy-start.50
  14.2 4.9 %copy-start.53 = (s32[16]{0:T(128)S(1)}, s32[16]{0:T(128)}, u32[]{:S(2)}) copy-start(s32[16]{0:T(128)} %constant.103.clone) | copy-start | bytes 196
  14.3 4.9 %copy-start.54 = (s32[16]{0:T(128)S(1)}, s32[16]{0:T(128)}, u32[]{:S(2)}) copy-start(s32[16]{0:T(128)} %constant.104.clone) | copy-start | bytes 196
  14.3 5.1 %copy-start.51 = (f32[96]{0:T(128)S(1)}, f32[96]{0:T(128)}, u32[]{:S(2)}) copy-start(f32[96]{0:T(128)} %constant.106.clone) | copy-start | bytes 1156
  14.3 5.1 %copy-start.52 = (f32[96]{0:T(128)S(1)}, f32[96]{0:T(128)}, u32[]{:S(2)}) copy-start(f32[96]{0:T(128)} %constant.105.clone) | copy-start | bytes 1156
  14.3 6.2 %copy-start.48 = (f32[768]{0:T(1024)S(1)}, f32[768]{0:T(1024)}, u32[]{:S(2)}) copy-start(f32[768]{0:T(1024)} %constant.102.clone) | copy-start | bytes 9220
  14.3 6.2 %copy-start.49 = (f32[768]{0:T(1024)S(1)}, f32[768]{0:T(1024)}, u32[]{:S(2)}) copy-start(f32[768]{0:T(1024)} %constant.101.clone) | copy-start | bytes 9220
  14.4 31.6 %copy-start.11 = (bf16[768,1536]{1,0:T(8,128)(2,1)S(1)}, bf16[768,1536]{1,0:T(8,128)(2,1)}, u32[]{:S(2)}) copy-start(bf16[768,1536]{1,0:T(8,128)(2,1)} %param.23) | copy-start | bytes 7077892
  14.9 2.8 copy-start.34
  15.7 29.1 %collective-permute-start.4 = (bf16[768,768]{1,0:T(8,128)(2,1)}, bf16[768,768]{1,0:T(8,128)(2,1)}, u32[]{:S(2)}, u32[]{:S(2)}) collective-permute-start(bf16[768,768]{1,0:T(8,128)(2,1)} %constant_dynamic-slice_fusion.8), channel_id=1, source_target_pairs={{0,1},{1,0},{2,3},{3,2},{4,5},{5,4},{6,7},{7,6},{8,9},{9,8},{10,11... | collective-permute-start | bytes 3538952 | tf_op jit(solution)/shard_map/ppermute | solution.py:732
  44.8 87.6 %collective-permute-start.5 = (bf16[768,768]{1,0:T(8,128)(2,1)}, bf16[768,768]{1,0:T(8,128)(2,1)}, u32[]{:S(2)}, u32[]{:S(2)}) collective-permute-start(bf16[768,768]{1,0:T(8,128)(2,1)} %collective-permute-done.4), channel_id=1, source_target_pairs={{0,2},{2,0},{4,6},{6,4},{8,10},{10,8},{12,14},{14,12},{16,18},{18,... | collective-permute-start | bytes 3538952 | tf_op jit(solution)/shard_map/ppermute | solution.py:737
  46.0 2.7 copy-start.29
  46.8 16.3 %copy-start.4 = (bf16[1,128,1536]{2,1,0:T(8,128)(2,1)S(1)}, bf16[1,128,1536]{2,1,0:T(8,128)(2,1)}, u32[]{:S(2)}) copy-start(bf16[1,128,1536]{2,1,0:T(8,128)(2,1)} %param.19) | copy-start | bytes 1179652
  46.8 69.8 %collective-permute-start.1 = (bf16[128,1536]{1,0:T(8,128)(2,1)S(1)}, bf16[128,1536]{1,0:T(8,128)(2,1)S(1)}, u32[]{:S(2)}, u32[]{:S(2)}) collective-permute-start(bf16[128,1536]{1,0:T(8,128)(2,1)S(1)} %slice.340), channel_id=1, source_target_pairs={{0,1},{1,0},{2,3},{3,2},{4,5},{5,4},{6,7},{7,6},{8,9},{9,8},{10,11... | collective-permute-start | bytes 1179656 | tf_op jit(solution)/shard_map/ppermute | solution.py:732
  49.2 13.9 %collective-permute-start.2 = (bf16[128,768]{1,0:T(8,128)(2,1)S(1)}, bf16[128,768]{1,0:T(8,128)(2,1)S(1)}, u32[]{:S(2)}, u32[]{:S(2)}) collective-permute-start(bf16[128,768]{1,0:T(8,128)(2,1)S(1)} %slice.343), channel_id=1, source_target_pairs={{0,1},{1,0},{2,3},{3,2},{4,5},{5,4},{6,7},{7,6},{8,9},{9,8},{10,11... | collective-permute-start | bytes 589832 | tf_op jit(solution)/shard_map/ppermute | solution.py:732
  49.6 17.7 %collective-permute-start.3 = (bf16[128,768]{1,0:T(8,128)(2,1)S(1)}, bf16[128,768]{1,0:T(8,128)(2,1)S(1)}, u32[]{:S(2)}, u32[]{:S(2)}) collective-permute-start(bf16[128,768]{1,0:T(8,128)(2,1)S(1)} %slice.342), channel_id=1, source_target_pairs={{0,1},{1,0},{2,3},{3,2},{4,5},{5,4},{6,7},{7,6},{8,9},{9,8},{10,11... | collective-permute-start | bytes 589832 | tf_op jit(solution)/shard_map/ppermute | solution.py:732
  63.1 4.2 copy-start.45
  63.1 83.1 %collective-permute-start.8 = (bf16[128,1536]{1,0:T(8,128)(2,1)S(1)}, bf16[128,1536]{1,0:T(8,128)(2,1)S(1)}, u32[]{:S(2)}, u32[]{:S(2)}) collective-permute-start(bf16[128,1536]{1,0:T(8,128)(2,1)S(1)} %bitcast.108), channel_id=1, source_target_pairs={{0,1},{1,0},{2,3},{3,2},{4,5},{5,4},{6,7},{7,6},{8,9},{9,8},{10,11... | collective-permute-start | bytes 1179656 | tf_op jit(solution)/shard_map/ppermute | solution.py:732
  114.0 2.6 copy-start
  132.5 2.8 copy-start.24
  132.5 3.2 copy-start.41
  135.3 3.6 copy-start.35
  135.7 5.0 %copy-start.14 = (f32[128,1536]{1,0:T(8,128)S(1)}, f32[128,1536]{1,0:T(8,128)}, u32[]{:S(2)}) copy-start(f32[128,1536]{1,0:T(8,128)} %copy-done.13) | copy-start | bytes 2359300
  135.7 5.0 %copy-start.16 = (f32[128,1536]{1,0:T(8,128)S(1)}, f32[128,1536]{1,0:T(8,128)}, u32[]{:S(2)}) copy-start(f32[128,1536]{1,0:T(8,128)} %copy-done.15) | copy-start | bytes 2359300
  138.9 59.3 %copy-start.10 = (f32[128,1536]{1,0:T(8,128)}, f32[128,1536]{1,0:T(8,128)S(1)}, u32[]{:S(2)}) copy-start(f32[128,1536]{1,0:T(8,128)S(1)} %get-tuple-element.107) | copy-start | bytes 2359300
  139.0 12.1 %collective-permute-start.7 = (bf16[128,1536]{1,0:T(8,128)(2,1)S(1)}, bf16[128,1536]{1,0:T(8,128)(2,1)S(1)}, u32[]{:S(2)}, u32[]{:S(2)}) collective-permute-start(bf16[128,1536]{1,0:T(8,128)(2,1)S(1)} %multiply_convert_fusion.n_own), channel_id=1, source_target_pairs={{0,1},{1,0},{2,3},{3,2},{4,5},{5,4},{6,7},{7,6},{8,9},{9,8},{10,11... | collective-permute-start | bytes 1179656 | tf_op jit(solution)/shard_map/ppermute | solution.py:732
  140.7 10.4 %copy-start.5 = (bf16[1,128,1536]{2,1,0:T(8,128)(2,1)S(1)}, bf16[1,128,1536]{2,1,0:T(8,128)(2,1)}, u32[]{:S(2)}) copy-start(bf16[1,128,1536]{2,1,0:T(8,128)(2,1)} %param.19) | copy-start | bytes 1179652
  145.7 148.7 %collective-permute-start.16 = (bf16[128,1536]{1,0:T(8,128)(2,1)}, bf16[128,1536]{1,0:T(8,128)(2,1)}, u32[]{:S(2)}, u32[]{:S(2)}) collective-permute-start(bf16[128,1536]{1,0:T(8,128)(2,1)} %get-tuple-element.37.o_ref), channel_id=1, source_target_pairs={{0,1},{1,0},{2,3},{3,2},{4,5},{5,4},{6,7},{7,6},{8,9},{9,8},{10,11... | collective-permute-start | bytes 1179656 | tf_op jit(solution)/shard_map/ppermute | solution.py:732
  179.2 48.9 %collective-permute-start.9 = (bf16[128,1536]{1,0:T(8,128)(2,1)}, bf16[128,1536]{1,0:T(8,128)(2,1)}, u32[]{:S(2)}, u32[]{:S(2)}) collective-permute-start(bf16[128,1536]{1,0:T(8,128)(2,1)} %get-tuple-element.41), channel_id=1, source_target_pairs={{0,1},{1,0},{2,3},{3,2},{4,5},{5,4},{6,7},{7,6},{8,9},{9,8},{10,11... | collective-permute-start | bytes 1179656 | tf_op jit(solution)/shard_map/ppermute | solution.py:732
  180.8 17.1 %collective-permute-start.10 = (bf16[128,1536]{1,0:T(8,128)(2,1)S(1)}, bf16[128,1536]{1,0:T(8,128)(2,1)S(1)}, u32[]{:S(2)}, u32[]{:S(2)}) collective-permute-start(bf16[128,1536]{1,0:T(8,128)(2,1)S(1)} %get-tuple-element.44), channel_id=1, source_target_pairs={{0,1},{1,0},{2,3},{3,2},{4,5},{5,4},{6,7},{7,6},{8,9},{9,8},{10,11... | collective-permute-start | bytes 1179656 | tf_op jit(solution)/shard_map/ppermute | solution.py:732
  183.3 164.8 %collective-permute-start.17 = (bf16[8,96,2048]{2,1,0:T(8,128)(2,1)}, bf16[8,96,2048]{2,1,0:T(8,128)(2,1)}, u32[]{:S(2)}, u32[]{:S(2)}) collective-permute-start(bf16[8,96,2048]{2,1,0:T(8,128)(2,1)} %bitcast.22), channel_id=1, source_target_pairs={{0,2},{2,0},{4,6},{6,4},{8,10},{10,8},{12,14},{14,12},{16,18},{18,... | collective-permute-start | bytes 9437192 | tf_op jit(solution)/shard_map/ppermute | solution.py:737
  197.9 2.8 copy-start.42
  204.4 74.2 %collective-permute-start.15 = (bf16[128,1536]{1,0:T(8,128)(2,1)}, bf16[128,1536]{1,0:T(8,128)(2,1)}, u32[]{:S(2)}, u32[]{:S(2)}) collective-permute-start(bf16[128,1536]{1,0:T(8,128)(2,1)} %get-tuple-element.70), channel_id=1, source_target_pairs={{0,1},{1,0},{2,3},{3,2},{4,5},{5,4},{6,7},{7,6},{8,9},{9,8},{10,11... | collective-permute-start | bytes 1179656 | tf_op jit(solution)/shard_map/ppermute | solution.py:732
  228.1 56.3 %collective-permute-start.11 = (bf16[128,1536]{1,0:T(8,128)(2,1)}, bf16[128,1536]{1,0:T(8,128)(2,1)}, u32[]{:S(2)}, u32[]{:S(2)}) collective-permute-start(bf16[128,1536]{1,0:T(8,128)(2,1)} %get-tuple-element.46), channel_id=1, source_target_pairs={{0,1},{1,0},{2,3},{3,2},{4,5},{5,4},{6,7},{7,6},{8,9},{9,8},{10,11... | collective-permute-start | bytes 1179656 | tf_op jit(solution)/shard_map/ppermute | solution.py:732
  234.7 43.8 %copy-start.43 = (bf16[128,1536]{1,0:T(8,128)(2,1)S(1)}, bf16[128,1536]{1,0:T(8,128)(2,1)}, u32[]{:S(2)}) copy-start(bf16[128,1536]{1,0:T(8,128)(2,1)} %get-tuple-element.46) | copy-start | bytes 1179652
  278.5 11.3 %copy-start.26 = (bf16[128,1536]{1,0:T(8,128)(2,1)S(1)}, bf16[128,1536]{1,0:T(8,128)(2,1)}, u32[]{:S(2)}) copy-start(bf16[128,1536]{1,0:T(8,128)(2,1)} %shard_map.263) | copy-start | bytes 1179652
  278.5 11.3 %copy-start.28 = (bf16[768,768]{1,0:T(8,128)(2,1)S(1)}, bf16[768,768]{1,0:T(8,128)(2,1)}, u32[]{:S(2)}) copy-start(bf16[768,768]{1,0:T(8,128)(2,1)} %param.25) | copy-start | bytes 3538948
  278.6 11.2 %collective-permute-start.12 = (bf16[128,1536]{1,0:T(8,128)(2,1)}, bf16[128,1536]{1,0:T(8,128)(2,1)S(1)}, u32[]{:S(2)}, u32[]{:S(2)}) collective-permute-start(bf16[128,1536]{1,0:T(8,128)(2,1)} %shard_map.263), channel_id=1, source_target_pairs={{0,1},{1,0},{2,3},{3,2},{4,5},{5,4},{6,7},{7,6},{8,9},{9,8},{10,11... | collective-permute-start | bytes 1179656 | tf_op jit(solution)/shard_map/ppermute | solution.py:732
  282.1 8.2 %copy-start.32 = (bf16[16,1,48,256]{3,2,1,0:T(8,128)(2,1)S(1)}, bf16[16,1,48,256]{3,2,1,0:T(8,128)(2,1)}, u32[]{:S(2)}) copy-start(bf16[16,1,48,256]{3,2,1,0:T(8,128)(2,1)} %constant_dynamic-slice_fusion.3) | copy-start | bytes 1179652
  284.5 69.2 %collective-permute-start.21 = (bf16[8,96,2048]{2,1,0:T(8,128)(2,1)}, bf16[8,96,2048]{2,1,0:T(8,128)(2,1)S(1)}, u32[]{:S(2)}, u32[]{:S(2)}) collective-permute-start(bf16[8,96,2048]{2,1,0:T(8,128)(2,1)} %bitcast.26), channel_id=1, source_target_pairs={{0,2},{2,0},{4,6},{6,4},{8,10},{10,8},{12,14},{14,12},{16,18},{18,... | collective-permute-start | bytes 9437192 | tf_op jit(solution)/shard_map/ppermute | solution.py:737
  289.8 66.2 %collective-permute-start.26 = (bf16[8,96,2048]{2,1,0:T(8,128)(2,1)}, bf16[8,96,2048]{2,1,0:T(8,128)(2,1)S(1)}, u32[]{:S(2)}, u32[]{:S(2)}) collective-permute-start(bf16[8,96,2048]{2,1,0:T(8,128)(2,1)} %bitcast.36), channel_id=1, source_target_pairs={{0,2},{2,0},{4,6},{6,4},{8,10},{10,8},{12,14},{14,12},{16,18},{18,... | collective-permute-start | bytes 9437192 | tf_op jit(solution)/shard_map/ppermute | solution.py:737
  294.4 53.4 %collective-permute-start.13 = (bf16[128,768]{1,0:T(8,128)(2,1)S(1)}, bf16[128,768]{1,0:T(8,128)(2,1)S(1)}, u32[]{:S(2)}, u32[]{:S(2)}) collective-permute-start(bf16[128,768]{1,0:T(8,128)(2,1)S(1)} %slice.341), channel_id=1, source_target_pairs={{0,1},{1,0},{2,3},{3,2},{4,5},{5,4},{6,7},{7,6},{8,9},{9,8},{10,11... | collective-permute-start | bytes 589832 | tf_op jit(solution)/shard_map/ppermute | solution.py:732
  297.8 49.0 %copy-start.38 = (bf16[2,48,3072]{2,1,0:T(8,128)(2,1)S(1)}, bf16[2,48,3072]{2,1,0:T(8,128)(2,1)}, u32[]{:S(2)}) copy-start(bf16[2,48,3072]{2,1,0:T(8,128)(2,1)} %copy-done.37) | copy-start | bytes 1769476
  297.8 50.0 %copy-start.25 = (bf16[1,128,1536]{2,1,0:T(8,128)(2,1)S(1)}, bf16[1,128,1536]{2,1,0:T(8,128)(2,1)}, u32[]{:S(2)}) copy-start(bf16[1,128,1536]{2,1,0:T(8,128)(2,1)} %param.18) | copy-start | bytes 1179652
  348.7 4.9 %copy-start.19 = (bf16[384,2048]{1,0:T(8,128)(2,1)S(1)}, bf16[384,2048]{1,0:T(8,128)(2,1)}, u32[]{:S(2)}) copy-start(bf16[384,2048]{1,0:T(8,128)(2,1)} %get-tuple-element.84) | copy-start | bytes 4718596
  348.7 4.9 %copy-start.20 = (bf16[384,2048]{1,0:T(8,128)(2,1)S(1)}, bf16[384,2048]{1,0:T(8,128)(2,1)}, u32[]{:S(2)}) copy-start(bf16[384,2048]{1,0:T(8,128)(2,1)} %get-tuple-element.85) | copy-start | bytes 4718596
  352.1 37.3 %collective-permute-start.18 = (bf16[4,96,2048]{2,1,0:T(8,128)(2,1)S(1)}, bf16[4,96,2048]{2,1,0:T(8,128)(2,1)S(1)}, u32[]{:S(2)}, u32[]{:S(2)}) collective-permute-start(bf16[4,96,2048]{2,1,0:T(8,128)(2,1)S(1)} %get-tuple-element.89), channel_id=1, source_target_pairs={{0,4},{2,6},{4,0},{6,2},{8,12},{10,14},{12,8},{14,10},{16,20},{18,... | collective-permute-start | bytes 4718600 | tf_op jit(solution)/shard_map/ppermute | solution.py:737
  355.3 66.6 %collective-permute-start.22 = (bf16[4,96,2048]{2,1,0:T(8,128)(2,1)S(1)}, bf16[4,96,2048]{2,1,0:T(8,128)(2,1)S(1)}, u32[]{:S(2)}, u32[]{:S(2)}) collective-permute-start(bf16[4,96,2048]{2,1,0:T(8,128)(2,1)S(1)} %get-tuple-element.83), channel_id=1, source_target_pairs={{0,4},{2,6},{4,0},{6,2},{8,12},{10,14},{12,8},{14,10},{16,20},{18,... | collective-permute-start | bytes 4718600 | tf_op jit(solution)/shard_map/ppermute | solution.py:737
  355.9 3.2 copy-start.33
  357.6 66.3 %collective-permute-start.27 = (bf16[4,96,2048]{2,1,0:T(8,128)(2,1)S(1)}, bf16[4,96,2048]{2,1,0:T(8,128)(2,1)S(1)}, u32[]{:S(2)}, u32[]{:S(2)}) collective-permute-start(bf16[4,96,2048]{2,1,0:T(8,128)(2,1)S(1)} %get-tuple-element.77), channel_id=1, source_target_pairs={{0,8},{2,10},{4,12},{6,14},{8,0},{10,2},{12,4},{14,6},{16,24},{18,... | collective-permute-start | bytes 4718600 | tf_op jit(solution)/shard_map/ppermute | solution.py:737
  390.1 34.7 %collective-permute-start.19 = (bf16[2,96,2048]{2,1,0:T(8,128)(2,1)S(1)}, bf16[2,96,2048]{2,1,0:T(8,128)(2,1)S(1)}, u32[]{:S(2)}, u32[]{:S(2)}) collective-permute-start(bf16[2,96,2048]{2,1,0:T(8,128)(2,1)S(1)} %get-tuple-element.87), channel_id=1, source_target_pairs={{0,8},{2,10},{4,12},{6,14},{8,0},{10,2},{12,4},{14,6},{16,24},{18,... | collective-permute-start | bytes 2359304 | tf_op jit(solution)/shard_map/ppermute | solution.py:737
  422.6 26.8 %collective-permute-start.23 = (bf16[2,96,2048]{2,1,0:T(8,128)(2,1)S(1)}, bf16[2,96,2048]{2,1,0:T(8,128)(2,1)S(1)}, u32[]{:S(2)}, u32[]{:S(2)}) collective-permute-start(bf16[2,96,2048]{2,1,0:T(8,128)(2,1)S(1)} %get-tuple-element.81), channel_id=1, source_target_pairs={{0,8},{2,10},{4,12},{6,14},{8,0},{10,2},{12,4},{14,6},{16,24},{18,... | collective-permute-start | bytes 2359304 | tf_op jit(solution)/shard_map/ppermute | solution.py:737
  424.4 25.1 %collective-permute-start.28 = (bf16[2,96,2048]{2,1,0:T(8,128)(2,1)S(1)}, bf16[2,96,2048]{2,1,0:T(8,128)(2,1)S(1)}, u32[]{:S(2)}, u32[]{:S(2)}) collective-permute-start(bf16[2,96,2048]{2,1,0:T(8,128)(2,1)S(1)} %get-tuple-element.75), channel_id=1, source_target_pairs={{0,4},{2,6},{4,0},{6,2},{8,12},{10,14},{12,8},{14,10},{16,20},{18,... | collective-permute-start | bytes 2359304 | tf_op jit(solution)/shard_map/ppermute | solution.py:737
  424.9 27.8 %collective-permute-start.20 = (bf16[1,96,2048]{2,1,0:T(8,128)(2,1)S(1)}, bf16[1,96,2048]{2,1,0:T(8,128)(2,1)S(1)}, u32[]{:S(2)}, u32[]{:S(2)}) collective-permute-start(bf16[1,96,2048]{2,1,0:T(8,128)(2,1)S(1)} %add_convert_fusion.10), channel_id=1, source_target_pairs={{0,16},{2,18},{4,20},{6,22},{8,24},{10,26},{12,28},{14,30},{16,0},... | collective-permute-start | bytes 1179656 | tf_op jit(solution)/shard_map/ppermute | solution.py:737
  449.5 25.9 %collective-permute-start.24 = (bf16[1,96,2048]{2,1,0:T(8,128)(2,1)S(1)}, bf16[1,96,2048]{2,1,0:T(8,128)(2,1)S(1)}, u32[]{:S(2)}, u32[]{:S(2)}) collective-permute-start(bf16[1,96,2048]{2,1,0:T(8,128)(2,1)S(1)} %add_convert_fusion.8), channel_id=1, source_target_pairs={{0,16},{2,18},{4,20},{6,22},{8,24},{10,26},{12,28},{14,30},{16,0},... | collective-permute-start | bytes 1179656 | tf_op jit(solution)/shard_map/ppermute | solution.py:737
  449.7 34.1 %collective-permute-start.29 = (bf16[1,96,2048]{2,1,0:T(8,128)(2,1)S(1)}, bf16[1,96,2048]{2,1,0:T(8,128)(2,1)S(1)}, u32[]{:S(2)}, u32[]{:S(2)}) collective-permute-start(bf16[1,96,2048]{2,1,0:T(8,128)(2,1)S(1)} %add_convert_fusion.6), channel_id=1, source_target_pairs={{0,16},{2,18},{4,20},{6,22},{8,24},{10,26},{12,28},{14,30},{16,0},... | collective-permute-start | bytes 1179656 | tf_op jit(solution)/shard_map/ppermute | solution.py:737
  478.3 6.5 %collective-permute-start.25 = (f32[48]{0:T(128)S(1)}, f32[48]{0:T(128)S(1)}, u32[]{:S(2)}, u32[]{:S(2)}) collective-permute-start(f32[48]{0:T(128)S(1)} %fusion.33), channel_id=1, source_target_pairs={{0,1},{1,0},{2,3},{3,2},{4,5},{5,4},{6,7},{7,6},{8,9},{9,8},{10,11... | collective-permute-start | bytes 584 | tf_op jit(solution)/shard_map/ppermute | solution.py:732
  (21 other events, 30.6 us)
